TPU v7x, 8 devices: a whole 2x2x1 slice. The times are simulated.
8 devices in a mesh: dp: 1 (over z), tp: 2 (over y), ep: 4 (over x, core).
Axes of the slice: x: 2, y: 2, z: 1, core: 2. Of those that a mesh axis runs over, the one named last changes fastest.
Arguments:
- tokens: bfloat16 [4096, 2048], P(('dp', 'ep', 'tp'))
- expert_ids: int32 [4096, 4], P(('dp', 'ep', 'tp'))
- gates: float32 [4096, 4], P(('dp', 'ep', 'tp'))
- slots: int32 [4096, 4], P(('dp', 'ep', 'tp'))
- shared_w1: bfloat16 [2048, 5632], P(None, 'tp')
- shared_w3: bfloat16 [2048, 5632], P(None, 'tp')
- shared_w2: bfloat16 [5632, 2048], P('tp')
- expert_w1: bfloat16 [60, 2048, 1408], P('ep')
- expert_w3: bfloat16 [60, 2048, 1408], P('ep')
- expert_w2: bfloat16 [60, 1408, 2048], P('ep')
Outputs:
- output: bfloat16 [4096, 2048], P(('dp', 'ep', 'tp'))
All inputs are finite; a program needn't handle non-finite values.
Results may differ from a plain program's by a relative error of at most 0.00136.
Values are sent between devices in bfloat16 or wider.
A program may use at most 1.25 GiB of HBM per device.

v0:
```python
import jax
import jax.numpy as jnp
from jax import lax
from jax.sharding import PartitionSpec as P


def capacity_rows(tok_dev, top_k, n_exp):
    return 8 * max(1, (2 * tok_dev * top_k + 8 * n_exp - 1) // (8 * n_exp))


def swiglu_rows(token_rows, w_gate, w_up, w_down):
    gate_pre = jnp.dot(token_rows, w_gate, preferred_element_type=jnp.float32)
    up_pre = jnp.dot(token_rows, w_up, preferred_element_type=jnp.float32)
    hidden = (jax.nn.silu(gate_pre) * up_pre).astype(jnp.bfloat16)
    return jnp.dot(hidden, w_down, preferred_element_type=jnp.float32)


def solution(mesh):
    ep_size = mesh.shape["ep"]
    row_spec = P(("dp", "ep", "tp"), None)
    expert_spec = P("ep", None, None)

    def local_layer(tokens, expert_ids, gates, slots, shared_w1, shared_w3, shared_w2, expert_w1, expert_w3, expert_w2):
        tok_dev, d_model = tokens.shape
        top_k = expert_ids.shape[1]
        local_exp = expert_w1.shape[0]
        cap_rows = capacity_rows(tok_dev, top_k, local_exp * ep_size)
        n_rows = local_exp * ep_size * cap_rows

        group_rows = lax.all_gather(tokens, "tp", axis=0, tiled=True)
        part_sum = swiglu_rows(group_rows, shared_w1, shared_w3, shared_w2)
        shared_out = lax.psum_scatter(part_sum, "tp", scatter_dimension=0, tiled=True)

        owner = expert_ids // local_exp
        row_code = (expert_ids % local_exp) * (ep_size * cap_rows) + owner * cap_rows + slots
        row_code = jnp.where(slots >= 0, row_code, n_rows)
        copy_tok = jnp.broadcast_to(jnp.arange(tok_dev, dtype=jnp.int32)[:, None], (tok_dev, top_k))
        inverse = jnp.full((n_rows,), tok_dev, jnp.int32).at[row_code.reshape(-1)].set(copy_tok.reshape(-1), mode="drop")
        send_rows = jnp.take(tokens, inverse, axis=0, mode="fill", fill_value=0).reshape(local_exp, ep_size, cap_rows, d_model)
        recv_rows = lax.all_to_all(send_rows, "ep", 1, 1, tiled=True)
        gate_pre = jnp.einsum("lscd,ldf->lscf", recv_rows, expert_w1, preferred_element_type=jnp.float32)
        up_pre = jnp.einsum("lscd,ldf->lscf", recv_rows, expert_w3, preferred_element_type=jnp.float32)
        hidden = (jax.nn.silu(gate_pre) * up_pre).astype(jnp.bfloat16)
        expert_out = jnp.einsum("lscf,lfd->lscd", hidden, expert_w2, preferred_element_type=jnp.float32).astype(jnp.bfloat16)
        back_rows = lax.all_to_all(expert_out, "ep", 1, 1, tiled=True).reshape(n_rows, d_model)
        routed = jnp.take(back_rows, row_code, axis=0, mode="fill", fill_value=0)
        routed_sum = jnp.sum(gates[:, :, None] * routed.astype(jnp.float32), axis=1)
        return (tokens.astype(jnp.float32) + shared_out + routed_sum).astype(jnp.bfloat16)

    return jax.shard_map(local_layer, mesh=mesh, in_specs=(row_spec, row_spec, row_spec, row_spec, P(None, "tp"), P(None, "tp"), P("tp", None), expert_spec, expert_spec, expert_spec), out_specs=row_spec, check_vma=False)
```

profile of v0, /device:TPU:0, one launch (start us, length us, event | category | flops | bytes accessed | tf_op | source)
XLA Modules:
  0.0 712.4 jit_solution(10441944655675013165)
XLA Ops:
  6.5 1.3 compare_and_fusion.1
  7.9 0.1 copy.28
  8.0 0.2 reshape.55
  8.2 0.2 reshape.78
  8.4 8.1 %scatter_custom_fusion = s32[4320]{0:T(1024)S(1)} fusion(s32[2048]{0:T(1024)S(1)} %bitcast.39, s32[2048]{0:T(1024)S(1)} %reshape.78, s32[]{:T(128)} %constant.61.clone.1), kind=kCustom, calls=%fused_computation.24 | custom fusion | bytes 17284 | tf_op jit(solution)/shard_map/scatter | solution.py:38
  16.5 0.1 broadcast_in_dim.45
  16.7 35.1 %gather_fusion = bf16[4320,2048]{1,0:T(8,128)(2,1)} fusion(bf16[512,2048]{1,0:T(8,128)(2,1)} %param.10, s32[5120]{0:T(1024)S(1)} %pad_clamp_fusion), kind=kCustom, calls=%fused_computation | custom fusion | bytes 35406720 | tf_op jit(solution)/shard_map/jit(_take)/gather | solution.py:39
  51.7 16.1 %copy_select_fusion = bf16[15,4,72,2048]{3,2,0,1:T(8,128)(2,1)} fusion(bf16[15,4,72,2048]{3,2,1,0:T(8,128)(2,1)} %bitcast.38, pred[15,4,72]{2,0,1:T(8,128)(4,1)S(1)} %copy.29), kind=kLoop, calls=%fused_computation.10 | loop fusion | flops 8847360 | bytes 35393760 | tf_op jit(solution)/shard_map/jit(_take)/select_n | solution.py:39
  67.8 7.2 %all-to-all-start = ((bf16[15,4,72,2048]{3,2,0,1:T(8,128)(2,1)}), bf16[15,4,72,2048]{3,2,0,1:T(8,128)(2,1)}, u32[]{:S(2)}, u32[]{:S(2)}) async-start(bf16[15,4,72,2048]{3,2,0,1:T(8,128)(2,1)} %copy_select_fusion), calls=%async_computation.1 | async-start | bytes 35389440 | tf_op jit(solution)/shard_map/all_to_all | solution.py:40
  75.0 0.0 all-gather.2.cloned.1.call-start
  75.1 0.7 all-gather.2.cloned.1.call-update
  75.8 0.2 reduce-scatter.2.cloned.1.call-start
  76.0 58.9 %all-gather.2.cloned.1.call-done = bf16[1024,2048]{1,0:T(8,128)(2,1)} async-done(((bf16[512,2048]{1,0:T(8,128)(2,1)}), bf16[1024,2048]{1,0:T(8,128)(2,1)}) %all-gather.2.cloned.1.call-update) | async-done | bytes 4194320 | tf_op jit(solution)/shard_map/all_gather | solution.py:30
  134.9 18.7 %fusion.21 = f32[1024,2816]{1,0:T(8,128)} fusion(bf16[1024,2048]{1,0:T(8,128)(2,1)} %all-gather.2.cloned.1.call-done, bf16[2048,2816]{1,0:T(8,128)(2,1)} %param.14), kind=kOutput, calls=%fused_computation.35 | convolution fusion | flops 11811160064 | bytes 27262976 | tf_op jit(solution)/shard_map/dot_general | solution.py:12
  153.5 36.2 %fusion.22 = f32[1024,2048]{1,0:T(8,128)} fusion(bf16[2816,2048]{1,0:T(8,128)(2,1)} %param.16, f32[1024,2816]{1,0:T(8,128)} %fusion.21, bf16[1024,2048]{1,0:T(8,128)(2,1)} %all-gather.2.cloned.1.call-done, bf16[2048,2816]{1,0:T(8,128)(2,1)} %param.15), kind=kOutput, calls=%fused_computation.36 | convolution fusion | flops 23639621632 | bytes 47185920 | tf_op jit(solution)/shard_map/dot_general | solution.py:15
  189.7 0.0 reduce-scatter.2.cloned.1.call-update
  189.7 78.8 %all-to-all-done = bf16[15,4,72,2048]{3,2,0,1:T(8,128)(2,1)} async-done(((bf16[15,4,72,2048]{3,2,0,1:T(8,128)(2,1)}), bf16[15,4,72,2048]{3,2,0,1:T(8,128)(2,1)}, u32[]{:S(2)}, u32[]{:S(2)}) %all-to-all-start) | async-done | bytes 17694752 | tf_op jit(solution)/shard_map/all_to_all | solution.py:40
  268.5 47.2 %fusion.2 = f32[15,4,72,1408]{3,2,1,0:T(8,128)} fusion(bf16[15,2048,1408]{2,1,0:T(8,128)(2,1)} %param.18, bf16[15,4,72,2048]{3,2,0,1:T(8,128)(2,1)} %all-to-all-done), kind=kOutput, calls=%fused_computation.5 | convolution fusion | flops 24914165760 | bytes 128532480 | tf_op jit(solution)/shard_map/lscd,ldf->lscf/dot_general | solution.py:42
  315.7 49.2 %multiply_convert_fusion = bf16[15,4,72,1408]{3,2,1,0:T(8,128)(2,1)} fusion(f32[15,4,72,1408]{3,2,1,0:T(8,128)} %fusion.2, bf16[15,2048,1408]{2,1,0:T(8,128)(2,1)} %param.17, bf16[15,4,72,2048]{3,2,0,1:T(8,128)(2,1)} %all-to-all-done), kind=kOutput, calls=%fused_computation.9 | convolution fusion | flops 24950661120 | bytes 140697600 | tf_op jit(solution)/shard_map/lscd,ldf->lscf/dot_general | solution.py:41
  364.9 43.9 %fusion.10 = bf16[15,4,72,2048]{3,2,1,0:T(8,128)(2,1)} fusion(bf16[15,4,72,1408]{3,2,1,0:T(8,128)(2,1)} %multiply_convert_fusion, bf16[15,1408,2048]{2,1,0:T(8,128)(2,1)} %param.19), kind=kOutput, calls=%fused_computation.14 | convolution fusion | flops 24923013120 | bytes 116367360 | tf_op jit(solution)/shard_map/lscf,lfd->lscd/dot_general | solution.py:44
  408.8 16.2 %copy.33 = bf16[15,4,72,2048]{3,2,0,1:T(8,128)(2,1)} copy(bf16[15,4,72,2048]{3,2,1,0:T(8,128)(2,1)} %fusion.10) | data formatting | bytes 35389440 | tf_op jit(solution)/shard_map/convert_element_type | solution.py:44
  425.1 7.5 %all-to-all-start.1 = ((bf16[15,4,72,2048]{3,2,0,1:T(8,128)(2,1)}), bf16[15,4,72,2048]{3,2,0,1:T(8,128)(2,1)}, u32[]{:S(2)}, u32[]{:S(2)}) async-start(bf16[15,4,72,2048]{3,2,0,1:T(8,128)(2,1)} %copy.33), calls=%async_computation.2 | async-start | bytes 35389440 | tf_op jit(solution)/shard_map/all_to_all | solution.py:45
  432.6 0.1 copy.35
  432.8 0.2 reshape.68
  433.0 0.2 copy.27
  433.2 0.1 copy.26
  433.3 191.6 %all-to-all-done.1 = bf16[15,4,72,2048]{3,2,0,1:T(8,128)(2,1)} async-done(((bf16[15,4,72,2048]{3,2,0,1:T(8,128)(2,1)}), bf16[15,4,72,2048]{3,2,0,1:T(8,128)(2,1)}, u32[]{:S(2)}, u32[]{:S(2)}) %all-to-all-start.1) | async-done | bytes 17694752 | tf_op jit(solution)/shard_map/all_to_all | solution.py:45
  624.9 16.2 %copy.34 = bf16[15,4,72,2048]{3,2,1,0:T(8,128)(2,1)} copy(bf16[15,4,72,2048]{3,2,0,1:T(8,128)(2,1)} %all-to-all-done.1) | data formatting | bytes 35389440 | tf_op jit(solution)/shard_map/all_to_all | solution.py:45
  641.1 24.7 %gather_fusion.1 = bf16[2048,2048]{1,0:T(8,128)(2,1)} fusion(bf16[4320,2048]{1,0:T(8,128)(2,1)} %bitcast.37, s32[2048]{0:T(1024)S(1)} %broadcast_clamp_fusion), kind=kCustom, calls=%fused_computation.1 | custom fusion | bytes 16785408 | tf_op jit(solution)/shard_map/jit(_take)/gather | solution.py:46
  665.7 13.2 %reshape.67 = bf16[512,4,2048]{2,1,0:T(4,128)(2,1)} reshape(bf16[2048,2048]{1,0:T(8,128)(2,1)} %gather_fusion.1) | data formatting | bytes 16777216 | tf_op jit(solution)/shard_map/jit(_take)/gather | solution.py:46
  679.0 20.6 %multiply_reduce_fusion = f32[512,2048]{1,0:T(8,128)} fusion(bf16[512,4,2048]{2,1,0:T(4,128)(2,1)} %reshape.67, f32[512,4]{1,0:T(8,128)S(1)} %copy.26, pred[512,4]{1,0:T(8,128)(4,1)S(1)} %copy.27), kind=kLoop, calls=%fused_computation.11 | loop fusion | flops 15728640 | bytes 12593152 | tf_op jit(solution)/shard_map/reduce_sum | solution.py:47
  699.6 6.0 add_convert_fusion
  (19 shorter events, 0.1 us)
Async XLA Ops:
  7.9 43.9 %copy-start.1 = (s32[512,4]{0,1:T(4,128)}, s32[512,4]{0,1:T(4,128)S(1)}, u32[]{:S(2)}) copy-start(s32[512,4]{0,1:T(4,128)S(1)} %get-tuple-element.6) | copy-start | bytes 24580
  67.8 200.7 %all-to-all-start = ((bf16[15,4,72,2048]{3,2,0,1:T(8,128)(2,1)}), bf16[15,4,72,2048]{3,2,0,1:T(8,128)(2,1)}, u32[]{:S(2)}, u32[]{:S(2)}) async-start(bf16[15,4,72,2048]{3,2,0,1:T(8,128)(2,1)} %copy_select_fusion), calls=%async_computation.1 | async-start | bytes 35389440 | tf_op jit(solution)/shard_map/all_to_all | solution.py:40
  75.0 59.8 %all-gather.2.cloned.1.call-start = ((), (), s32[]{:S(2)}) async-start(), calls=%async_computation.3 | async-start | bytes 6291456 | tf_op jit(solution)/shard_map/all_gather | solution.py:30
  75.8 623.8 %reduce-scatter.2.cloned.1.call-start = ((), (), s32[]{:S(2)}) async-start(), calls=%async_computation.4 | async-start | bytes 12582912 | tf_op jit(solution)/shard_map/reduce_scatter | solution.py:32
  425.1 7.5 %copy-start.2 = (s32[512,4]{0,1:T(4,128)S(1)}, s32[512,4]{0,1:T(4,128)}, u32[]{:S(2)}) copy-start(s32[512,4]{0,1:T(4,128)} %copy-done.1) | copy-start | bytes 24580
  425.1 7.9 %copy-start.4 = (pred[512,4]{0,1:T(4,128)(4,1)S(1)}, pred[512,4]{0,1:T(4,128)(4,1)}, u32[]{:S(2)}) copy-start(pred[512,4]{0,1:T(4,128)(4,1)} %get-tuple-element.5) | copy-start | bytes 6148
  425.1 8.1 %copy-start.3 = (f32[512,4]{0,1:T(4,128)S(1)}, f32[512,4]{0,1:T(4,128)}, u32[]{:S(2)}) copy-start(f32[512,4]{0,1:T(4,128)} %param.12) | copy-start | bytes 24580
  425.1 199.8 %all-to-all-start.1 = ((bf16[15,4,72,2048]{3,2,0,1:T(8,128)(2,1)}), bf16[15,4,72,2048]{3,2,0,1:T(8,128)(2,1)}, u32[]{:S(2)}, u32[]{:S(2)}) async-start(bf16[15,4,72,2048]{3,2,0,1:T(8,128)(2,1)} %copy.33), calls=%async_computation.2 | async-start | bytes 35389440 | tf_op jit(solution)/shard_map/all_to_all | solution.py:45
  665.7 33.8 %copy-start = (bf16[512,2048]{1,0:T(8,128)(2,1)S(1)}, bf16[512,2048]{1,0:T(8,128)(2,1)}, u32[]{:S(2)}) copy-start(bf16[512,2048]{1,0:T(8,128)(2,1)} %param.10) | copy-start | bytes 6291460
Sparse Core Ops, SparseCore 0:
  77.3 57.4 all-gather.1
  189.9 96.4 reduce-scatter.1
where the time goes:
time: 713 us; the launch traced here: 712 us
  waiting for transfers between devices  330 us (46%)
  matrix products  195 us (27%)
  local copies, waits for them, and re-layouts  115 us (16%)
  other arithmetic  44 us (6%)
  starting transfers between devices  15 us (2%)
  between operations  13.6 us (2%)
    all_to_all x1, waiting for transfers between devices, local_layer(): lax.all_to_all(expert_out, 'ep', 1, 1, tiled=True).reshape(n_rows, d_model)  192 us
    all_to_all x1, waiting for transfers between devices, local_layer(): recv_rows = lax.all_to_all(send_rows, 'ep', 1, 1, tiled=True)  78.8 us
    all_gather x1, waiting for transfers between devices, local_layer(): group_rows = lax.all_gather(tokens, 'tp', axis=0, tiled=True)  58.9 us
    dot_general x1, matrix products, local_layer(): jnp.einsum('lscd,ldf->lscf', recv_rows, expert_w1, preferred_element_type...  49.2 us
    dot_general x1, matrix products, local_layer(): jnp.einsum('lscd,ldf->lscf', recv_rows, expert_w3, preferred_element_type...  47.2 us
    dot_general x1, matrix products, local_layer(): jnp.einsum('lscf,lfd->lscd', hidden, expert_w2, preferred_element_type=jn...  43.9 us
    gather x2, local copies, waits for them, and re-layouts, local_layer(): routed = jnp.take(back_rows, row_code, axis=0, mode='fill', fill_value=0)  37.9 us
    dot_general x1, matrix products, swiglu_rows(): return jnp.dot(hidden, w_down, preferred_element_type=jnp.float32)  36.2 us
  transfers between devices with their start and end apart: 4, of which 3 were waited for; matrix products, arithmetic and copies ran while one was open for 40% of the time, Pallas kernels for 0%

commit v1 on v0

v1 whole, which is shorter than its diff:
```python
import functools

import jax
import jax.numpy as jnp
from jax import lax
from jax.experimental import pallas as pl
from jax.experimental.pallas import tpu as pltpu
from jax.sharding import PartitionSpec as P

COL_BLOCKS = 4
GATE_MAX = 3.3895313892515355e38


def capacity_rows(tok_dev, top_k, n_exp):
    return 8 * max(1, (2 * tok_dev * top_k + 8 * n_exp - 1) // (8 * n_exp))


def swiglu_rows(token_rows, w_gate, w_up, w_down):
    gate_pre = jnp.dot(token_rows, w_gate, preferred_element_type=jnp.float32)
    up_pre = jnp.dot(token_rows, w_up, preferred_element_type=jnp.float32)
    hidden = (jax.nn.silu(gate_pre) * up_pre).astype(jnp.bfloat16)
    return jnp.dot(hidden, w_down, preferred_element_type=jnp.float32)


def params(mib):
    return pltpu.CompilerParams(vmem_limit_bytes=mib * 2**20)


def gather_kernel(cap, group, code_ref, first_ref, second_ref, out_ref):
    rows = group * cap
    slot = lax.broadcasted_iota(jnp.int32, (rows, code_ref.shape[2]), 0) + pl.program_id(0) * rows
    for source, tok_ref in enumerate((first_ref, second_ref)):
        code = code_ref[source]
        hit = slot == code[0:1, :]
        for j in range(1, code.shape[0]):
            hit = hit | (slot == code[j : j + 1, :])
        pick = jnp.where(hit, 1.0, 0.0).astype(jnp.bfloat16)
        picked = jnp.dot(pick, tok_ref[...], preferred_element_type=jnp.float32).astype(jnp.bfloat16)
        for k in range(group):
            out_ref[k, source * cap : (source + 1) * cap, :] = picked[k * cap : (k + 1) * cap, :]


def gather_rows(codes, first, second, local_exp, cap):
    tok_dev, d_model = first.shape
    group = 3
    rows = 2 * local_exp * cap
    return pl.pallas_call(
        functools.partial(gather_kernel, cap, group),
        grid=(local_exp // group,),
        out_shape=jax.ShapeDtypeStruct((local_exp, 2 * cap, d_model), jnp.bfloat16),
        in_specs=[
            pl.BlockSpec(codes.shape, lambda b: (0, 0, 0)),
            pl.BlockSpec((tok_dev, d_model), lambda b: (0, 0)),
            pl.BlockSpec((tok_dev, d_model), lambda b: (0, 0)),
        ],
        out_specs=pl.BlockSpec((group, 2 * cap, d_model), lambda b: (b, 0, 0)),
        compiler_params=params(40),
        cost_estimate=pl.CostEstimate(flops=2 * rows * tok_dev * d_model, bytes_accessed=2 * rows * d_model, transcendentals=0),
        name="gather_rows",
    )(codes, first, second)


def combine_kernel(cap, code_ref, gate_ref, out_ref):
    rows, top_k = code_ref.shape
    width = 3 * cap
    lane = lax.broadcasted_iota(jnp.int32, (rows, width), 1)
    piece = (lane >= cap).astype(jnp.int32) + (lane >= 2 * cap).astype(jnp.int32)
    target = lane - piece * cap + pl.program_id(0) * cap
    value = jnp.zeros((rows, width), jnp.float32)
    for j in range(top_k):
        value = jnp.where(target == code_ref[:, j : j + 1], gate_ref[:, j : j + 1], value)
    high = jnp.minimum(value, GATE_MAX).astype(jnp.bfloat16).astype(jnp.float32)
    rest = value - high
    middle = rest.astype(jnp.bfloat16).astype(jnp.float32)
    low = rest - middle
    out_ref[0] = jnp.where(piece == 0, high, jnp.where(piece == 1, middle, low)).astype(jnp.bfloat16)


def combine_matrix(code_cols, gate_cols, local_exp, cap):
    rows, top_k = code_cols.shape
    return pl.pallas_call(
        functools.partial(combine_kernel, cap),
        grid=(local_exp,),
        out_shape=jax.ShapeDtypeStruct((local_exp, rows, 3 * cap), jnp.bfloat16),
        in_specs=[pl.BlockSpec((rows, top_k), lambda e: (0, 0))] * 2,
        out_specs=pl.BlockSpec((1, rows, 3 * cap), lambda e: (e, 0, 0)),
        compiler_params=params(40),
        cost_estimate=pl.CostEstimate(flops=local_exp * rows * 3 * cap * 400, bytes_accessed=local_exp * rows * 512, transcendentals=0),
        name="combine_matrix",
    )(code_cols, gate_cols)


def hidden_kernel(near_ref, far_ref, gate_w_ref, up_w_ref, out_ref):
    rows = jnp.concatenate([near_ref[0], far_ref[0]], axis=0)
    width = out_ref.shape[2]
    step = 256
    for start in range(0, width, step):
        cols = slice(start, min(start + step, width))
        gate_pre = jnp.dot(rows, gate_w_ref[0, :, cols], preferred_element_type=jnp.float32)
        up_pre = jnp.dot(rows, up_w_ref[0, :, cols], preferred_element_type=jnp.float32)
        out_ref[0, :, cols] = (jax.nn.silu(gate_pre) * up_pre).astype(jnp.bfloat16)


def expert_hidden(near, far, w_gate, w_up):
    local_exp, half, d_model = near.shape
    width = w_gate.shape[2]
    row_spec = pl.BlockSpec((1, half, d_model), lambda e: (e, 0, 0))
    weight_spec = pl.BlockSpec((1, d_model, width), lambda e: (e, 0, 0))
    return pl.pallas_call(
        hidden_kernel,
        grid=(local_exp,),
        out_shape=jax.ShapeDtypeStruct((local_exp, 2 * half, width), jnp.bfloat16),
        in_specs=[row_spec, row_spec, weight_spec, weight_spec],
        out_specs=pl.BlockSpec((1, 2 * half, width), lambda e: (e, 0, 0)),
        compiler_params=params(56),
        cost_estimate=pl.CostEstimate(
            flops=local_exp * 2 * half * d_model * width * 4,
            bytes_accessed=local_exp * d_model * width * 4,
            transcendentals=local_exp * 2 * half * width,
        ),
        name="expert_hidden",
    )(near, far, w_gate, w_up)


def partial_kernel(cap, tok_dev, hidden_ref, weight_ref, combine_ref, out_ref):
    result = jnp.dot(hidden_ref[0], weight_ref[0], preferred_element_type=jnp.float32)
    n_sources = out_ref.shape[0]

    @pl.when(pl.program_id(0) == 0)
    def _():
        out_ref[...] = jnp.zeros_like(out_ref)

    for source in range(n_sources):
        part = result[source * cap : (source + 1) * cap, :].astype(jnp.bfloat16).astype(jnp.float32)
        stacked = jnp.concatenate([part, part, part], axis=0).astype(jnp.bfloat16)
        weights = combine_ref[0, source * tok_dev : (source + 1) * tok_dev, :]
        out_ref[source] += jnp.dot(weights, stacked, preferred_element_type=jnp.float32)


def expert_partial(hidden, w_down, combine, n_sources, block, n_blocks):
    local_exp, rows, width = hidden.shape
    cap = rows // n_sources
    tok_dev = combine.shape[1] // n_sources
    cols = w_down.shape[2] // n_blocks
    return pl.pallas_call(
        functools.partial(partial_kernel, cap, tok_dev),
        grid=(local_exp,),
        out_shape=jax.ShapeDtypeStruct((n_sources, tok_dev, cols), jnp.float32),
        in_specs=[
            pl.BlockSpec((1, rows, width), lambda e: (e, 0, 0)),
            pl.BlockSpec((1, width, cols), lambda e: (e, 0, block)),
            pl.BlockSpec((1, n_sources * tok_dev, 3 * cap), lambda e: (e, 0, 0)),
        ],
        out_specs=pl.BlockSpec((n_sources, tok_dev, cols), lambda e: (0, 0, 0)),
        compiler_params=params(40),
        cost_estimate=pl.CostEstimate(
            flops=2 * local_exp * cols * (rows * width + n_sources * tok_dev * 256),
            bytes_accessed=local_exp * 2 * (width * cols + rows * width + n_sources * tok_dev * 256),
            transcendentals=0,
        ),
        name="expert_partial",
    )(hidden, w_down, combine)


def solution(mesh):
    ep_size = mesh.shape["ep"]
    tp_size = mesh.shape["tp"]
    row_spec = P(("dp", "ep", "tp"), None)
    expert_spec = P("ep", None, None)
    core_swap = [(i, i ^ 1) for i in range(ep_size)]
    chip_swap = [(i, i ^ 2) for i in range(ep_size)]
    both_swap = [(i, i ^ 3) for i in range(ep_size)]
    tp_swap = [(i, i ^ 1) for i in range(tp_size)]

    def local_layer(tokens, expert_ids, gates, slots, shared_w1, shared_w3, shared_w2, expert_w1, expert_w3, expert_w2):
        tok_dev, d_model = tokens.shape
        top_k = expert_ids.shape[1]
        local_exp = expert_w1.shape[0]
        cap = capacity_rows(tok_dev, top_k, local_exp * ep_size)
        me = lax.axis_index("ep")

        code = jnp.where(slots >= 0, expert_ids * cap + slots, -1)
        meta = jnp.concatenate([code.astype(jnp.float32).T, gates.T], axis=0)
        metas = [meta] + [lax.ppermute(meta, "ep", perm) for perm in (core_swap, chip_swap, both_swap)]
        metas = jnp.stack(metas)
        codes = metas[:, :top_k].astype(jnp.int32)
        mine = (codes >= 0) & (codes // (local_exp * cap) == me)
        codes = jnp.where(mine, codes - me * (local_exp * cap), -1)
        code_cols = codes.transpose(0, 2, 1).reshape(ep_size * tok_dev, top_k)
        gate_cols = metas[:, top_k:].transpose(0, 2, 1).reshape(ep_size * tok_dev, top_k)

        other_tp = lax.ppermute(tokens, "tp", tp_swap)
        tok_core = lax.ppermute(tokens, "ep", core_swap)
        tok_chip = lax.ppermute(tokens, "ep", chip_swap)
        tok_both = lax.ppermute(tok_chip, "ep", core_swap)

        shared_own = swiglu_rows(tokens, shared_w1, shared_w3, shared_w2)
        shared_other = swiglu_rows(other_tp, shared_w1, shared_w3, shared_w2)
        shared_back = lax.ppermute(shared_other, "tp", tp_swap)

        combine = combine_matrix(code_cols, gate_cols, local_exp, cap)
        near = gather_rows(codes[:2], tokens, tok_core, local_exp, cap)
        far = gather_rows(codes[2:], tok_chip, tok_both, local_exp, cap)
        hidden = expert_hidden(near, far, expert_w1, expert_w3)

        n_blocks = COL_BLOCKS
        cols = d_model // n_blocks
        outs = []
        for block in range(n_blocks):
            part = expert_partial(hidden, expert_w2, combine, ep_size, block, n_blocks)
            from_core = lax.ppermute(part[1::2], "ep", core_swap)
            for_chip = part[2] + from_core[1]
            from_chip = lax.ppermute(for_chip, "ep", chip_swap)
            here = slice(block * cols, (block + 1) * cols)
            routed = part[0] + from_core[0] + from_chip
            shared = shared_own[:, here] + shared_back[:, here]
            outs.append((tokens[:, here].astype(jnp.float32) + shared + routed).astype(jnp.bfloat16))
        return jnp.concatenate(outs, axis=1)

    return jax.shard_map(local_layer, mesh=mesh, in_specs=(row_spec, row_spec, row_spec, row_spec, P(None, "tp"), P(None, "tp"), P("tp", None), expert_spec, expert_spec, expert_spec), out_specs=row_spec, check_vma=False)
```

time: 713 us -> 432 us (0.61); the launches traced: 712 us -> 424 us
  waiting for transfers between devices: 330 us -> 53.3 us
  Pallas kernels: 0 us -> 247 us
  matrix products: 195 us -> 75.8 us
  local copies, waits for them, and re-layouts: 115 us -> 11.7 us
  other arithmetic: 44 us -> 23.7 us
  between operations: 13.6 us -> 0.66 us
    all_to_all x2 -> x0, waiting for transfers between devices: 270 us -> none  [the longest x1 192 us: local_layer(): lax.all_to_all(expert_out, 'ep', 1, 1, tiled=True).reshape(n_rows, d_model)]
    pallas_call x0 -> x8, Pallas kernels: none -> 247 us  [the longest x4 111 us: expert_partial(): pl.pallas_call(functools.partial(partial_kernel, cap, tok_dev), grid=(loc...]
    dot_general x3 -> x0, matrix products: 140 us -> none  [the longest x1 49.2 us: local_layer(): jnp.einsum('lscd,ldf->lscf', recv_rows, expert_w1, preferred_element_type...]
    gather x3 -> x0, local copies, waits for them, and re-layouts: 73 us -> none  [the longest x2 37.9 us: local_layer(): routed = jnp.take(back_rows, row_code, axis=0, mode='fill', fill_value=0)]
    all_gather x1 -> x0, waiting for transfers between devices: 58.9 us -> none  [local_layer(): group_rows = lax.all_gather(tokens, 'tp', axis=0, tiled=True)]
    ppermute x0 -> x16, waiting for transfers between devices: none -> 53.3 us  [the longest x1 52.4 us: local_layer(): shared_back = lax.ppermute(shared_other, 'tp', tp_swap)]
    reduce_sum x1 -> x0, other arithmetic: 20.6 us -> none  [local_layer(): routed_sum = jnp.sum(gates[:, :, None] * routed.astype(jnp.float32), axis=1)]
    convert_element_type x1 -> x0, local copies, waits for them, and re-layouts: 16.2 us -> none  [local_layer(): jnp.einsum('lscf,lfd->lscd', hidden, expert_w2, preferred_element_type=jn...]
  transfers between devices with their start and end apart: 4 -> 16, of which waited for: 3 -> 2; matrix products, arithmetic and copies ran while one was open for 40% -> 22% of each run, Pallas kernels for 0% -> 13%
where the time goes in v1:
time: 432 us; the launch traced here: 424 us
  Pallas kernels  247 us (57%)
  matrix products  75.8 us (18%)
  waiting for transfers between devices  53.3 us (12%)
  other arithmetic  23.7 us (5%)
  starting transfers between devices  12.4 us (3%)
  local copies, waits for them, and re-layouts  11.7 us (3%)
    pallas_call x4, Pallas kernels, expert_partial(): pl.pallas_call(functools.partial(partial_kernel, cap, tok_dev), grid=(loc...  111 us
    pallas_call x1, Pallas kernels, expert_hidden(): pl.pallas_call(hidden_kernel, grid=(local_exp,), out_shape=jax.ShapeDtype...  71.6 us
    ppermute x1, waiting for transfers between devices, local_layer(): shared_back = lax.ppermute(shared_other, 'tp', tp_swap)  52.4 us
    dot_general x2, matrix products, swiglu_rows(): return jnp.dot(hidden, w_down, preferred_element_type=jnp.float32)  47.7 us
    pallas_call x1, Pallas kernels, combine_matrix(): pl.pallas_call(functools.partial(combine_kernel, cap), grid=(local_exp,),...  47.6 us
    dot_general x2, matrix products, swiglu_rows(): gate_pre = jnp.dot(token_rows, w_gate, preferred_element_type=jnp.float32)  28.1 us
    pallas_call x2, Pallas kernels, gather_rows(): pl.pallas_call(functools.partial(gather_kernel, cap, group), grid=(local_...  16.2 us
    add x4, other arithmetic, local_layer(): for_chip = part[2] + from_core[1]  11 us
  transfers between devices with their start and end apart: 16, of which 2 were waited for; matrix products, arithmetic and copies ran while one was open for 22% of the time, Pallas kernels for 13%

profile of v1, /device:TPU:0, one launch (start us, length us, event | category | flops | bytes accessed | tf_op | source)
XLA Modules:
  0.0 424.1 jit_solution(3918593747966154990)
XLA Ops:
  1.4 0.9 collective-permute-start.2
  2.3 2.5 collective-permute-start.3
  4.9 1.7 collective-permute-start.6
  6.7 1.5 collective-permute-start
  8.2 12.5 %fusion.35 = f32[512,2816]{1,0:T(8,128)} fusion(bf16[512,2048]{1,0:T(8,128)(2,1)} %first_ref.1, bf16[2048,2816]{1,0:T(8,128)(2,1)} %param.14), kind=kOutput, calls=%fused_computation.58 | convolution fusion | flops 5905580032 | bytes 19398656 | tf_op jit(solution)/shard_map/dot_general | solution.py:19
  21.6 47.6 %combine_matrix.1.combine_ref = bf16[15,2048,216]{2,1,0:T(8,128)(2,1)} custom-call(s32[2048,4]{1,0:T(8,128)S(1)} %bitcast.64, f32[2048,4]{1,0:T(8,128)S(1)} %bitcast.65), custom_call_target="tpu_custom_call" | custom-call | flops 2654208000 | bytes 15728640 | tf_op jit(solution)/shard_map/combine_matrix/pallas_call | solution.py:81
  69.4 8.1 %gather_rows.2.near_ref = bf16[15,144,2048]{2,1,0:T(8,128)(2,1)S(1)} custom-call(s32[2,4,512]{2,1,0:T(4,128)S(1)} %get-tuple-element.9.code_ref, bf16[512,2048]{1,0:T(8,128)(2,1)S(1)} %copy-done.6, bf16[512,2048]{1,0:T(8,128)(2,1)} %collective-permute-done.5.second_ref), custom_call_target="tpu_custom_call" | custom-call | flops 4529848320 | bytes 8847360 | tf_op jit(solution)/shard_map/gather_rows/pallas_call | solution.py:47
  77.5 15.7 %fusion.36 = f32[512,2816]{1,0:T(8,128)} fusion(bf16[512,2048]{1,0:T(8,128)(2,1)} %collective-permute-done, bf16[2048,2816]{1,0:T(8,128)(2,1)} %param.14), kind=kOutput, calls=%fused_computation.59 | convolution fusion | flops 5905580032 | bytes 19398656 | tf_op jit(solution)/shard_map/dot_general | solution.py:19
  93.2 8.1 %gather_rows.3.far_ref = bf16[15,144,2048]{2,1,0:T(8,128)(2,1)S(1)} custom-call(s32[2,4,512]{2,1,0:T(4,128)S(1)} %get-tuple-element.8.code_ref, bf16[512,2048]{1,0:T(8,128)(2,1)} %collective-permute-done.6.first_ref, bf16[512,2048]{1,0:T(8,128)(2,1)S(1)} %collective-permute-done.7.second_ref), custom_call_target="tpu_custom_call" | custom-call | flops 4529848320 | bytes 8847360 | tf_op jit(solution)/shard_map/gather_rows/pallas_call | solution.py:47
  101.3 3.4 copy-done.5
  104.7 71.6 %expert_hidden.1.hidden_ref = bf16[15,288,1408]{2,1,0:T(8,128)(2,1)} custom-call(bf16[15,144,2048]{2,1,0:T(8,128)(2,1)} %copy-done.4, bf16[15,144,2048]{2,1,0:T(8,128)(2,1)} %copy-done.5, bf16[15,2048,1408]{2,1,0:T(8,128)(2,1)} %gate_w_ref.1, bf16[15,2048,1408]{2,1,0:T(8,128)(2,1)} %up_w_ref.1), custom_call_target="tpu_custom_call" | custom-call | flops 49828331520 | bytes 173015040 | tf_op jit(solution)/shard_map/expert_hidden/pallas_call | solution.py:109
  176.3 26.6 %expert_partial.5 = f32[4,512,512]{2,1,0:T(8,128)S(1)} custom-call(bf16[15,288,1408]{2,1,0:T(8,128)(2,1)} %expert_hidden.1.hidden_ref, bf16[15,1408,2048]{2,1,0:T(8,128)(2,1)} %weight_ref.7, bf16[15,2048,216]{2,1,0:T(8,128)(2,1)} %combine_matrix.1.combine_ref), custom_call_target="tpu_custom_call" | custom-call | flops 14281605120 | bytes 49520640 | tf_op jit(solution)/shard_map/expert_partial/pallas_call | solution.py:145
  202.9 28.2 %expert_partial.6 = f32[4,512,512]{2,1,0:T(8,128)S(1)} custom-call(bf16[15,288,1408]{2,1,0:T(8,128)(2,1)} %expert_hidden.1.hidden_ref, bf16[15,1408,2048]{2,1,0:T(8,128)(2,1)} %weight_ref.7, bf16[15,2048,216]{2,1,0:T(8,128)(2,1)} %combine_matrix.1.combine_ref), custom_call_target="tpu_custom_call" | custom-call | flops 14281605120 | bytes 49520640 | tf_op jit(solution)/shard_map/expert_partial/pallas_call | solution.py:145
  231.1 28.2 %expert_partial.7 = f32[4,512,512]{2,1,0:T(8,128)S(1)} custom-call(bf16[15,288,1408]{2,1,0:T(8,128)(2,1)} %expert_hidden.1.hidden_ref, bf16[15,1408,2048]{2,1,0:T(8,128)(2,1)} %weight_ref.7, bf16[15,2048,216]{2,1,0:T(8,128)(2,1)} %combine_matrix.1.combine_ref), custom_call_target="tpu_custom_call" | custom-call | flops 14281605120 | bytes 49520640 | tf_op jit(solution)/shard_map/expert_partial/pallas_call | solution.py:145
  259.3 28.4 %expert_partial.4 = f32[4,512,512]{2,1,0:T(8,128)S(1)} custom-call(bf16[15,288,1408]{2,1,0:T(8,128)(2,1)} %expert_hidden.1.hidden_ref, bf16[15,1408,2048]{2,1,0:T(8,128)(2,1)} %weight_ref.7, bf16[15,2048,216]{2,1,0:T(8,128)(2,1)} %combine_matrix.1.combine_ref), custom_call_target="tpu_custom_call" | custom-call | flops 14281605120 | bytes 49520640 | tf_op jit(solution)/shard_map/expert_partial/pallas_call | solution.py:145
  287.7 1.7 slice.124
  289.7 1.5 slice.132
  291.4 1.6 slice.140
  293.3 1.5 slice.116
  294.9 24.0 %fusion = f32[512,2048]{1,0:T(8,128)} fusion(bf16[2816,2048]{1,0:T(8,128)(2,1)} %param.16, f32[512,2816]{1,0:T(8,128)} %fusion.36, bf16[512,2048]{1,0:T(8,128)(2,1)} %collective-permute-done, bf16[2048,2816]{1,0:T(8,128)(2,1)} %param.15), kind=kOutput, calls=%fused_computation.2 | convolution fusion | flops 11819810816 | bytes 35127296 | tf_op jit(solution)/shard_map/dot_general | solution.py:22
  319.5 1.3 copy-done.9
  320.8 2.4 fusion.14
  323.5 3.0 fusion.8
  326.5 1.5 collective-permute-start.13
  328.1 2.8 fusion.2
  331.4 2.7 fusion.20
  334.1 1.5 collective-permute-start.9
  335.6 23.7 %fusion.26 = f32[512,2048]{1,0:T(8,128)} fusion(bf16[2816,2048]{1,0:T(8,128)(2,1)} %param.16, f32[512,2816]{1,0:T(8,128)} %fusion.35, bf16[512,2048]{1,0:T(8,128)(2,1)S(1)} %copy-done.7, bf16[2048,2816]{1,0:T(8,128)(2,1)} %param.15), kind=kOutput, calls=%fused_computation.41 | convolution fusion | flops 11819810816 | bytes 35127296 | tf_op jit(solution)/shard_map/dot_general | solution.py:22
  359.3 52.4 %collective-permute-done.1 = f32[512,2048]{1,0:T(8,128)} collective-permute-done((f32[512,2048]{1,0:T(8,128)}, f32[512,2048]{1,0:T(8,128)}, u32[]{:S(2)}, u32[]{:S(2)}) %collective-permute-start.1) | collective-permute-done | bytes 4194336 | tf_op jit(solution)/shard_map/ppermute | solution.py:199
  411.7 3.1 fusion.18
  415.7 6.4 %fusion.24 = (bf16[512,512]{1,0:T(8,128)(2,1)S(1)}, bf16[512,512]{1,0:T(8,128)(2,1)S(1)}, bf16[512,512]{1,0:T(8,128)(2,1)S(1)}) fusion(f32[512,512]{1,0:T(8,128)} %collective-permute-done.9, f32[2,512,512]{2,1,0:T(8,128)} %collective-permute-done.8, f32[4,512,512]{2,1,0:T(8,128)} %copy-done.2, f32[512,2048]{1,0:T(8,128)} %collective-permute-done.1, ...), kind=kLoop, calls=%fused_computation.38 | loop fusion | flops 5505024 | bytes 18874368 | tf_op jit(solution)/shard_map/convert_element_type | solution.py:217
  422.1 1.6 pad_maximum_fusion
  (52 shorter events, 5.8 us)
Async XLA Ops:
  1.4 5.2 %collective-permute-start.2 = (f32[8,512]{1,0:T(8,128)S(1)}, f32[8,512]{1,0:T(8,128)S(1)}, u32[]{:S(2)}, u32[]{:S(2)}) collective-permute-start(f32[8,512]{1,0:T(8,128)S(1)} %get-tuple-element.11), channel_id=1, source_target_pairs={{0,1},{1,0},{2,3},{3,2},{4,5},{5,4},{6,7},{7,6}} | collective-permute-start | bytes 49160 | tf_op jit(solution)/shard_map/ppermute | solution.py:184
  2.3 18.4 %collective-permute-start.3 = (f32[8,512]{1,0:T(8,128)S(1)}, f32[8,512]{1,0:T(8,128)S(1)}, u32[]{:S(2)}, u32[]{:S(2)}) collective-permute-start(f32[8,512]{1,0:T(8,128)S(1)} %get-tuple-element.11), channel_id=1, source_target_pairs={{0,2},{1,3},{2,0},{3,1},{4,6},{5,7},{6,4},{7,5}} | collective-permute-start | bytes 49160 | tf_op jit(solution)/shard_map/ppermute | solution.py:184
  4.8 15.9 %collective-permute-start.4 = (f32[8,512]{1,0:T(8,128)S(1)}, f32[8,512]{1,0:T(8,128)S(1)}, u32[]{:S(2)}, u32[]{:S(2)}) collective-permute-start(f32[8,512]{1,0:T(8,128)S(1)} %get-tuple-element.11), channel_id=1, source_target_pairs={{0,3},{1,2},{2,1},{3,0},{4,7},{5,6},{6,5},{7,4}} | collective-permute-start | bytes 49160 | tf_op jit(solution)/shard_map/ppermute | solution.py:184
  4.9 64.3 %collective-permute-start.6 = (bf16[512,2048]{1,0:T(8,128)(2,1)}, bf16[512,2048]{1,0:T(8,128)(2,1)}, u32[]{:S(2)}, u32[]{:S(2)}) collective-permute-start(bf16[512,2048]{1,0:T(8,128)(2,1)} %first_ref.1), channel_id=1, source_target_pairs={{0,2},{1,3},{2,0},{3,1},{4,6},{5,7},{6,4},{7,5}} | collective-permute-start | bytes 6291464 | tf_op jit(solution)/shard_map/ppermute | solution.py:194
  6.6 62.8 %collective-permute-start.5 = (bf16[512,2048]{1,0:T(8,128)(2,1)}, bf16[512,2048]{1,0:T(8,128)(2,1)}, u32[]{:S(2)}, u32[]{:S(2)}) collective-permute-start(bf16[512,2048]{1,0:T(8,128)(2,1)} %first_ref.1), channel_id=1, source_target_pairs={{0,1},{1,0},{2,3},{3,2},{4,5},{5,4},{6,7},{7,6}} | collective-permute-start | bytes 6291464 | tf_op jit(solution)/shard_map/ppermute | solution.py:193
  6.7 70.9 %collective-permute-start = (bf16[512,2048]{1,0:T(8,128)(2,1)}, bf16[512,2048]{1,0:T(8,128)(2,1)}, u32[]{:S(2)}, u32[]{:S(2)}) collective-permute-start(bf16[512,2048]{1,0:T(8,128)(2,1)} %first_ref.1), channel_id=1, source_target_pairs={{0,4},{4,0},{1,5},{5,1},{2,6},{6,2},{3,7},{7,3}} | collective-permute-start | bytes 6291464 | tf_op jit(solution)/shard_map/ppermute | solution.py:192
  21.6 47.8 %copy-start.6 = (bf16[512,2048]{1,0:T(8,128)(2,1)S(1)}, bf16[512,2048]{1,0:T(8,128)(2,1)}, u32[]{:S(2)}) copy-start(bf16[512,2048]{1,0:T(8,128)(2,1)} %first_ref.1) | copy-start | bytes 6291460
  69.2 24.0 %collective-permute-start.7 = (bf16[512,2048]{1,0:T(8,128)(2,1)}, bf16[512,2048]{1,0:T(8,128)(2,1)S(1)}, u32[]{:S(2)}, u32[]{:S(2)}) collective-permute-start(bf16[512,2048]{1,0:T(8,128)(2,1)} %collective-permute-done.6.first_ref), channel_id=1, source_target_pairs={{0,1},{1,0},{2,3},{3,2},{4,5},{5,4},{6,7},{7,6}} | collective-permute-start | bytes 6291464 | tf_op jit(solution)/shard_map/ppermute | solution.py:195
  77.5 15.7 %copy-start.4 = (bf16[15,144,2048]{2,1,0:T(8,128)(2,1)}, bf16[15,144,2048]{2,1,0:T(8,128)(2,1)S(1)}, u32[]{:S(2)}) copy-start(bf16[15,144,2048]{2,1,0:T(8,128)(2,1)S(1)} %gather_rows.2.near_ref) | copy-start | bytes 26542084
  101.3 3.4 copy-start.5
  202.9 84.7 %copy-start.3 = (f32[4,512,512]{2,1,0:T(8,128)}, f32[4,512,512]{2,1,0:T(8,128)S(1)}, u32[]{:S(2)}) copy-start(f32[4,512,512]{2,1,0:T(8,128)S(1)} %expert_partial.5) | copy-start | bytes 12582916
  231.1 58.6 %copy-start = (f32[4,512,512]{2,1,0:T(8,128)}, f32[4,512,512]{2,1,0:T(8,128)S(1)}, u32[]{:S(2)}) copy-start(f32[4,512,512]{2,1,0:T(8,128)S(1)} %expert_partial.6) | copy-start | bytes 12582916
  259.3 32.1 %copy-start.1 = (f32[4,512,512]{2,1,0:T(8,128)}, f32[4,512,512]{2,1,0:T(8,128)S(1)}, u32[]{:S(2)}) copy-start(f32[4,512,512]{2,1,0:T(8,128)S(1)} %expert_partial.7) | copy-start | bytes 12582916
  287.7 5.6 %copy-start.2 = (f32[4,512,512]{2,1,0:T(8,128)}, f32[4,512,512]{2,1,0:T(8,128)S(1)}, u32[]{:S(2)}) copy-start(f32[4,512,512]{2,1,0:T(8,128)S(1)} %expert_partial.4) | copy-start | bytes 12582916
  289.3 30.1 %collective-permute-start.10 = (f32[2,512,512]{2,1,0:T(8,128)}, f32[2,512,512]{2,1,0:T(8,128)S(1)}, u32[]{:S(2)}, u32[]{:S(2)}) collective-permute-start(f32[2,512,512]{2,1,0:T(8,128)} %slice.124), channel_id=1, source_target_pairs={{0,1},{1,0},{2,3},{3,2},{4,5},{5,4},{6,7},{7,6}} | collective-permute-start | bytes 6291464 | tf_op jit(solution)/shard_map/ppermute | solution.py:211
  291.2 32.3 %collective-permute-start.12 = (f32[2,512,512]{2,1,0:T(8,128)}, f32[2,512,512]{2,1,0:T(8,128)}, u32[]{:S(2)}, u32[]{:S(2)}) collective-permute-start(f32[2,512,512]{2,1,0:T(8,128)} %slice.132), channel_id=1, source_target_pairs={{0,1},{1,0},{2,3},{3,2},{4,5},{5,4},{6,7},{7,6}} | collective-permute-start | bytes 6291464 | tf_op jit(solution)/shard_map/ppermute | solution.py:211
  292.9 35.1 %collective-permute-start.14 = (f32[2,512,512]{2,1,0:T(8,128)}, f32[2,512,512]{2,1,0:T(8,128)}, u32[]{:S(2)}, u32[]{:S(2)}) collective-permute-start(f32[2,512,512]{2,1,0:T(8,128)} %slice.140), channel_id=1, source_target_pairs={{0,1},{1,0},{2,3},{3,2},{4,5},{5,4},{6,7},{7,6}} | collective-permute-start | bytes 6291464 | tf_op jit(solution)/shard_map/ppermute | solution.py:211
  294.8 36.6 %collective-permute-start.8 = (f32[2,512,512]{2,1,0:T(8,128)}, f32[2,512,512]{2,1,0:T(8,128)}, u32[]{:S(2)}, u32[]{:S(2)}) collective-permute-start(f32[2,512,512]{2,1,0:T(8,128)} %slice.116), channel_id=1, source_target_pairs={{0,1},{1,0},{2,3},{3,2},{4,5},{5,4},{6,7},{7,6}} | collective-permute-start | bytes 6291464 | tf_op jit(solution)/shard_map/ppermute | solution.py:211
  318.9 92.8 %collective-permute-start.1 = (f32[512,2048]{1,0:T(8,128)}, f32[512,2048]{1,0:T(8,128)}, u32[]{:S(2)}, u32[]{:S(2)}) collective-permute-start(f32[512,2048]{1,0:T(8,128)} %fusion), channel_id=1, source_target_pairs={{0,4},{4,0},{1,5},{5,1},{2,6},{6,2},{3,7},{7,3}} | collective-permute-start | bytes 12582920 | tf_op jit(solution)/shard_map/ppermute | solution.py:199
  319.5 1.3 copy-start.9
  323.2 12.4 %copy-start.7 = (bf16[512,2048]{1,0:T(8,128)(2,1)S(1)}, bf16[512,2048]{1,0:T(8,128)(2,1)}, u32[]{:S(2)}) copy-start(bf16[512,2048]{1,0:T(8,128)(2,1)} %first_ref.1) | copy-start | bytes 6291460
  323.2 88.5 %collective-permute-start.11 = (f32[512,512]{1,0:T(8,128)}, f32[512,512]{1,0:T(8,128)}, u32[]{:S(2)}, u32[]{:S(2)}) collective-permute-start(f32[512,512]{1,0:T(8,128)} %fusion.14), channel_id=1, source_target_pairs={{0,2},{1,3},{2,0},{3,1},{4,6},{5,7},{6,4},{7,5}} | collective-permute-start | bytes 3145736 | tf_op jit(solution)/shard_map/ppermute | solution.py:213
  326.5 88.4 %collective-permute-start.13 = (f32[512,512]{1,0:T(8,128)}, f32[512,512]{1,0:T(8,128)S(1)}, u32[]{:S(2)}, u32[]{:S(2)}) collective-permute-start(f32[512,512]{1,0:T(8,128)} %fusion.8), channel_id=1, source_target_pairs={{0,2},{1,3},{2,0},{3,1},{4,6},{5,7},{6,4},{7,5}} | collective-permute-start | bytes 3145736 | tf_op jit(solution)/shard_map/ppermute | solution.py:213
  330.9 84.0 %collective-permute-start.15 = (f32[512,512]{1,0:T(8,128)}, f32[512,512]{1,0:T(8,128)}, u32[]{:S(2)}, u32[]{:S(2)}) collective-permute-start(f32[512,512]{1,0:T(8,128)} %fusion.2), channel_id=1, source_target_pairs={{0,2},{1,3},{2,0},{3,1},{4,6},{5,7},{6,4},{7,5}} | collective-permute-start | bytes 3145736 | tf_op jit(solution)/shard_map/ppermute | solution.py:213
  334.1 81.6 %collective-permute-start.9 = (f32[512,512]{1,0:T(8,128)}, f32[512,512]{1,0:T(8,128)}, u32[]{:S(2)}, u32[]{:S(2)}) collective-permute-start(f32[512,512]{1,0:T(8,128)} %fusion.20), channel_id=1, source_target_pairs={{0,2},{1,3},{2,0},{3,1},{4,6},{5,7},{6,4},{7,5}} | collective-permute-start | bytes 3145736 | tf_op jit(solution)/shard_map/ppermute | solution.py:213
  359.3 56.4 %copy-start.8 = (f32[512,2048]{1,0:T(8,128)S(1)}, f32[512,2048]{1,0:T(8,128)}, u32[]{:S(2)}) copy-start(f32[512,2048]{1,0:T(8,128)} %fusion.26) | copy-start | bytes 12582916

commit v2 on v0

v2 whole, which is shorter than its diff:
```python
import functools

import jax
import jax.numpy as jnp
from jax import lax
from jax.experimental import pallas as pl
from jax.experimental.pallas import tpu as pltpu
from jax.sharding import PartitionSpec as P

COL_BLOCKS = 8
GROUP = 3
FEW_SLOTS = 48
MESH = pl.DeviceIdType.MESH
GATE_MAX = 3.3895313892515355e38


def capacity_rows(tok_dev, top_k, n_exp):
    return 8 * max(1, (2 * tok_dev * top_k + 8 * n_exp - 1) // (8 * n_exp))


ANY = pl.BlockSpec(memory_space=pl.ANY)


def params():
    return pltpu.CompilerParams(vmem_limit_bytes=62 * 2**20)


def cost(flops, nbytes):
    return pl.CostEstimate(flops=flops, bytes_accessed=nbytes, transcendentals=0)


def gather_kernel(cap, few_ref, code_ref, first_ref, second_ref, after_ref, out_ref):
    rows = GROUP * cap
    base = pl.program_id(0) * GROUP
    slot = lax.broadcasted_iota(jnp.int32, (rows, code_ref.shape[2]), 0) + base * cap
    for source, tok_ref in enumerate((first_ref, second_ref)):
        code = code_ref[source]
        hit = slot == code[0:1, :]
        for j in range(1, code.shape[0]):
            hit = hit | (slot == code[j : j + 1, :])
        pick = jnp.where(hit, 1.0, 0.0).astype(jnp.bfloat16)
        picked = jnp.dot(pick, tok_ref[...], preferred_element_type=jnp.float32).astype(jnp.bfloat16)
        for k in range(GROUP):

            @pl.when(few_ref[base + k] == 1)
            def _():
                out_ref[k, source * FEW_SLOTS : (source + 1) * FEW_SLOTS, :] = picked[k * cap : k * cap + FEW_SLOTS, :]

            @pl.when(few_ref[base + k] == 0)
            def _():
                out_ref[k, source * cap : (source + 1) * cap, :] = picked[k * cap : (k + 1) * cap, :]


def gather_rows(few, codes, first, second, after, local_exp, cap):
    tok_dev, d_model = first.shape
    rows = 2 * local_exp * cap
    tok_spec = pl.BlockSpec((tok_dev, d_model), lambda b, few: (0, 0))
    return pl.pallas_call(
        functools.partial(gather_kernel, cap),
        grid_spec=pltpu.PrefetchScalarGridSpec(
            num_scalar_prefetch=1,
            grid=(local_exp // GROUP,),
            in_specs=[pl.BlockSpec(codes.shape, lambda b, few: (0, 0, 0)), tok_spec, tok_spec, ANY],
            out_specs=pl.BlockSpec((GROUP, 2 * cap, d_model), lambda b, few: (b, 0, 0)),
        ),
        out_shape=jax.ShapeDtypeStruct((local_exp, 2 * cap, d_model), jnp.bfloat16),
        compiler_params=params(),
        cost_estimate=cost(2 * rows * tok_dev * d_model, 2 * rows * d_model),
        name="gather_rows",
    )(few, codes, first, second, after)


def combine_kernel(cap, slot_ref, gate_ref, out_ref):
    gate = gate_ref[...]
    high = jnp.minimum(gate, GATE_MAX).astype(jnp.bfloat16).astype(jnp.float32)
    rest = gate - high
    middle = rest.astype(jnp.bfloat16).astype(jnp.float32)
    pieces = (high, middle, rest - middle)
    lane = lax.broadcasted_iota(jnp.int32, (gate.shape[0], 256), 1)
    for g in range(out_ref.shape[0]):
        values = [jnp.zeros(lane.shape, jnp.float32)] * 3
        for k in range(GROUP):
            e = g * GROUP + k
            hit = lane == slot_ref[:, e : e + 1] + k * cap
            values = [jnp.where(hit, piece[:, e : e + 1], value) for piece, value in zip(pieces, values)]
        for i, value in enumerate(values):
            out_ref[g, :, i * 256 : (i + 1) * 256] = value.astype(jnp.bfloat16)


def combine_matrix(slot_of, gate_of, cap):
    rows, local_exp = slot_of.shape
    step = 128
    n_groups = local_exp // GROUP
    in_spec = pl.BlockSpec((step, local_exp), lambda i: (i, 0))
    return pl.pallas_call(
        functools.partial(combine_kernel, cap),
        grid=(rows // step,),
        out_shape=jax.ShapeDtypeStruct((n_groups, rows, 768), jnp.bfloat16),
        in_specs=[in_spec, in_spec],
        out_specs=pl.BlockSpec((n_groups, step, 768), lambda i: (0, i, 0)),
        compiler_params=params(),
        cost_estimate=cost(n_groups * rows * 768 * 500, n_groups * rows * 1536),
        name="combine_matrix",
    )(slot_of, gate_of)


def swiglu_cols(rows, gate_w_ref, up_w_ref, cols):
    gate_pre = jnp.dot(rows, gate_w_ref[0, :, cols], preferred_element_type=jnp.float32)
    up_pre = jnp.dot(rows, up_w_ref[0, :, cols], preferred_element_type=jnp.float32)
    return jax.nn.silu(gate_pre) * up_pre


def hidden_kernel(cap, few_ref, near_ref, far_ref, gate_w_ref, up_w_ref, out_ref):
    few = few_ref[pl.program_id(0)]
    width = out_ref.shape[2]
    spans = [slice(start, min(start + 256, width)) for start in range(0, width, 256)]

    @pl.when(few == 1)
    def _():
        half = 2 * FEW_SLOTS
        rows = jnp.concatenate([near_ref[0, :half], far_ref[0, :half]], axis=0)
        for cols in spans:
            hidden = swiglu_cols(rows, gate_w_ref, up_w_ref, cols)
            gap = jnp.zeros((cap - FEW_SLOTS, hidden.shape[1]), jnp.float32)
            pieces = []
            for source in range(4):
                pieces += [hidden[source * FEW_SLOTS : (source + 1) * FEW_SLOTS], gap]
            out_ref[0, :, cols] = jnp.concatenate(pieces, axis=0).astype(jnp.bfloat16)

    @pl.when(few == 0)
    def _():
        rows = jnp.concatenate([near_ref[0], far_ref[0]], axis=0)
        for cols in spans:
            out_ref[0, :, cols] = swiglu_cols(rows, gate_w_ref, up_w_ref, cols).astype(jnp.bfloat16)


def expert_hidden(few, near, far, w_gate, w_up):
    local_exp, half, d_model = near.shape
    width = w_gate.shape[2]
    row_spec = pl.BlockSpec((1, half, d_model), lambda e, few: (e, 0, 0))
    weight_spec = pl.BlockSpec((1, d_model, width), lambda e, few: (e, 0, 0))
    return pl.pallas_call(
        functools.partial(hidden_kernel, half // 2),
        grid_spec=pltpu.PrefetchScalarGridSpec(
            num_scalar_prefetch=1,
            grid=(local_exp,),
            in_specs=[row_spec, row_spec, weight_spec, weight_spec],
            out_specs=pl.BlockSpec((1, 2 * half, width), lambda e, few: (e, 0, 0)),
        ),
        out_shape=jax.ShapeDtypeStruct((local_exp, 2 * half, width), jnp.bfloat16),
        compiler_params=params(),
        cost_estimate=cost(local_exp * 2 * half * d_model * width * 4, local_exp * d_model * width * 4),
        name="expert_hidden",
    )(few, near, far, w_gate, w_up)


def shared_hidden_kernel(row_ref, gate_w_ref, up_w_ref, after_ref, out_ref):
    rows = row_ref[...]
    gate_pre = jnp.dot(rows, gate_w_ref[...], preferred_element_type=jnp.float32)
    up_pre = jnp.dot(rows, up_w_ref[...], preferred_element_type=jnp.float32)
    out_ref[...] = (jax.nn.silu(gate_pre) * up_pre).astype(jnp.bfloat16)


def shared_hidden(rows, w_gate, w_up, after):
    n_rows, d_model = rows.shape
    width = w_gate.shape[1]
    step = 256
    weight_spec = pl.BlockSpec((d_model, step), lambda i: (0, i))
    return pl.pallas_call(
        shared_hidden_kernel,
        grid=(width // step,),
        out_shape=jax.ShapeDtypeStruct((n_rows, width), jnp.bfloat16),
        in_specs=[pl.BlockSpec((n_rows, d_model), lambda i: (0, 0)), weight_spec, weight_spec, ANY],
        out_specs=pl.BlockSpec((n_rows, step), lambda i: (0, i)),
        compiler_params=params(),
        cost_estimate=cost(4 * n_rows * d_model * width, 4 * d_model * width),
        name="shared_hidden",
    )(rows, w_gate, w_up, after)


def shared_down_kernel(hidden_ref, weight_ref, after_ref, out_ref):
    out_ref[...] = jnp.dot(hidden_ref[...], weight_ref[...], preferred_element_type=jnp.float32)


def shared_down(hidden, w_down, after):
    n_rows, width = hidden.shape
    d_model = w_down.shape[1]
    step = 512
    return pl.pallas_call(
        shared_down_kernel,
        grid=(d_model // step,),
        out_shape=jax.ShapeDtypeStruct((n_rows, d_model), jnp.float32),
        in_specs=[pl.BlockSpec((n_rows, width), lambda i: (0, 0)), pl.BlockSpec((width, step), lambda i: (0, i)), ANY],
        out_specs=pl.BlockSpec((n_rows, step), lambda i: (0, i)),
        compiler_params=params(),
        cost_estimate=cost(2 * n_rows * d_model * width, 2 * d_model * width + 4 * n_rows * d_model),
        name="shared_down",
    )(hidden, w_down, after)


def finish_kernel(
    cap, n_blocks, hidden_hbm, combine_hbm, base_ref, weight_ref, out_ref,
    hidden, combine, total, from_core, from_chip,
    hidden_sem, combine_sem, core_send, core_recv, chip_send, chip_recv,
):
    block, group = pl.program_id(0), pl.program_id(1)
    n_groups = pl.num_programs(1)
    last_group = n_groups - 1
    tok_dev, cols = base_ref.shape
    me = lax.axis_index("ep")
    dp, tp = lax.axis_index("dp"), lax.axis_index("tp")
    core = (dp, tp, me + 1 - 2 * lax.rem(me, 2))
    chip = (dp, tp, lax.rem(me + 2, 4))

    def load(g):
        return (
            pltpu.make_async_copy(hidden_hbm.at[pl.ds(g * GROUP, GROUP)], hidden.at[pl.ds(g * GROUP, GROUP)], hidden_sem.at[g]),
            pltpu.make_async_copy(combine_hbm.at[g], combine.at[g], combine_sem.at[g]),
        )

    def core_copy(n):
        return pltpu.make_async_remote_copy(
            src_ref=total.at[lax.rem(n, 2), pl.ds(2, 2)], dst_ref=from_core.at[n],
            send_sem=core_send.at[n], recv_sem=core_recv.at[n], device_id=core, device_id_type=MESH,
        )

    def chip_copy(n):
        return pltpu.make_async_remote_copy(
            src_ref=from_core.at[n, 1], dst_ref=from_chip.at[n],
            send_sem=chip_send.at[n], recv_sem=chip_recv.at[n], device_id=chip, device_id_type=MESH,
        )

    def forward(n):
        core_copy(n).wait()
        from_core[n] += total[lax.rem(n, 2), 0:2]
        chip_copy(n).start()

    def finalize(n):
        chip_copy(n).wait()
        here = pl.ds(pl.multiple_of(n * cols, cols), cols)
        out_ref[:, here] = (from_core[n, 0] + from_chip[n]).astype(jnp.bfloat16)

    @pl.when((block == 0) & (group == 0))
    def _():
        for g in range(hidden_sem.shape[0]):
            for copy in load(g):
                copy.start()
        barrier = pltpu.get_barrier_semaphore()
        for peer in (core, chip):
            pl.semaphore_signal(barrier, inc=1, device_id=peer, device_id_type=MESH)
        pl.semaphore_wait(barrier, 2)

    @pl.when(block == 0)
    def _():
        for copy in load(group):
            copy.wait()

    slot = lax.rem(block, 2)

    @pl.when(group == 0)
    def _():
        total[slot, 0] = base_ref[...]
        for s in range(1, 4):
            total[slot, s] = jnp.zeros((tok_dev, cols), jnp.float32)

    results = []
    for k in range(GROUP):
        results.append(jnp.dot(hidden[group * GROUP + k], weight_ref[k], preferred_element_type=jnp.float32))
    gap = jnp.zeros((256 - GROUP * cap, cols), jnp.float32)
    for source, place in enumerate((0, 2, 1, 3)):
        rows = jnp.concatenate([r[source * cap : (source + 1) * cap] for r in results] + [gap], axis=0).astype(jnp.bfloat16)
        rows = jnp.concatenate([rows, rows, rows], axis=0)
        gates = combine[group, source * tok_dev : (source + 1) * tok_dev, :]
        total[slot, place] += jnp.dot(gates, rows, preferred_element_type=jnp.float32)

    @pl.when((group == 1) & (block >= 1))
    def _():
        forward(block - 1)

    @pl.when((group == 3) & (block >= 4))
    def _():
        finalize(block - 4)

    @pl.when(group == last_group)
    def _():
        core_copy(block).start()

    @pl.when((group == last_group) & (block == n_blocks - 1))
    def _():
        forward(block)
        for n in range(n_blocks - 4, n_blocks):
            finalize(n)


def finish(hidden, combine, base, w_down):
    local_exp, rows, width = hidden.shape
    n_groups, _, depth = combine.shape
    tok_dev, d_model = base.shape
    cols = d_model // COL_BLOCKS
    sems = pltpu.SemaphoreType.DMA((COL_BLOCKS,))
    return pl.pallas_call(
        functools.partial(finish_kernel, rows // 4, COL_BLOCKS),
        grid=(COL_BLOCKS, n_groups),
        out_shape=jax.ShapeDtypeStruct((tok_dev, d_model), jnp.bfloat16),
        in_specs=[
            ANY,
            ANY,
            pl.BlockSpec((tok_dev, cols), lambda n, g: (0, n)),
            pl.BlockSpec((GROUP, width, cols), lambda n, g: (g, 0, n)),
        ],
        out_specs=pl.BlockSpec((tok_dev, d_model), lambda n, g: (0, 0)),
        scratch_shapes=[
            pltpu.VMEM(hidden.shape, jnp.bfloat16),
            pltpu.VMEM(combine.shape, jnp.bfloat16),
            pltpu.VMEM((2, 4, tok_dev, cols), jnp.float32),
            pltpu.VMEM((COL_BLOCKS, 2, tok_dev, cols), jnp.float32),
            pltpu.VMEM((COL_BLOCKS, tok_dev, cols), jnp.float32),
            pltpu.SemaphoreType.DMA((n_groups,)),
            pltpu.SemaphoreType.DMA((n_groups,)),
            sems, sems, sems, sems,
        ],
        compiler_params=pltpu.CompilerParams(
            collective_id=0, has_side_effects=True, vmem_limit_bytes=62 * 2**20, dimension_semantics=("arbitrary", "arbitrary")
        ),
        cost_estimate=cost(2 * d_model * local_exp * (rows * width + 4 * tok_dev * 256), 2 * local_exp * width * d_model),
        name="finish",
    )(hidden, combine, base, w_down)


def solution(mesh):
    ep_size = mesh.shape["ep"]
    tp_size = mesh.shape["tp"]
    row_spec = P(("dp", "ep", "tp"), None)
    expert_spec = P("ep", None, None)
    core_swap = [(i, i ^ 1) for i in range(ep_size)]
    chip_swap = [(i, i ^ 2) for i in range(ep_size)]
    both_swap = [(i, i ^ 3) for i in range(ep_size)]
    tp_swap = [(i, i ^ 1) for i in range(tp_size)]

    def local_layer(tokens, expert_ids, gates, slots, shared_w1, shared_w3, shared_w2, expert_w1, expert_w3, expert_w2):
        tok_dev, d_model = tokens.shape
        top_k = expert_ids.shape[1]
        local_exp = expert_w1.shape[0]
        cap = capacity_rows(tok_dev, top_k, local_exp * ep_size)
        me = lax.axis_index("ep")

        tok_core = lax.ppermute(tokens, "ep", core_swap)
        half = tok_dev // 2
        other_parts = [lax.ppermute(tokens[i * half : (i + 1) * half], "tp", tp_swap) for i in range(2)]
        tok_chip = lax.ppermute(tokens, "ep", chip_swap)
        tok_both = lax.ppermute(tok_chip, "ep", core_swap)

        code = jnp.where(slots >= 0, expert_ids * cap + slots, -1)
        meta = jnp.concatenate([code.astype(jnp.float32).T, gates.T], axis=0)
        metas = [meta] + [lax.ppermute(meta, "ep", perm) for perm in (core_swap, chip_swap, both_swap)]
        metas = jnp.stack(metas)
        codes = metas[:, :top_k].astype(jnp.int32)
        first = me * (local_exp * cap)
        codes = jnp.where((codes >= first) & (codes < first + local_exp * cap), codes - first, -1)
        experts = jnp.arange(local_exp, dtype=jnp.int32)[:, None, None, None] * cap
        inside = (codes[None] >= experts) & (codes[None] < experts + cap)
        slot_of = jnp.max(jnp.where(inside, codes[None] - experts, -1024), axis=2)
        gate_of = jnp.sum(jnp.where(inside, metas[None, :, top_k:], 0.0), axis=2)
        few = (jnp.max(slot_of, axis=(1, 2)) < FEW_SLOTS).astype(jnp.int32)
        slot_of = slot_of.reshape(local_exp, ep_size * tok_dev).T
        gate_of = gate_of.reshape(local_exp, ep_size * tok_dev).T

        combine = combine_matrix(slot_of, gate_of, cap)
        near = gather_rows(few, codes[:2], tokens, tok_core, combine, local_exp, cap)
        hidden_0 = shared_hidden(other_parts[0], shared_w1, shared_w3, near)
        back_0 = lax.ppermute(shared_down(hidden_0, shared_w2, hidden_0), "tp", tp_swap)
        hidden_own = shared_hidden(tokens, shared_w1, shared_w3, hidden_0)
        hidden_1 = shared_hidden(other_parts[1], shared_w1, shared_w3, hidden_own)
        down_1 = shared_down(hidden_1, shared_w2, tok_chip)
        back_1 = lax.ppermute(down_1, "tp", tp_swap)
        far = gather_rows(few, codes[2:], tok_chip, tok_both, down_1, local_exp, cap)
        hidden = expert_hidden(few, near, far, expert_w1, expert_w3)
        shared_own = shared_down(hidden_own, shared_w2, hidden)
        base = tokens.astype(jnp.float32) + shared_own + jnp.concatenate([back_0, back_1], axis=0)
        return finish(hidden, combine, base, expert_w2)

    return jax.shard_map(local_layer, mesh=mesh, in_specs=(row_spec, row_spec, row_spec, row_spec, P(None, "tp"), P(None, "tp"), P("tp", None), expert_spec, expert_spec, expert_spec), out_specs=row_spec, check_vma=False)
```

time: 713 us -> 360 us (0.50)
  waiting for transfers between devices: 330 us -> 18.7 us
  Pallas kernels: 0 us -> 307 us
  matrix products: 195 us -> 0 us
  local copies, waits for them, and re-layouts: 115 us -> 10.6 us
  other arithmetic: 44 us -> 11.2 us
  between operations: 13.6 us -> 0.06 us
    pallas_call x0 -> x11, Pallas kernels: none -> 307 us  [the longest x1 123 us: finish(): pl.pallas_call(functools.partial(finish_kernel, rows // 4, COL_BLOCKS), g...]
    all_to_all x2 -> x0, waiting for transfers between devices: 270 us -> none  [the longest x1 192 us: local_layer(): lax.all_to_all(expert_out, 'ep', 1, 1, tiled=True).reshape(n_rows, d_model)]
    dot_general x5 -> x0, matrix products: 195 us -> none  [the longest x1 49.2 us: local_layer(): jnp.einsum('lscd,ldf->lscf', recv_rows, expert_w1, preferred_element_type...]
    gather x3 -> x0, local copies, waits for them, and re-layouts: 73 us -> none  [the longest x2 37.9 us: local_layer(): routed = jnp.take(back_rows, row_code, axis=0, mode='fill', fill_value=0)]
    all_gather x1 -> x0, waiting for transfers between devices: 58.9 us -> none  [local_layer(): group_rows = lax.all_gather(tokens, 'tp', axis=0, tiled=True)]
    reduce_sum x1, other arithmetic: 20.6 us -> 0.48 us  [local_layer(): gate_of = jnp.sum(jnp.where(inside, metas[None, :, top_k:], 0.0), axis=2)]
    ppermute x0 -> x10, waiting for transfers between devices: none -> 18.7 us  [the longest x1 18.7 us: local_layer(): tok_chip = lax.ppermute(tokens, 'ep', chip_swap)]
    convert_element_type x1 -> x0, local copies, waits for them, and re-layouts: 16.2 us -> none  [local_layer(): jnp.einsum('lscf,lfd->lscd', hidden, expert_w2, preferred_element_type=jn...]
  transfers between devices with their start and end apart: 4 -> 10, of which waited for: 3 -> 1; matrix products, arithmetic and copies ran while one was open for 40% -> 2% of each run, Pallas kernels for 0% -> 52%
where the time goes in v2:
time: 360 us; the launch traced here: 357 us
  Pallas kernels  307 us (85%)
  waiting for transfers between devices  18.7 us (5%)
  other arithmetic  11.2 us (3%)
  local copies, waits for them, and re-layouts  10.6 us (3%)
  starting transfers between devices  9.58 us (3%)
    pallas_call x1, Pallas kernels, finish(): pl.pallas_call(functools.partial(finish_kernel, rows // 4, COL_BLOCKS), g...  123 us
    pallas_call x1, Pallas kernels, expert_hidden(): pl.pallas_call(functools.partial(hidden_kernel, half // 2), grid_spec=plt...  66.4 us
    pallas_call x3, Pallas kernels, shared_hidden(): pl.pallas_call(shared_hidden_kernel, grid=(width // step,), out_shape=jax...  49.6 us
    pallas_call x3, Pallas kernels, shared_down(): pl.pallas_call(shared_down_kernel, grid=(d_model // step,), out_shape=jax...  27.2 us
    pallas_call x2, Pallas kernels, gather_rows(): pl.pallas_call(functools.partial(gather_kernel, cap), grid_spec=pltpu.Pre...  24.2 us
    ppermute x1, waiting for transfers between devices, local_layer(): tok_chip = lax.ppermute(tokens, 'ep', chip_swap)  18.7 us
    pallas_call x1, Pallas kernels, combine_matrix(): pl.pallas_call(functools.partial(combine_kernel, cap), grid=(rows // step...  16.8 us
    add x1, other arithmetic, local_layer(): tokens.astype(jnp.float32) + shared_own  7.62 us
  transfers between devices with their start and end apart: 10, of which 1 were waited for; matrix products, arithmetic and copies ran while one was open for 2% of the time, Pallas kernels for 52%

profile of v2, /device:TPU:0, one launch (start us, length us, event | category | flops | bytes accessed | tf_op | source)
XLA Modules:
  0.0 357.4 jit_solution(8276079659926714373)
XLA Ops:
  0.0 0.7 convert_bitcast_fusion
  0.7 0.7 fusion.2
  1.4 0.9 collective-permute-start
  2.3 2.5 collective-permute-start.1
  4.9 0.1 collective-permute-start.3
  5.0 1.9 collective-permute-start.4
  6.9 3.1 fusion.3
  10.1 1.5 collective-permute-start.7
  11.6 0.5 collective-permute-start.6
  12.2 1.0 fusion
  13.2 0.6 compare_convert_fusion.few_ref
  13.8 0.5 select_reduce_fusion
  14.3 1.4 copy.12
  15.7 1.3 copy.11
  17.0 0.6 fusion.4
  17.6 16.8 %combine_matrix.1.after_ref.combine_hbm = bf16[5,2048,768]{2,1,0:T(8,128)(2,1)} custom-call(s32[2048,15]{1,0:T(8,128)} %bitcast.15, f32[2048,15]{1,0:T(8,128)} %bitcast.14), custom_call_target="tpu_custom_call" | custom-call | flops 3932160000 | bytes 15728640 | tf_op jit(solution)/shard_map/combine_matrix/pallas_call | solution.py:95
  34.4 18.7 %collective-permute-done.4.after_ref.first_ref = bf16[512,2048]{1,0:T(8,128)(2,1)} collective-permute-done((bf16[512,2048]{1,0:T(8,128)(2,1)}, bf16[512,2048]{1,0:T(8,128)(2,1)}, u32[]{:S(2)}, u32[]{:S(2)}) %collective-permute-start.4) | collective-permute-done | bytes 2097184 | tf_op jit(solution)/shard_map/ppermute | solution.py:350
  53.1 12.1 %gather_rows.2.after_ref.near_ref = bf16[15,144,2048]{2,1,0:T(8,128)(2,1)} custom-call(s32[15]{0:T(128)} %compare_convert_fusion.few_ref, s32[2,4,512]{2,1,0:T(4,128)} %get-tuple-element.10.code_ref, bf16[512,2048]{1,0:T(8,128)(2,1)} %row_ref.1, bf16[512,2048]{1,0:T(8,128)(2,1)} %collective-permute-done.3.second_ref, ...), custom_call_target="tpu_custom_call" | custom-call | flops 4529848320 | bytes 8847360 | tf_op jit(solution)/shard_map/gather_rows/pallas_call | solution.py:58
  65.2 15.3 %shared_hidden.3.after_ref.hidden_ref = bf16[256,2816]{1,0:T(8,128)(2,1)} custom-call(bf16[256,2048]{1,0:T(8,128)(2,1)} %collective-permute-done.7.row_ref, bf16[2048,2816]{1,0:T(8,128)(2,1)} %gate_w_ref.6, bf16[2048,2816]{1,0:T(8,128)(2,1)} %up_w_ref.6, bf16[15,144,2048]{2,1,0:T(8,128)(2,1)} %gather_rows.2.after_ref.near_ref), custom_call_target="tpu_custom_call" | custom-call | flops 5905580032 | bytes 23068672 | tf_op jit(solution)/shard_map/shared_hidden/pallas_call | solution.py:169
  80.6 19.0 %shared_hidden.4.after_ref.hidden_ref = bf16[512,2816]{1,0:T(8,128)(2,1)} custom-call(bf16[512,2048]{1,0:T(8,128)(2,1)} %row_ref.1, bf16[2048,2816]{1,0:T(8,128)(2,1)} %gate_w_ref.6, bf16[2048,2816]{1,0:T(8,128)(2,1)} %up_w_ref.6, bf16[256,2816]{1,0:T(8,128)(2,1)} %shared_hidden.3.after_ref.hidden_ref), custom_call_target="tpu_custom_call" | custom-call | flops 11811160064 | bytes 23068672 | tf_op jit(solution)/shard_map/shared_hidden/pallas_call | solution.py:169
  99.6 1.0 copy-done
  100.6 15.3 %shared_hidden.5.hidden_ref = bf16[256,2816]{1,0:T(8,128)(2,1)} custom-call(bf16[256,2048]{1,0:T(8,128)(2,1)} %copy-done, bf16[2048,2816]{1,0:T(8,128)(2,1)} %gate_w_ref.6, bf16[2048,2816]{1,0:T(8,128)(2,1)} %up_w_ref.6, bf16[512,2816]{1,0:T(8,128)(2,1)} %shared_hidden.4.after_ref.hidden_ref), custom_call_target="tpu_custom_call" | custom-call | flops 5905580032 | bytes 23068672 | tf_op jit(solution)/shard_map/shared_hidden/pallas_call | solution.py:169
  115.8 8.0 %shared_down.3.after_ref = f32[256,2048]{1,0:T(8,128)} custom-call(bf16[256,2816]{1,0:T(8,128)(2,1)} %shared_hidden.5.hidden_ref, bf16[2816,2048]{1,0:T(8,128)(2,1)} %weight_ref.6, bf16[512,2048]{1,0:T(8,128)(2,1)} %collective-permute-done.4.after_ref.first_ref), custom_call_target="tpu_custom_call" | custom-call | flops 2952790016 | bytes 13631488 | tf_op jit(solution)/shard_map/shared_down/pallas_call | solution.py:189
  123.9 1.7 collective-permute-start.9
  125.6 8.1 %shared_down.5 = f32[256,2048]{1,0:T(8,128)} custom-call(bf16[256,2816]{1,0:T(8,128)(2,1)} %shared_hidden.3.after_ref.hidden_ref, bf16[2816,2048]{1,0:T(8,128)(2,1)} %weight_ref.6, bf16[256,2816]{1,0:T(8,128)(2,1)} %shared_hidden.3.after_ref.hidden_ref), custom_call_target="tpu_custom_call" | custom-call | flops 2952790016 | bytes 13631488 | tf_op jit(solution)/shard_map/shared_down/pallas_call | solution.py:189
  133.7 0.3 collective-permute-start.8
  134.0 12.1 %gather_rows.3.far_ref = bf16[15,144,2048]{2,1,0:T(8,128)(2,1)} custom-call(s32[15]{0:T(128)} %compare_convert_fusion.few_ref, s32[2,4,512]{2,1,0:T(4,128)} %get-tuple-element.9.code_ref, bf16[512,2048]{1,0:T(8,128)(2,1)} %collective-permute-done.4.after_ref.first_ref, bf16[512,2048]{1,0:T(8,128)(2,1)} %collective-permute-done.5.second_ref, ...), custom_call_target="tpu_custom_call" | custom-call | flops 4529848320 | bytes 8847360 | tf_op jit(solution)/shard_map/gather_rows/pallas_call | solution.py:58
  146.2 66.4 %expert_hidden.1.after_ref.hidden_hbm = bf16[15,288,1408]{2,1,0:T(8,128)(2,1)} custom-call(s32[15]{0:T(128)} %compare_convert_fusion.few_ref, bf16[15,144,2048]{2,1,0:T(8,128)(2,1)} %gather_rows.2.after_ref.near_ref, bf16[15,144,2048]{2,1,0:T(8,128)(2,1)} %gather_rows.3.far_ref, bf16[15,2048,1408]{2,1,0:T(8,128)(2,1)} %gate_w_ref.7, ...), custom_call_target="tpu_custom_call" | custom-call | flops 49828331520 | bytes 173015040 | tf_op jit(solution)/shard_map/expert_hidden/pallas_call | solution.py:142
  212.6 11.0 %shared_down.4 = f32[512,2048]{1,0:T(8,128)} custom-call(bf16[512,2816]{1,0:T(8,128)(2,1)} %shared_hidden.4.after_ref.hidden_ref, bf16[2816,2048]{1,0:T(8,128)(2,1)} %weight_ref.6, bf16[15,288,1408]{2,1,0:T(8,128)(2,1)} %expert_hidden.1.after_ref.hidden_hbm), custom_call_target="tpu_custom_call" | custom-call | flops 5905580032 | bytes 15728640 | tf_op jit(solution)/shard_map/shared_down/pallas_call | solution.py:189
  223.6 7.6 %maximum_add_fusion.base_ref = f32[512,2048]{1,0:T(8,128)} fusion(f32[256,2048]{1,0:T(8,128)} %collective-permute-done.9, f32[256,2048]{1,0:T(8,128)} %collective-permute-done.8, f32[512,2048]{1,0:T(8,128)} %shared_down.4, bf16[512,2048]{1,0:T(8,128)(2,1)} %row_ref.1), kind=kLoop, calls=%fused_computation | loop fusion | flops 4194304 | bytes 14680064 | tf_op jit(solution)/shard_map/add | solution.py:379
  231.2 123.0 %finish.1 = bf16[512,2048]{1,0:T(8,128)(2,1)} custom-call(bf16[15,288,1408]{2,1,0:T(8,128)(2,1)} %expert_hidden.1.after_ref.hidden_hbm, bf16[5,2048,768]{2,1,0:T(8,128)(2,1)} %combine_matrix.1.after_ref.combine_hbm, f32[512,2048]{1,0:T(8,128)} %maximum_add_fusion.base_ref, bf16[15,1408,2048]{2,1,0:T(8,128)(2,1)} %weight_ref.7), custom_call_target="tpu_custom_call" | custom-call | flops 57126420480 | bytes 86507520 | tf_op jit(solution)/shard_map/finish/pallas_call | solution.py:301
  354.3 3.2 copy.14
  (16 shorter events, 0.2 us)
Async XLA Ops:
  1.4 8.6 %collective-permute-start = (f32[8,512]{1,0:T(8,128)S(1)}, f32[8,512]{1,0:T(8,128)S(1)}, u32[]{:S(2)}, u32[]{:S(2)}) collective-permute-start(f32[8,512]{1,0:T(8,128)S(1)} %get-tuple-element.12), channel_id=1, source_target_pairs={{0,1},{1,0},{2,3},{3,2},{4,5},{5,4},{6,7},{7,6}} | collective-permute-start | bytes 49160 | tf_op jit(solution)/shard_map/ppermute | solution.py:355
  2.3 9.3 %collective-permute-start.1 = (f32[8,512]{1,0:T(8,128)S(1)}, f32[8,512]{1,0:T(8,128)S(1)}, u32[]{:S(2)}, u32[]{:S(2)}) collective-permute-start(f32[8,512]{1,0:T(8,128)S(1)} %get-tuple-element.12), channel_id=1, source_target_pairs={{0,2},{1,3},{2,0},{3,1},{4,6},{5,7},{6,4},{7,5}} | collective-permute-start | bytes 49160 | tf_op jit(solution)/shard_map/ppermute | solution.py:355
  4.8 7.3 %collective-permute-start.2 = (f32[8,512]{1,0:T(8,128)S(1)}, f32[8,512]{1,0:T(8,128)S(1)}, u32[]{:S(2)}, u32[]{:S(2)}) collective-permute-start(f32[8,512]{1,0:T(8,128)S(1)} %get-tuple-element.12), channel_id=1, source_target_pairs={{0,3},{1,2},{2,1},{3,0},{4,7},{5,6},{6,5},{7,4}} | collective-permute-start | bytes 49160 | tf_op jit(solution)/shard_map/ppermute | solution.py:355
  4.9 48.2 %collective-permute-start.3 = (bf16[512,2048]{1,0:T(8,128)(2,1)}, bf16[512,2048]{1,0:T(8,128)(2,1)}, u32[]{:S(2)}, u32[]{:S(2)}) collective-permute-start(bf16[512,2048]{1,0:T(8,128)(2,1)} %row_ref.1), channel_id=1, source_target_pairs={{0,1},{1,0},{2,3},{3,2},{4,5},{5,4},{6,7},{7,6}} | collective-permute-start | bytes 6291464 | tf_op jit(solution)/shard_map/ppermute | solution.py:347
  5.0 48.1 %collective-permute-start.4 = (bf16[512,2048]{1,0:T(8,128)(2,1)}, bf16[512,2048]{1,0:T(8,128)(2,1)}, u32[]{:S(2)}, u32[]{:S(2)}) collective-permute-start(bf16[512,2048]{1,0:T(8,128)(2,1)} %row_ref.1), channel_id=1, source_target_pairs={{0,2},{1,3},{2,0},{3,1},{4,6},{5,7},{6,4},{7,5}} | collective-permute-start | bytes 6291464 | tf_op jit(solution)/shard_map/ppermute | solution.py:350
  10.1 55.2 %collective-permute-start.7 = (bf16[256,2048]{1,0:T(8,128)(2,1)}, bf16[256,2048]{1,0:T(8,128)(2,1)}, u32[]{:S(2)}, u32[]{:S(2)}) collective-permute-start(bf16[256,2048]{1,0:T(8,128)(2,1)} %get-tuple-element.7), channel_id=1, source_target_pairs={{0,4},{4,0},{1,5},{5,1},{2,6},{6,2},{3,7},{7,3}} | collective-permute-start | bytes 3145736 | tf_op jit(solution)/shard_map/ppermute | solution.py:349
  11.6 88.0 %collective-permute-start.6 = (bf16[256,2048]{1,0:T(8,128)(2,1)}, bf16[256,2048]{1,0:T(8,128)(2,1)S(1)}, u32[]{:S(2)}, u32[]{:S(2)}) collective-permute-start(bf16[256,2048]{1,0:T(8,128)(2,1)} %get-tuple-element.8), channel_id=1, source_target_pairs={{0,4},{4,0},{1,5},{5,1},{2,6},{6,2},{3,7},{7,3}} | collective-permute-start | bytes 3145736 | tf_op jit(solution)/shard_map/ppermute | solution.py:349
  53.1 80.9 %collective-permute-start.5 = (bf16[512,2048]{1,0:T(8,128)(2,1)}, bf16[512,2048]{1,0:T(8,128)(2,1)}, u32[]{:S(2)}, u32[]{:S(2)}) collective-permute-start(bf16[512,2048]{1,0:T(8,128)(2,1)} %collective-permute-done.4.after_ref.first_ref), channel_id=1, source_target_pairs={{0,1},{1,0},{2,3},{3,2},{4,5},{5,4},{6,7},{7,6}} | collective-permute-start | bytes 6291464 | tf_op jit(solution)/shard_map/ppermute | solution.py:351
  99.6 1.0 copy-start
  123.9 99.7 %collective-permute-start.9 = (f32[256,2048]{1,0:T(8,128)}, f32[256,2048]{1,0:T(8,128)}, u32[]{:S(2)}, u32[]{:S(2)}) collective-permute-start(f32[256,2048]{1,0:T(8,128)} %shared_down.3.after_ref), channel_id=1, source_target_pairs={{0,4},{4,0},{1,5},{5,1},{2,6},{6,2},{3,7},{7,3}} | collective-permute-start | bytes 6291464 | tf_op jit(solution)/shard_map/ppermute | solution.py:375
  133.7 89.9 %collective-permute-start.8 = (f32[256,2048]{1,0:T(8,128)}, f32[256,2048]{1,0:T(8,128)}, u32[]{:S(2)}, u32[]{:S(2)}) collective-permute-start(f32[256,2048]{1,0:T(8,128)} %shared_down.5), channel_id=1, source_target_pairs={{0,4},{4,0},{1,5},{5,1},{2,6},{6,2},{3,7},{7,3}} | collective-permute-start | bytes 6291464 | tf_op jit(solution)/shard_map/ppermute | solution.py:371

commit v3 on v0

v3 whole, which is shorter than its diff:
```python
import functools

import jax
import jax.numpy as jnp
from jax import lax
from jax.experimental import pallas as pl
from jax.experimental.pallas import tpu as pltpu
from jax.sharding import PartitionSpec as P

COL_BLOCKS = 8
GROUP = 3
FEW_SLOTS = 48
SPAN = 512
CHUNK = 128
MESH = pl.DeviceIdType.MESH
GATE_MAX = 3.3895313892515355e38


def capacity_rows(tok_dev, top_k, n_exp):
    return 8 * max(1, (2 * tok_dev * top_k + 8 * n_exp - 1) // (8 * n_exp))


ANY = pl.BlockSpec(memory_space=pl.ANY)


def params():
    return pltpu.CompilerParams(vmem_limit_bytes=62 * 2**20)


def cost(flops, nbytes):
    return pl.CostEstimate(flops=flops, bytes_accessed=nbytes, transcendentals=0)


def peers():
    dp, tp, me = lax.axis_index("dp"), lax.axis_index("tp"), lax.axis_index("ep")
    core = me + 1 - 2 * lax.rem(me, 2)
    chip = lax.rem(me + 2, 4)
    both = lax.rem(core + 2, 4)
    return (dp, tp, core), (dp, tp, chip), (dp, tp, both), (dp, 1 - tp, me)


def greet(devices):
    barrier = pltpu.get_barrier_semaphore()
    for device in devices:
        pl.semaphore_signal(barrier, inc=1, device_id=device, device_id_type=MESH)
    pl.semaphore_wait(barrier, len(devices))


def combine_chunk(cap, local_exp, meta, out_ref):
    top_k = meta.shape[0] // 2
    cols = meta.T
    base = (lax.broadcasted_iota(jnp.int32, (CHUNK, local_exp), 1) + lax.axis_index("ep") * local_exp) * cap
    base = base.astype(jnp.float32)
    slot_of = jnp.full(base.shape, -1024.0, jnp.float32)
    gate = jnp.zeros(base.shape, jnp.float32)
    for j in range(top_k):
        offset = cols[:, j : j + 1] - base
        inside = (offset >= 0.0) & (offset < float(cap))
        slot_of = jnp.where(inside, offset, slot_of)
        gate = jnp.where(inside, cols[:, top_k + j : top_k + j + 1], gate)
    slot_of = slot_of.astype(jnp.int32)
    high = jnp.minimum(gate, GATE_MAX).astype(jnp.bfloat16).astype(jnp.float32)
    rest = gate - high
    middle = rest.astype(jnp.bfloat16).astype(jnp.float32)
    pieces = (high, middle, rest - middle)
    lane = lax.broadcasted_iota(jnp.int32, (CHUNK, 256), 1)
    depth = out_ref.shape[1] // 3
    for g in range(depth // 256):
        values = [jnp.zeros(lane.shape, jnp.float32)] * 3
        for k in range(GROUP):
            e = g * GROUP + k
            hit = lane == slot_of[:, e : e + 1] + k * cap
            values = [jnp.where(hit, piece[:, e : e + 1], value) for piece, value in zip(pieces, values)]
        for i, value in enumerate(values):
            out_ref[:, i * depth + g * 256 : i * depth + (g + 1) * 256] = value.astype(jnp.bfloat16)


def start_kernel(
    cap, local_exp, meta_ref, tok_hbm, w_gate_hbm, w_up_hbm, w_down_hbm,
    metas, tok_core, tok_chip, tok_both, combine_hbm, base_hbm, peer_hidden,
    own, other, own_hidden, load_sem, send_sem, recv_sem,
):
    core, chip, both, tp = peers()
    tok_dev, d_model = own.shape
    width = peer_hidden.shape[1]

    def remote(src, dst, device, i):
        return pltpu.make_async_remote_copy(
            src_ref=src, dst_ref=dst, send_sem=send_sem.at[i], recv_sem=recv_sem.at[i], device_id=device, device_id_type=MESH
        )

    load = pltpu.make_async_copy(tok_hbm, own, load_sem)
    load.start()
    greet((core, chip, both, tp))
    meta_copies = [remote(meta_ref, metas.at[i + 1], device, i) for i, device in enumerate((core, chip, both))]
    for copy in meta_copies:
        copy.start()
    to_chip = remote(tok_hbm, tok_chip, chip, 3)
    to_tp = remote(tok_hbm, other, tp, 4)
    to_core = remote(tok_hbm, tok_core, core, 5)
    onward = remote(tok_chip, tok_both, core, 6)
    for copy in (to_chip, to_tp, to_core):
        copy.start()
    metas[0] = meta_ref[...]
    for copy in meta_copies:
        copy.wait()

    per_source = tok_dev // CHUNK

    def write_combine(index, out_ref):
        i = index.index[0]
        here = pl.ds(pl.multiple_of(lax.rem(i, per_source) * CHUNK, CHUNK), CHUNK)
        combine_chunk(cap, local_exp, metas[i // per_source, :, here], out_ref)

    pltpu.emit_pipeline(
        write_combine,
        grid=(4 * per_source,),
        out_specs=[pl.BlockSpec((CHUNK, combine_hbm.shape[1]), lambda i: (i, 0))],
        _explicit_indices=True,
    )(combine_hbm)

    def hidden_of(rows, result):
        def body(index, gate_w_ref, up_w_ref):
            gate_pre = jnp.dot(rows[...], gate_w_ref[...], preferred_element_type=jnp.float32)
            up_pre = jnp.dot(rows[...], up_w_ref[...], preferred_element_type=jnp.float32)
            here = pl.ds(pl.multiple_of(index.index[0] * 256, 256), 256)
            result[:, here] = (jax.nn.silu(gate_pre) * up_pre).astype(jnp.bfloat16)

        spec = pl.BlockSpec((d_model, 256), lambda i: (0, i))
        pltpu.emit_pipeline(body, grid=(width // 256,), in_specs=[spec, spec], _explicit_indices=True)(w_gate_hbm, w_up_hbm)

    load.wait()
    hidden_of(own, own_hidden)

    def down(index, weight_ref, out_ref):
        here = pl.ds(pl.multiple_of(index.index[0] * 512, 512), 512)
        result = jnp.dot(own_hidden[...], weight_ref[...], preferred_element_type=jnp.float32)
        out_ref[...] = own[:, here].astype(jnp.float32) + result

    pltpu.emit_pipeline(
        down,
        grid=(d_model // 512,),
        in_specs=[pl.BlockSpec((width, 512), lambda i: (0, i))],
        out_specs=[pl.BlockSpec((tok_dev, 512), lambda i: (0, i))],
        _explicit_indices=True,
    )(w_down_hbm, base_hbm)

    to_chip.wait()
    onward.start()
    to_tp.wait()
    hidden_of(other, peer_hidden)
    to_core.wait()
    onward.wait()


def start(meta, tokens, w_gate, w_up, w_down, cap, local_exp):
    tok_dev, d_model = tokens.shape
    width = w_gate.shape[1]
    vmem = pl.BlockSpec(memory_space=pltpu.VMEM)
    tok_shape = jax.ShapeDtypeStruct((tok_dev, d_model), jnp.bfloat16)
    return pl.pallas_call(
        functools.partial(start_kernel, cap, local_exp),
        out_shape=[
            jax.ShapeDtypeStruct((4,) + meta.shape, jnp.float32),
            tok_shape, tok_shape, tok_shape,
            jax.ShapeDtypeStruct((4 * tok_dev, local_exp // GROUP * 768), jnp.bfloat16),
            jax.ShapeDtypeStruct((tok_dev, d_model), jnp.float32),
            jax.ShapeDtypeStruct((tok_dev, width), jnp.bfloat16),
        ],
        in_specs=[vmem, ANY, ANY, ANY, ANY],
        out_specs=[vmem, ANY, ANY, ANY, ANY, ANY, vmem],
        scratch_shapes=[
            pltpu.VMEM((tok_dev, d_model), jnp.bfloat16),
            pltpu.VMEM((tok_dev, d_model), jnp.bfloat16),
            pltpu.VMEM((tok_dev, width), jnp.bfloat16),
            pltpu.SemaphoreType.DMA,
            pltpu.SemaphoreType.DMA((7,)),
            pltpu.SemaphoreType.DMA((7,)),
        ],
        compiler_params=pltpu.CompilerParams(collective_id=1, has_side_effects=True, vmem_limit_bytes=67043328),
        cost_estimate=cost(10 * tok_dev * d_model * width, 10 * d_model * width),
        name="start",
    )(meta, tokens, w_gate, w_up, w_down)


def swiglu_cols(rows, gate_w_ref, up_w_ref, cols):
    gate_pre = jnp.dot(rows, gate_w_ref[0, :, cols], preferred_element_type=jnp.float32)
    up_pre = jnp.dot(rows, up_w_ref[0, :, cols], preferred_element_type=jnp.float32)
    return jax.nn.silu(gate_pre) * up_pre


def hidden_kernel(cap, meta_ref, *refs):
    tok_refs, (gate_w_ref, up_w_ref, out_ref, row_ref) = refs[:4], refs[4:]
    e = pl.program_id(0)
    top_k = meta_ref.shape[1] // 2
    first = (lax.axis_index("ep") * pl.num_programs(0) + e) * cap
    slots = [meta_ref[source, :top_k].astype(jnp.int32) - first for source in range(4)]
    last = jnp.max(jnp.stack([jnp.where(slot < cap, slot, -1) for slot in slots]))
    width = out_ref.shape[2]
    spans = [slice(start, min(start + SPAN, width)) for start in range(0, width, SPAN)]

    def pick_rows(n_slots):
        picked = []
        for source, tok_ref in enumerate(tok_refs):
            slot = slots[source]
            row = lax.broadcasted_iota(jnp.int32, (n_slots, slot.shape[1]), 0)
            hit = row == slot[0:1, :]
            for j in range(1, top_k):
                hit = hit | (row == slot[j : j + 1, :])
            pick = jnp.where(hit, 1.0, 0.0).astype(jnp.bfloat16)
            picked.append(jnp.dot(pick, tok_ref[...], preferred_element_type=jnp.float32))
        row_ref[: 4 * n_slots] = jnp.concatenate(picked, axis=0).astype(jnp.bfloat16)

    @pl.when(last < FEW_SLOTS)
    def _():
        pick_rows(FEW_SLOTS)
        for cols in spans:
            hidden = swiglu_cols(row_ref[: 4 * FEW_SLOTS], gate_w_ref, up_w_ref, cols)
            gap = jnp.zeros((cap - FEW_SLOTS, hidden.shape[1]), jnp.float32)
            pieces = []
            for source in range(4):
                pieces += [hidden[source * FEW_SLOTS : (source + 1) * FEW_SLOTS], gap]
            out_ref[0, :, cols] = jnp.concatenate(pieces, axis=0).astype(jnp.bfloat16)

    @pl.when(last >= FEW_SLOTS)
    def _():
        pick_rows(cap)
        for cols in spans:
            out_ref[0, :, cols] = swiglu_cols(row_ref[...], gate_w_ref, up_w_ref, cols).astype(jnp.bfloat16)


def expert_hidden(metas, sources, w_gate, w_up, cap):
    local_exp, d_model, width = w_gate.shape
    tok_dev = sources[0].shape[0]
    rows = 4 * cap
    tok_spec = pl.BlockSpec((tok_dev, d_model), lambda e: (0, 0))
    weight_spec = pl.BlockSpec((1, d_model, width), lambda e: (e, 0, 0))
    return pl.pallas_call(
        functools.partial(hidden_kernel, cap),
        grid=(local_exp,),
        in_specs=[pl.BlockSpec(metas.shape, lambda e: (0, 0, 0))] + [tok_spec] * 4 + [weight_spec, weight_spec],
        out_specs=pl.BlockSpec((1, rows, width), lambda e: (e, 0, 0)),
        scratch_shapes=[pltpu.VMEM((rows, d_model), jnp.bfloat16)],
        out_shape=jax.ShapeDtypeStruct((local_exp, rows, width), jnp.bfloat16),
        compiler_params=params(),
        cost_estimate=cost(local_exp * rows * d_model * width * 4, local_exp * d_model * width * 4),
        name="expert_hidden",
    )(metas, *sources, w_gate, w_up)


def finish_kernel(
    cap, n_blocks, combine_hbm, peer_hbm, base_ref, hidden_ref, weight_ref, shared_ref, out_hbm,
    combine, peer, rows, total, for_tp, from_core, from_chip, from_tp, out,
    load_sem, store_sem, core_send, core_recv, chip_send, chip_recv, tp_send, tp_recv,
):
    block, group = pl.program_id(0), pl.program_id(1)
    tok_dev, cols = base_ref.shape
    core_peer, chip_peer, _, tp_peer = peers()
    load_combine = pltpu.make_async_copy(combine_hbm, combine, load_sem.at[0])
    load_peer = pltpu.make_async_copy(peer_hbm, peer, load_sem.at[1])

    def core_copy(n):
        return pltpu.make_async_remote_copy(
            src_ref=total.at[pl.ds(2, 2)], dst_ref=from_core.at[n],
            send_sem=core_send.at[n], recv_sem=core_recv.at[n], device_id=core_peer, device_id_type=MESH,
        )

    def chip_copy(n):
        return pltpu.make_async_remote_copy(
            src_ref=from_core.at[n, 1], dst_ref=from_chip.at[n],
            send_sem=chip_send.at[n], recv_sem=chip_recv.at[n], device_id=chip_peer, device_id_type=MESH,
        )

    def tp_copy(n):
        return pltpu.make_async_remote_copy(
            src_ref=for_tp.at[n], dst_ref=from_tp.at[n],
            send_sem=tp_send.at[n], recv_sem=tp_recv.at[n], device_id=tp_peer, device_id_type=MESH,
        )

    def store(n):
        here = pl.ds(pl.multiple_of(n * cols, cols), cols)
        return pltpu.make_async_copy(out.at[n], out_hbm.at[:, here], store_sem.at[n])

    def finalize(n):
        chip_copy(n).wait()
        tp_copy(n).wait()
        out[n] = (from_core[n, 0] + from_chip[n] + from_tp[n]).astype(jnp.bfloat16)
        store(n).start()

    def gated(source):
        r = rows[lax.rem(block + 1, 2), source]
        stacked = jnp.concatenate([r, r, r], axis=0)
        gates = combine[source * tok_dev : (source + 1) * tok_dev, :]
        return jnp.dot(gates, stacked, preferred_element_type=jnp.float32)

    @pl.when((block == 0) & (group == 0))
    def _():
        load_peer.start()
        load_combine.start()
        greet((core_peer, chip_peer, tp_peer))

    @pl.when(block < n_blocks)
    def _():
        results = []
        for k in range(GROUP):
            results.append(jnp.dot(hidden_ref[k], weight_ref[k], preferred_element_type=jnp.float32))
        gap = jnp.zeros((256 - GROUP * cap, cols), jnp.float32)
        place = pl.ds(pl.multiple_of(group * 256, 256), 256)
        for source in range(4):
            part = jnp.concatenate([r[source * cap : (source + 1) * cap] for r in results] + [gap], axis=0)
            rows[lax.rem(block, 2), source, place, :] = part.astype(jnp.bfloat16)

    @pl.when((block == 0) & (group == 2))
    def _():
        load_peer.wait()

    @pl.when((block == 1) & (group == 0))
    def _():
        load_combine.wait()

    @pl.when((block >= 1) & (group == 0))
    def _():
        total[2] = gated(1)

    @pl.when((block >= 1) & (group == 1))
    def _():
        total[3] = gated(3)
        core_copy(block - 1).start()

    @pl.when((block >= 1) & (group == 2))
    def _():
        total[1] = gated(2)

    @pl.when((block >= 1) & (group == 3))
    def _():
        core_copy(block - 1).wait()
        from_core[block - 1, 1] += total[1]
        chip_copy(block - 1).start()
        total[0] = gated(0) + base_ref[...]
        from_core[block - 1, 0] += total[0]

    @pl.when((block < n_blocks) & (group == 4))
    def _():
        for_tp[block] = jnp.dot(peer[...], shared_ref[...], preferred_element_type=jnp.float32)
        tp_copy(block).start()

    @pl.when((block >= 4) & (group == 4))
    def _():
        finalize(block - 4)

    @pl.when((block == n_blocks) & (group == 4))
    def _():
        for n in range(n_blocks - 3, n_blocks):
            finalize(n)
        for n in range(n_blocks):
            store(n).wait()


def finish(hidden, combine, base, peer_hidden, w_down, shared_down_w):
    local_exp, n_rows, width = hidden.shape
    n_groups = local_exp // GROUP
    tok_dev, d_model = base.shape
    shared_width = peer_hidden.shape[1]
    cols = d_model // COL_BLOCKS
    last_block, last_group = COL_BLOCKS - 1, n_groups - 1
    sems = pltpu.SemaphoreType.DMA((COL_BLOCKS,))
    blocks = (COL_BLOCKS, tok_dev, cols)

    def group_of(n, g):
        return jnp.where(n > last_block, last_group, g)

    return pl.pallas_call(
        functools.partial(finish_kernel, n_rows // 4, COL_BLOCKS),
        grid=(COL_BLOCKS + 1, n_groups),
        out_shape=jax.ShapeDtypeStruct((tok_dev, d_model), jnp.bfloat16),
        in_specs=[
            ANY,
            ANY,
            pl.BlockSpec((tok_dev, cols), lambda n, g: (0, jnp.maximum(n - 1, 0))),
            pl.BlockSpec((GROUP, n_rows, width), lambda n, g: (group_of(n, g), 0, 0)),
            pl.BlockSpec((GROUP, width, cols), lambda n, g: (group_of(n, g), 0, jnp.minimum(n, last_block))),
            pl.BlockSpec((shared_width, cols), lambda n, g: (0, jnp.minimum(n, last_block))),
        ],
        out_specs=ANY,
        scratch_shapes=[
            pltpu.VMEM(combine.shape, jnp.bfloat16),
            pltpu.VMEM(peer_hidden.shape, jnp.bfloat16),
            pltpu.VMEM((2, 4, n_groups * 256, cols), jnp.bfloat16),
            pltpu.VMEM((4, tok_dev, cols), jnp.float32),
            pltpu.VMEM(blocks, jnp.float32),
            pltpu.VMEM((COL_BLOCKS, 2, tok_dev, cols), jnp.float32),
            pltpu.VMEM(blocks, jnp.float32),
            pltpu.VMEM(blocks, jnp.float32),
            pltpu.VMEM(blocks, jnp.bfloat16),
            pltpu.SemaphoreType.DMA((2,)),
            sems, sems, sems, sems, sems, sems, sems,
        ],
        compiler_params=pltpu.CompilerParams(
            collective_id=0, has_side_effects=True, vmem_limit_bytes=67043328, dimension_semantics=("arbitrary", "arbitrary")
        ),
        cost_estimate=cost(2 * d_model * local_exp * (n_rows * width + 4 * tok_dev * 256), 2 * local_exp * width * d_model),
        name="finish",
    )(combine, peer_hidden, base, hidden, w_down, shared_down_w)


def solution(mesh):
    ep_size = mesh.shape["ep"]
    row_spec = P(("dp", "ep", "tp"), None)
    expert_spec = P("ep", None, None)

    def local_layer(tokens, expert_ids, gates, slots, shared_w1, shared_w3, shared_w2, expert_w1, expert_w3, expert_w2):
        tok_dev, d_model = tokens.shape
        top_k = expert_ids.shape[1]
        local_exp = expert_w1.shape[0]
        cap = capacity_rows(tok_dev, top_k, local_exp * ep_size)
        code = jnp.where(slots >= 0, expert_ids * cap + slots, -1)
        meta = jnp.concatenate([code.astype(jnp.float32).T, gates.T], axis=0)
        metas, tok_core, tok_chip, tok_both, combine, base, peer_hidden = start(meta, tokens, shared_w1, shared_w3, shared_w2, cap, local_exp)
        hidden = expert_hidden(metas, (tokens, tok_core, tok_chip, tok_both), expert_w1, expert_w3, cap)
        return finish(hidden, combine, base, peer_hidden, expert_w2, shared_w2)

    return jax.shard_map(local_layer, mesh=mesh, in_specs=(row_spec, row_spec, row_spec, row_spec, P(None, "tp"), P(None, "tp"), P("tp", None), expert_spec, expert_spec, expert_spec), out_specs=row_spec, check_vma=False)
```

time: 713 us -> 275 us (0.39)
  waiting for transfers between devices: 330 us -> 0 us
  Pallas kernels: 0 us -> 269 us
  matrix products: 195 us -> 0 us
  local copies, waits for them, and re-layouts: 115 us -> 3.16 us
  other arithmetic: 44 us -> 2.03 us
  starting transfers between devices: 15 us -> 0 us
  between operations: 13.6 us -> 0.02 us
    all_to_all x2 -> x0, waiting for transfers between devices: 270 us -> none  [the longest x1 192 us: local_layer(): lax.all_to_all(expert_out, 'ep', 1, 1, tiled=True).reshape(n_rows, d_model)]
    pallas_call x0 -> x3, Pallas kernels: none -> 269 us  [the longest x1 119 us: finish(): pl.pallas_call(functools.partial(finish_kernel, n_rows // 4, COL_BLOCKS),...]
    dot_general x5 -> x0, matrix products: 195 us -> none  [the longest x1 49.2 us: local_layer(): jnp.einsum('lscd,ldf->lscf', recv_rows, expert_w1, preferred_element_type...]
    gather x3 -> x0, local copies, waits for them, and re-layouts: 73 us -> none  [the longest x2 37.9 us: local_layer(): routed = jnp.take(back_rows, row_code, axis=0, mode='fill', fill_value=0)]
    all_gather x1 -> x0, waiting for transfers between devices: 58.9 us -> none  [local_layer(): group_rows = lax.all_gather(tokens, 'tp', axis=0, tiled=True)]
    reduce_sum x1 -> x0, other arithmetic: 20.6 us -> none  [local_layer(): routed_sum = jnp.sum(gates[:, :, None] * routed.astype(jnp.float32), axis=1)]
    convert_element_type x1 -> x0, local copies, waits for them, and re-layouts: 16.2 us -> none  [local_layer(): jnp.einsum('lscf,lfd->lscd', hidden, expert_w2, preferred_element_type=jn...]
    all_to_all x1 -> x0, local copies, waits for them, and re-layouts: 16.2 us -> none  [local_layer(): lax.all_to_all(expert_out, 'ep', 1, 1, tiled=True).reshape(n_rows, d_model)]
  transfers between devices with their start and end apart: 4 -> 0, of which waited for: 3 -> 0; matrix products, arithmetic and copies ran while one was open for 40% -> 0% of each run, Pallas kernels for 0% -> 0%
where the time goes in v3:
time: 275 us; the launch traced here: 274 us
  Pallas kernels  269 us (98%)
  local copies, waits for them, and re-layouts  3.16 us (1%)
    pallas_call x1, Pallas kernels, finish(): pl.pallas_call(functools.partial(finish_kernel, n_rows // 4, COL_BLOCKS),...  119 us
    pallas_call x1, Pallas kernels, expert_hidden(): pl.pallas_call(functools.partial(hidden_kernel, cap), grid=(local_exp,),...  75.4 us
    pallas_call x1, Pallas kernels, start(): pl.pallas_call(functools.partial(start_kernel, cap, local_exp), out_shape...  73.7 us

profile of v3, /device:TPU:0, one launch (start us, length us, event | category | flops | bytes accessed | tf_op | source)
XLA Modules:
  0.0 273.7 jit_solution(2613251344970050747)
XLA Ops:
  0.0 0.7 convert_bitcast_fusion
  0.7 1.3 pad_maximum_fusion.meta_ref
  2.0 73.7 %start.1 = (f32[4,8,512]{2,1,0:T(8,128)}, bf16[512,2048]{1,0:T(8,128)(2,1)}, bf16[512,2048]{1,0:T(8,128)(2,1)}, bf16[512,2048]{1,0:T(8,128)(2,1)}, bf16[2048,384...) custom-call(f32[8,512]{1,0:T(8,128)} %pad_maximum_fusion.meta_ref, bf16[512,2048]{1,0:T(8,128)(2,1)} %refs_0_.1, ...), custom_call_target="tpu_custom_call" | custom-call | flops 29527900160 | bytes 57671680 | tf_op jit(solution)/shard_map/start/pallas_call | solution.py:161
  75.7 75.4 %expert_hidden.1.hidden_ref = bf16[15,288,1408]{2,1,0:T(8,128)(2,1)} custom-call(f32[4,8,512]{2,1,0:T(8,128)} %get-tuple-element.15.meta_ref, bf16[512,2048]{1,0:T(8,128)(2,1)} %refs_0_.1, bf16[512,2048]{1,0:T(8,128)(2,1)} %get-tuple-element.16.refs_1_, bf16[512,2048]{1,0:T(8,128)(2,1)} %get-tuple-element.17.refs_2_, ...), custom_call_target="tpu_custom_call" | custom-call | flops 49828331520 | bytes 173015040 | tf_op jit(solution)/shard_map/expert_hidden/pallas_call | solution.py:238
  151.2 119.4 %finish.1 = bf16[512,2048]{1,0:T(8,128)(2,1)} custom-call(bf16[2048,3840]{1,0:T(8,128)(2,1)} %get-tuple-element.12.combine_hbm, bf16[512,2816]{1,0:T(8,128)(2,1)} %get-tuple-element.13.peer_hbm, f32[512,2048]{1,0:T(8,128)} %get-tuple-element.14.base_ref, bf16[15,288,1408]{2,1,0:T(8,128)(2,1)} %expert_hidden.1.hidden_ref, bf16[15,1408,2048]{2,1,0:T(8,128)(2,1)} %weight_ref.1, ...), custom_call_target="tpu_custom_call" | custom-call | flops 57126420480 | bytes 86507520 | tf_op jit(solution)/shard_map/finish/pallas_call | solution.py:372
  270.6 3.2 %copy.12 = bf16[512,2048]{1,0:T(8,128)(2,1)} copy(bf16[512,2048]{1,0:T(8,128)(2,1)} %finish.1) | data formatting | bytes 4194304

commit v4 on v3

v4 whole, which is shorter than its diff:
```python
import functools

import jax
import jax.numpy as jnp
from jax import lax
from jax.experimental import pallas as pl
from jax.experimental.pallas import tpu as pltpu
from jax.sharding import PartitionSpec as P
import numpy as np

COL_BLOCKS = 8
GROUP = 5
BATCH = 4
FEW_SLOTS = 48
SPAN = 512
CHUNK = 128
MESH = pl.DeviceIdType.MESH
GATE_MAX = 3.3895313892515355e38


def capacity_rows(tok_dev, top_k, n_exp):
    return 8 * max(1, (2 * tok_dev * top_k + 8 * n_exp - 1) // (8 * n_exp))


ANY = pl.BlockSpec(memory_space=pl.ANY)


def params():
    return pltpu.CompilerParams(vmem_limit_bytes=62 * 2**20)


def cost(flops, nbytes):
    return pl.CostEstimate(flops=flops, bytes_accessed=nbytes, transcendentals=0)


def peers():
    dp, tp, me = lax.axis_index("dp"), lax.axis_index("tp"), lax.axis_index("ep")
    core = me + 1 - 2 * lax.rem(me, 2)
    chip = lax.rem(me + 2, 4)
    both = lax.rem(core + 2, 4)
    return (dp, tp, core), (dp, tp, chip), (dp, tp, both), (dp, 1 - tp, me)


def greet(devices):
    barrier = pltpu.get_barrier_semaphore()
    for device in devices:
        pl.semaphore_signal(barrier, inc=1, device_id=device, device_id_type=MESH)
    pl.semaphore_wait(barrier, len(devices))


def lane_tables(cap, local_exp):
    span = 128 * ((GROUP * cap + 127) // 128)
    lane = np.arange(local_exp // GROUP * span)
    place = lane % span
    expert = np.where(place < GROUP * cap, lane // span * GROUP + place // cap, -1)
    owner = (np.arange(128)[:, None] == expert[None, :]).astype(np.float32)
    slot = np.where(expert >= 0, place % cap, -1).astype(np.float32)
    return span, jnp.asarray(owner, jnp.bfloat16), jnp.asarray(np.tile(slot, (8, 1)))


def combine_chunk(cap, local_exp, meta, owner_ref, slot_ref, out_ref):
    top_k = meta.shape[0] // 2
    cols = meta.T
    lane = lax.broadcasted_iota(jnp.int32, (CHUNK, 128), 1)
    base = ((lane + lax.axis_index("ep") * local_exp) * cap).astype(jnp.float32)
    slot_of = jnp.full(base.shape, -1024.0, jnp.float32)
    gate = jnp.zeros(base.shape, jnp.float32)
    for j in range(top_k):
        offset = cols[:, j : j + 1] - base
        inside = (offset >= 0.0) & (offset < float(cap)) & (lane < local_exp)
        slot_of = jnp.where(inside, offset, slot_of)
        gate = jnp.where(inside, cols[:, top_k + j : top_k + j + 1], gate)
    high = jnp.minimum(gate, GATE_MAX).astype(jnp.bfloat16).astype(jnp.float32)
    rest = gate - high
    middle = rest.astype(jnp.bfloat16).astype(jnp.float32)
    table = jnp.concatenate([slot_of, high, middle, rest - middle], axis=0).astype(jnp.bfloat16)
    spread = jnp.dot(table, owner_ref[...], preferred_element_type=jnp.float32)
    hit = spread[:CHUNK] == slot_ref[0:1, :]
    depth = spread.shape[1]
    for i in range(3):
        out_ref[:, i * depth : (i + 1) * depth] = jnp.where(hit, spread[(i + 1) * CHUNK : (i + 2) * CHUNK], 0.0).astype(jnp.bfloat16)


def start_kernel(
    cap, local_exp, meta_ref, owner_ref, slot_ref, tok_hbm, w_gate_hbm, w_up_hbm, w_down_hbm,
    metas, tok_core, tok_chip, tok_both, combine_hbm, base_hbm, peer_hidden,
    own, other, own_hidden, load_sem, send_sem, recv_sem,
):
    core, chip, both, tp = peers()
    tok_dev, d_model = own.shape
    width = peer_hidden.shape[1]

    def remote(src, dst, device, i):
        return pltpu.make_async_remote_copy(
            src_ref=src, dst_ref=dst, send_sem=send_sem.at[i], recv_sem=recv_sem.at[i], device_id=device, device_id_type=MESH
        )

    load = pltpu.make_async_copy(tok_hbm, own, load_sem)
    load.start()
    greet((core, chip, both, tp))
    meta_copies = [remote(meta_ref, metas.at[i + 1], device, i) for i, device in enumerate((core, chip, both))]
    for copy in meta_copies:
        copy.start()
    to_chip = remote(tok_hbm, tok_chip, chip, 3)
    to_tp = remote(tok_hbm, other, tp, 4)
    to_core = remote(tok_hbm, tok_core, core, 5)
    onward = remote(tok_chip, tok_both, core, 6)
    for copy in (to_chip, to_tp, to_core):
        copy.start()
    metas[0] = meta_ref[...]
    for copy in meta_copies:
        copy.wait()

    per_source = tok_dev // CHUNK

    def write_combine(index, out_ref):
        i = index.index[0]
        here = pl.ds(pl.multiple_of(lax.rem(i, per_source) * CHUNK, CHUNK), CHUNK)
        combine_chunk(cap, local_exp, metas[i // per_source, :, here], owner_ref, slot_ref, out_ref)

    pltpu.emit_pipeline(
        write_combine,
        grid=(4 * per_source,),
        out_specs=[pl.BlockSpec((CHUNK, combine_hbm.shape[1]), lambda i: (i, 0))],
        _explicit_indices=True,
    )(combine_hbm)

    def hidden_of(rows, result):
        def part(first, step, count):
            def body(index, gate_w_ref, up_w_ref):
                gate_pre = jnp.dot(rows[...], gate_w_ref[...], preferred_element_type=jnp.float32)
                up_pre = jnp.dot(rows[...], up_w_ref[...], preferred_element_type=jnp.float32)
                here = pl.ds(pl.multiple_of((first + index.index[0]) * step, step), step)
                result[:, here] = (jax.nn.silu(gate_pre) * up_pre).astype(jnp.bfloat16)

            spec = pl.BlockSpec((d_model, step), lambda i: (0, first + i))
            pltpu.emit_pipeline(body, grid=(count,), in_specs=[spec, spec], _explicit_indices=True)(w_gate_hbm, w_up_hbm)

        part(0, 256, width // 256)

    load.wait()
    hidden_of(own, own_hidden)

    def down(index, weight_ref, out_ref):
        here = pl.ds(pl.multiple_of(index.index[0] * 512, 512), 512)
        result = jnp.dot(own_hidden[...], weight_ref[...], preferred_element_type=jnp.float32)
        out_ref[...] = own[:, here].astype(jnp.float32) + result

    pltpu.emit_pipeline(
        down,
        grid=(d_model // 512,),
        in_specs=[pl.BlockSpec((width, 512), lambda i: (0, i))],
        out_specs=[pl.BlockSpec((tok_dev, 512), lambda i: (0, i))],
        _explicit_indices=True,
    )(w_down_hbm, base_hbm)

    to_chip.wait()
    onward.start()
    to_tp.wait()
    hidden_of(other, peer_hidden)
    to_core.wait()
    onward.wait()


def start(meta, owner, slot, tokens, w_gate, w_up, w_down, cap, local_exp):
    tok_dev, d_model = tokens.shape
    width = w_gate.shape[1]
    vmem = pl.BlockSpec(memory_space=pltpu.VMEM)
    tok_shape = jax.ShapeDtypeStruct((tok_dev, d_model), jnp.bfloat16)
    return pl.pallas_call(
        functools.partial(start_kernel, cap, local_exp),
        out_shape=[
            jax.ShapeDtypeStruct((4,) + meta.shape, jnp.float32),
            tok_shape, tok_shape, tok_shape,
            jax.ShapeDtypeStruct((4 * tok_dev, 3 * owner.shape[1]), jnp.bfloat16),
            jax.ShapeDtypeStruct((tok_dev, d_model), jnp.float32),
            jax.ShapeDtypeStruct((tok_dev, width), jnp.bfloat16),
        ],
        in_specs=[vmem, vmem, vmem, ANY, ANY, ANY, ANY],
        out_specs=[vmem, ANY, ANY, ANY, ANY, ANY, vmem],
        scratch_shapes=[
            pltpu.VMEM((tok_dev, d_model), jnp.bfloat16),
            pltpu.VMEM((tok_dev, d_model), jnp.bfloat16),
            pltpu.VMEM((tok_dev, width), jnp.bfloat16),
            pltpu.SemaphoreType.DMA,
            pltpu.SemaphoreType.DMA((7,)),
            pltpu.SemaphoreType.DMA((7,)),
        ],
        compiler_params=pltpu.CompilerParams(collective_id=1, has_side_effects=True, vmem_limit_bytes=67043328),
        cost_estimate=cost(10 * tok_dev * d_model * width, 10 * d_model * width),
        name="start",
    )(meta, owner, slot, tokens, w_gate, w_up, w_down)


def hidden_kernel(cap, pitch, meta_ref, *refs):
    tok_hbm, (gate_hbm, up_hbm, out_ref, tok, rows, gate_w, up_w, tok_sem, gate_sem, up_sem) = refs[:4], refs[4:]
    e = pl.program_id(0)
    n_exp = pl.num_programs(0)
    width = out_ref.shape[2]
    d_model = tok.shape[2]
    top_k = meta_ref.shape[1] // 2
    spans = [slice(start, min(start + SPAN, width)) for start in range(0, width, SPAN)]
    now = lax.rem(e, 2)
    first = (lax.axis_index("ep") * n_exp) * cap

    def load_tok(s):
        return pltpu.make_async_copy(tok_hbm[s], tok.at[s], tok_sem.at[s])

    def load(i):
        slot = lax.rem(i, 2)
        return (
            pltpu.make_async_copy(gate_hbm.at[i], gate_w.at[slot], gate_sem.at[slot]),
            pltpu.make_async_copy(up_hbm.at[i], up_w.at[slot], up_sem.at[slot]),
        )

    def pick_rows(batch, source):
        slot = meta_ref[source, :top_k].astype(jnp.int32) - (first + batch * (BATCH * cap))
        row = lax.broadcasted_iota(jnp.int32, (BATCH * cap, slot.shape[1]), 0)
        hit = row == slot[0:1, :]
        for j in range(1, top_k):
            hit = hit | (row == slot[j : j + 1, :])
        pick = jnp.where(hit, 1.0, 0.0).astype(jnp.bfloat16)
        place = pl.ds(pl.multiple_of(source * pitch, pitch), cap)
        for start in range(0, d_model, 512):
            picked = jnp.dot(pick, tok[source, :, start : start + 512], preferred_element_type=jnp.float32)
            for k in range(BATCH):
                part = picked[k * cap : (k + 1) * cap].astype(jnp.bfloat16)
                rows[lax.rem(batch, 2), k, place, start : start + 512] = part

    @pl.when(e == 0)
    def _():
        for s in range(4):
            load_tok(s).start()
        for copy in load(0):
            copy.start()
        for s in range(4):
            load_tok(s).wait()
        pl.loop(0, 4)(lambda s: pick_rows(0, s))

    @pl.when(e + 1 < n_exp)
    def _():
        for copy in load(e + 1):
            copy.start()

    @pl.when(e // BATCH < (n_exp - 1) // BATCH)
    def _():
        pick_rows(e // BATCH + 1, lax.rem(e, BATCH))

    for copy in load(e):
        copy.wait()

    mine = [meta_ref[source, :top_k].astype(jnp.int32) - (first + e * cap) for source in range(4)]
    last = jnp.max(jnp.stack([jnp.where(slot < cap, slot, -1) for slot in mine]))
    batch, k = lax.rem(e // BATCH, 2), lax.rem(e, BATCH)

    def swiglu_cols(x, cols):
        gate_pre = jnp.dot(x, gate_w[now, :, cols], preferred_element_type=jnp.float32)
        up_pre = jnp.dot(x, up_w[now, :, cols], preferred_element_type=jnp.float32)
        return jax.nn.silu(gate_pre) * up_pre

    @pl.when(last < FEW_SLOTS)
    def _():
        x = jnp.concatenate([rows[batch, k, s * pitch : s * pitch + FEW_SLOTS] for s in range(4)], axis=0)
        for cols in spans:
            hidden = swiglu_cols(x, cols)
            gap = jnp.zeros((cap - FEW_SLOTS, hidden.shape[1]), jnp.float32)
            pieces = []
            for s in range(4):
                pieces += [hidden[s * FEW_SLOTS : (s + 1) * FEW_SLOTS], gap]
            out_ref[0, :, cols] = jnp.concatenate(pieces, axis=0).astype(jnp.bfloat16)

    @pl.when(last >= FEW_SLOTS)
    def _():
        x = rows[batch, k]
        for cols in spans:
            hidden = swiglu_cols(x, cols)
            pieces = [hidden[s * pitch : s * pitch + cap] for s in range(4)]
            out_ref[0, :, cols] = jnp.concatenate(pieces, axis=0).astype(jnp.bfloat16)


def expert_hidden(metas, sources, w_gate, w_up, cap):
    local_exp, d_model, width = w_gate.shape
    tok_dev = sources[0].shape[0]
    pitch = 16 * ((cap + 15) // 16)
    rows = 4 * cap
    return pl.pallas_call(
        functools.partial(hidden_kernel, cap, pitch),
        grid=(local_exp,),
        in_specs=[pl.BlockSpec(metas.shape, lambda e: (0, 0, 0))] + [ANY] * 6,
        out_specs=pl.BlockSpec((1, rows, width), lambda e: (e, 0, 0)),
        scratch_shapes=[
            pltpu.VMEM((4, tok_dev, d_model), jnp.bfloat16),
            pltpu.VMEM((2, BATCH, 4 * pitch, d_model), jnp.bfloat16),
            pltpu.VMEM((2, d_model, width), jnp.bfloat16),
            pltpu.VMEM((2, d_model, width), jnp.bfloat16),
            pltpu.SemaphoreType.DMA((4,)),
            pltpu.SemaphoreType.DMA((2,)),
            pltpu.SemaphoreType.DMA((2,)),
        ],
        out_shape=jax.ShapeDtypeStruct((local_exp, rows, width), jnp.bfloat16),
        compiler_params=params(),
        cost_estimate=cost(local_exp * rows * d_model * width * 4, local_exp * d_model * width * 4),
        name="expert_hidden",
    )(metas, *sources, w_gate, w_up)


def finish_kernel(
    cap, span, n_blocks, combine_hbm, peer_hbm, hidden_hbm, base_ref, weight_ref, shared_ref, out_hbm,
    combine, peer, hidden, rows, kept, given, for_tp, from_core, from_chip, from_tp, out,
    peer_sem, combine_sem, hidden_sem, store_sem, core_send, core_recv, chip_send, chip_recv, tp_send, tp_recv,
):
    step, group = pl.program_id(0), pl.program_id(1)
    n_steps = 2 * n_blocks
    tok_dev, cols = base_ref.shape
    core_peer, chip_peer, _, tp_peer = peers()
    load_peer = pltpu.make_async_copy(peer_hbm, peer, peer_sem)

    def load_combine(near, half):
        source = half if near else 2 + half
        return pltpu.make_async_copy(combine_hbm.at[pl.ds(source * tok_dev, tok_dev)], combine.at[half], combine_sem.at[half])

    def load_hidden(near, g):
        experts = pl.ds(g * GROUP, GROUP)
        source = pl.ds(0 if near else 2 * cap, 2 * cap)
        return pltpu.make_async_copy(hidden_hbm.at[experts, source], hidden.at[experts], hidden_sem.at[g])

    def core_copy(i):
        return pltpu.make_async_remote_copy(
            src_ref=given, dst_ref=from_core.at[i],
            send_sem=core_send.at[i], recv_sem=core_recv.at[i], device_id=core_peer, device_id_type=MESH,
        )

    def chip_copy(n):
        return pltpu.make_async_remote_copy(
            src_ref=from_core.at[n], dst_ref=from_chip.at[n],
            send_sem=chip_send.at[n], recv_sem=chip_recv.at[n], device_id=chip_peer, device_id_type=MESH,
        )

    def tp_copy(n):
        return pltpu.make_async_remote_copy(
            src_ref=for_tp.at[n], dst_ref=from_tp.at[n],
            send_sem=tp_send.at[n], recv_sem=tp_recv.at[n], device_id=tp_peer, device_id_type=MESH,
        )

    def store(n):
        here = pl.ds(pl.multiple_of(n * cols, cols), cols)
        return pltpu.make_async_copy(out.at[n], out_hbm.at[:, here], store_sem.at[n])

    def finalize(n):
        chip_copy(n).wait()
        tp_copy(n).wait()
        out[n] = (from_core[n_blocks + n] + from_chip[n] + from_tp[n]).astype(jnp.bfloat16)
        store(n).start()

    def gated(half):
        r = rows[lax.rem(step + 1, 2), half]
        return jnp.dot(combine[half], jnp.concatenate([r, r, r], axis=0), preferred_element_type=jnp.float32)

    @pl.when((step == 0) & (group == 0))
    def _():
        for g in range(hidden_sem.shape[0]):
            load_hidden(False, g).start()
        load_peer.start()
        for half in (1, 0):
            load_combine(False, half).start()
        greet((core_peer, chip_peer, tp_peer))

    @pl.when(step == 0)
    def _():
        load_hidden(False, group).wait()

    @pl.when(step == n_blocks)
    def _():
        load_hidden(True, group).wait()

    @pl.when(step < n_steps)
    def _():
        results = []
        for k in range(GROUP):
            results.append(jnp.dot(hidden[group * GROUP + k], weight_ref[k], preferred_element_type=jnp.float32))
        gap = jnp.zeros((span - GROUP * cap, cols), jnp.float32)
        place = pl.ds(pl.multiple_of(group * span, span), span)
        for half in range(2):
            part = jnp.concatenate([r[half * cap : (half + 1) * cap] for r in results] + [gap], axis=0)
            rows[lax.rem(step, 2), half, place, :] = part.astype(jnp.bfloat16)

    @pl.when(step == n_blocks - 1)
    def _():
        load_hidden(True, group).start()

    for near in (False, True):
        start = n_blocks + 1 if near else 1

        @pl.when((step == start) & (group < 2))
        def _():
            load_combine(near, 1 - group).wait()

    @pl.when((step >= 1) & (group == 0))
    def _():
        given[...] = gated(1)
        core_copy(step - 1).start()

    @pl.when((step >= 1) & (group == 1))
    def _():
        kept[...] = gated(0)

    @pl.when((step == n_blocks) & (group < 2))
    def _():
        load_combine(True, 1 - group).start()

    @pl.when((step >= 1) & (group == 2))
    def _():
        core_copy(step - 1).wait()
        from_core[step - 1] += kept[...]

    @pl.when((step >= 1) & (step <= n_blocks) & (group == 2))
    def _():
        chip_copy(step - 1).start()

    @pl.when((step > n_blocks) & (group == 2))
    def _():
        from_core[step - 1] += base_ref[...]

    @pl.when((step == 0) & (group == 2))
    def _():
        load_peer.wait()

    @pl.when((step < n_blocks) & (group == 2))
    def _():
        for_tp[step] = jnp.dot(peer[...], shared_ref[...], preferred_element_type=jnp.float32)
        tp_copy(step).start()

    @pl.when((step > n_blocks) & (step <= n_blocks + 4) & (group == 2))
    def _():
        finalize(step - 1 - n_blocks)

    @pl.when((step == n_steps) & (group == 2))
    def _():
        for n in range(4, n_blocks):
            finalize(n)
        for n in range(n_blocks):
            store(n).wait()


def finish(hidden, combine, base, peer_hidden, w_down, shared_down_w):
    local_exp, n_rows, width = hidden.shape
    n_groups = local_exp // GROUP
    cap = n_rows // 4
    depth = combine.shape[1]
    tok_dev, d_model = base.shape
    shared_width = peer_hidden.shape[1]
    cols = d_model // COL_BLOCKS
    sems = pltpu.SemaphoreType.DMA((COL_BLOCKS,))
    two_sems = pltpu.SemaphoreType.DMA((2 * COL_BLOCKS,))
    blocks = (COL_BLOCKS, tok_dev, cols)

    def weight_map(i, g):
        running = i < 2 * COL_BLOCKS
        return jnp.where(running, g, n_groups - 1), 0, jnp.where(running, lax.rem(i, COL_BLOCKS), COL_BLOCKS - 1)

    return pl.pallas_call(
        functools.partial(finish_kernel, cap, depth // 3 // n_groups, COL_BLOCKS),
        grid=(2 * COL_BLOCKS + 1, n_groups),
        out_shape=jax.ShapeDtypeStruct((tok_dev, d_model), jnp.bfloat16),
        in_specs=[
            ANY,
            ANY,
            ANY,
            pl.BlockSpec((tok_dev, cols), lambda i, g: (0, jnp.maximum(i - COL_BLOCKS - 1, 0))),
            pl.BlockSpec((GROUP, width, cols), weight_map),
            pl.BlockSpec((shared_width, cols), lambda i, g: (0, jnp.minimum(i, COL_BLOCKS - 1))),
        ],
        out_specs=ANY,
        scratch_shapes=[
            pltpu.VMEM((2, tok_dev, depth), jnp.bfloat16),
            pltpu.VMEM(peer_hidden.shape, jnp.bfloat16),
            pltpu.VMEM((local_exp, 2 * cap, width), jnp.bfloat16),
            pltpu.VMEM((2, 2, depth // 3, cols), jnp.bfloat16),
            pltpu.VMEM((tok_dev, cols), jnp.float32),
            pltpu.VMEM((tok_dev, cols), jnp.float32),
            pltpu.VMEM(blocks, jnp.float32),
            pltpu.VMEM((2 * COL_BLOCKS, tok_dev, cols), jnp.float32),
            pltpu.VMEM(blocks, jnp.float32),
            pltpu.VMEM(blocks, jnp.float32),
            pltpu.VMEM(blocks, jnp.bfloat16),
            pltpu.SemaphoreType.DMA,
            pltpu.SemaphoreType.DMA((2,)),
            pltpu.SemaphoreType.DMA((n_groups,)),
            sems, two_sems, two_sems, sems, sems, sems, sems,
        ],
        compiler_params=pltpu.CompilerParams(
            collective_id=0, has_side_effects=True, vmem_limit_bytes=67043328, dimension_semantics=("arbitrary", "arbitrary")
        ),
        cost_estimate=cost(2 * d_model * local_exp * (n_rows * width + 4 * tok_dev * 256), 2 * local_exp * width * d_model),
        name="finish",
    )(combine, peer_hidden, hidden, base, w_down, shared_down_w)


def solution(mesh):
    ep_size = mesh.shape["ep"]
    row_spec = P(("dp", "ep", "tp"), None)
    expert_spec = P("ep", None, None)

    def local_layer(tokens, expert_ids, gates, slots, shared_w1, shared_w3, shared_w2, expert_w1, expert_w3, expert_w2):
        tok_dev, d_model = tokens.shape
        top_k = expert_ids.shape[1]
        local_exp = expert_w1.shape[0]
        cap = capacity_rows(tok_dev, top_k, local_exp * ep_size)
        code = jnp.where(slots >= 0, expert_ids * cap + slots, -1)
        meta = jnp.concatenate([code.astype(jnp.float32).T, gates.T], axis=0)
        _, owner, slot = lane_tables(cap, local_exp)
        metas, tok_core, tok_chip, tok_both, combine, base, peer_hidden = start(meta, owner, slot, tokens, shared_w1, shared_w3, shared_w2, cap, local_exp)
        hidden = expert_hidden(metas, (tokens, tok_core, tok_chip, tok_both), expert_w1, expert_w3, cap)
        return finish(hidden, combine, base, peer_hidden, expert_w2, shared_w2)

    return jax.shard_map(local_layer, mesh=mesh, in_specs=(row_spec, row_spec, row_spec, row_spec, P(None, "tp"), P(None, "tp"), P("tp", None), expert_spec, expert_spec, expert_spec), out_specs=row_spec, check_vma=False)
```

time: 275 us -> 257 us (0.935)
  Pallas kernels: 269 us -> 251 us
    pallas_call x2, Pallas kernels: 195 us -> 180 us  [the longest x1 110 us: finish(): pl.pallas_call(functools.partial(finish_kernel, cap, depth // 3 // n_grou...]
    pallas_call x1, Pallas kernels: 73.7 us -> 70.8 us  [start(): pl.pallas_call(functools.partial(start_kernel, cap, local_exp), out_shape...]
where the time goes in v4:
time: 257 us; the launch traced here: 256 us
  Pallas kernels  251 us (98%)
  local copies, waits for them, and re-layouts  3.16 us (1%)
    pallas_call x1, Pallas kernels, finish(): pl.pallas_call(functools.partial(finish_kernel, cap, depth // 3 // n_grou...  110 us
    pallas_call x1, Pallas kernels, start(): pl.pallas_call(functools.partial(start_kernel, cap, local_exp), out_shape...  70.8 us
    pallas_call x1, Pallas kernels, expert_hidden(): pl.pallas_call(functools.partial(hidden_kernel, cap, pitch), grid=(local_...  69.4 us

profile of v4, /device:TPU:0, one launch (start us, length us, event | category | flops | bytes accessed | tf_op | source)
XLA Modules:
  0.0 255.8 jit_solution(424253641038484615)
XLA Ops:
  0.0 0.7 convert_bitcast_fusion
  0.7 1.3 pad_maximum_fusion.meta_ref
  2.0 70.8 %start.1 = (f32[4,8,512]{2,1,0:T(8,128)}, bf16[512,2048]{1,0:T(8,128)(2,1)}, bf16[512,2048]{1,0:T(8,128)(2,1)}, bf16[512,2048]{1,0:T(8,128)(2,1)}, bf16[2048,345...) custom-call(f32[8,512]{1,0:T(8,128)} %pad_maximum_fusion.meta_ref, ...), custom_call_target="tpu_custom_call" | custom-call | flops 29527900160 | bytes 57671680 | tf_op jit(solution)/shard_map/start/pallas_call | solution.py:170
  72.9 69.4 %expert_hidden.1.hidden_hbm = bf16[15,288,1408]{2,1,0:T(8,128)(2,1)} custom-call(f32[4,8,512]{2,1,0:T(8,128)} %get-tuple-element.14.meta_ref, bf16[512,2048]{1,0:T(8,128)(2,1)} %refs_0_.1, bf16[512,2048]{1,0:T(8,128)(2,1)} %get-tuple-element.15.refs_1_, bf16[512,2048]{1,0:T(8,128)(2,1)} %get-tuple-element.16.refs_2_, ...), custom_call_target="tpu_custom_call" | custom-call | flops 49828331520 | bytes 173015040 | tf_op jit(solution)/shard_map/expert_hidden/pallas_call | solution.py:286
  142.3 110.3 %finish.1 = bf16[512,2048]{1,0:T(8,128)(2,1)} custom-call(bf16[2048,3456]{1,0:T(8,128)(2,1)} %get-tuple-element.12.combine_hbm, bf16[512,2816]{1,0:T(8,128)(2,1)} %get-tuple-element.13.peer_hbm, bf16[15,288,1408]{2,1,0:T(8,128)(2,1)} %expert_hidden.1.hidden_hbm, f32[512,2048]{1,0:T(8,128)} %get-tuple-element.18.base_ref, bf16[15,1408,2048]{2,1,0:T(8,128)(2,1)} %weight_ref.1, ...), custom_call_target="tpu_custom_call" | custom-call | flops 57126420480 | bytes 86507520 | tf_op jit(solution)/shard_map/finish/pallas_call | solution.py:461
  252.6 3.2 %copy.14 = bf16[512,2048]{1,0:T(8,128)(2,1)} copy(bf16[512,2048]{1,0:T(8,128)(2,1)} %finish.1) | data formatting | bytes 4194304

commit v5 on v4

--- a/solution.py
+++ b/solution.py
@@ -11,6 +11,7 @@
 COL_BLOCKS = 8
 GROUP = 5
 BATCH = 4
+BUFFERS = 3
 FEW_SLOTS = 48
 SPAN = 512
 CHUNK = 128
@@ -76,15 +77,19 @@
     table = jnp.concatenate([slot_of, high, middle, rest - middle], axis=0).astype(jnp.bfloat16)
     spread = jnp.dot(table, owner_ref[...], preferred_element_type=jnp.float32)
     hit = spread[:CHUNK] == slot_ref[0:1, :]
-    depth = spread.shape[1]
+    n_groups = out_ref.shape[0]
+    span = spread.shape[1] // n_groups
     for i in range(3):
-        out_ref[:, i * depth : (i + 1) * depth] = jnp.where(hit, spread[(i + 1) * CHUNK : (i + 2) * CHUNK], 0.0).astype(jnp.bfloat16)
+        value = jnp.where(hit, spread[(i + 1) * CHUNK : (i + 2) * CHUNK], 0.0).astype(jnp.bfloat16)
+        for g in range(n_groups):
+            out_ref[g, :, i * span : (i + 1) * span] = value[:, g * span : (g + 1) * span]
 
 
 def start_kernel(
     cap, local_exp, meta_ref, owner_ref, slot_ref, tok_hbm, w_gate_hbm, w_up_hbm, w_down_hbm,
-    metas, tok_core, tok_chip, tok_both, combine_hbm, base_hbm, peer_hidden,
-    own, other, own_hidden, load_sem, send_sem, recv_sem,
+    metas, tok_core, tok_chip, tok_both, combine_hbm, base_hbm, peer_hbm,
+    own, other, own_hidden, peer_hidden, base, w_gate, w_up, w_down,
+    load_sem, store_sem, peer_sem, send_sem, recv_sem,
 ):
     core, chip, both, tp = peers()
     tok_dev, d_model = own.shape
@@ -95,18 +100,23 @@
             src_ref=src, dst_ref=dst, send_sem=send_sem.at[i], recv_sem=recv_sem.at[i], device_id=device, device_id_type=MESH
         )
 
-    load = pltpu.make_async_copy(tok_hbm, own, load_sem)
-    load.start()
     greet((core, chip, both, tp))
     meta_copies = [remote(meta_ref, metas.at[i + 1], device, i) for i, device in enumerate((core, chip, both))]
     for copy in meta_copies:
         copy.start()
     to_chip = remote(tok_hbm, tok_chip, chip, 3)
-    to_tp = remote(tok_hbm, other, tp, 4)
-    to_core = remote(tok_hbm, tok_core, core, 5)
-    onward = remote(tok_chip, tok_both, core, 6)
-    for copy in (to_chip, to_tp, to_core):
+    to_core = remote(tok_hbm, tok_core, core, 4)
+    onward = remote(tok_chip, tok_both, core, 5)
+    parts = [pl.ds(0, tok_dev // 2), pl.ds(tok_dev // 2, tok_dev // 4), pl.ds(tok_dev // 4 * 3, tok_dev // 4)]
+    to_tp = [remote(tok_hbm.at[part], other.at[part], tp, 6 + i) for i, part in enumerate(parts)]
+    to_chip.start()
+    for copy in to_tp:
         copy.start()
+    to_core.start()
+    pairs = ((tok_hbm, own), (w_gate_hbm, w_gate), (w_up_hbm, w_up), (w_down_hbm, w_down))
+    loads = [pltpu.make_async_copy(src, dst, load_sem.at[i]) for i, (src, dst) in enumerate(pairs)]
+    for load in loads:
+        load.start()
     metas[0] = meta_ref[...]
     for copy in meta_copies:
         copy.wait()
@@ -118,46 +128,60 @@
         here = pl.ds(pl.multiple_of(lax.rem(i, per_source) * CHUNK, CHUNK), CHUNK)
         combine_chunk(cap, local_exp, metas[i // per_source, :, here], owner_ref, slot_ref, out_ref)
 
+    n_groups, _, depth = combine_hbm.shape
     pltpu.emit_pipeline(
         write_combine,
         grid=(4 * per_source,),
-        out_specs=[pl.BlockSpec((CHUNK, combine_hbm.shape[1]), lambda i: (i, 0))],
+        out_specs=[pl.BlockSpec((n_groups, CHUNK, depth), lambda i: (0, i, 0))],
         _explicit_indices=True,
     )(combine_hbm)
 
-    def hidden_of(rows, result):
-        def part(first, step, count):
-            def body(index, gate_w_ref, up_w_ref):
-                gate_pre = jnp.dot(rows[...], gate_w_ref[...], preferred_element_type=jnp.float32)
-                up_pre = jnp.dot(rows[...], up_w_ref[...], preferred_element_type=jnp.float32)
-                here = pl.ds(pl.multiple_of((first + index.index[0]) * step, step), step)
-                result[:, here] = (jax.nn.silu(gate_pre) * up_pre).astype(jnp.bfloat16)
-
-            spec = pl.BlockSpec((d_model, step), lambda i: (0, first + i))
-            pltpu.emit_pipeline(body, grid=(count,), in_specs=[spec, spec], _explicit_indices=True)(w_gate_hbm, w_up_hbm)
-
-        part(0, 256, width // 256)
-
-    load.wait()
-    hidden_of(own, own_hidden)
-
-    def down(index, weight_ref, out_ref):
-        here = pl.ds(pl.multiple_of(index.index[0] * 512, 512), 512)
-        result = jnp.dot(own_hidden[...], weight_ref[...], preferred_element_type=jnp.float32)
-        out_ref[...] = own[:, here].astype(jnp.float32) + result
-
-    pltpu.emit_pipeline(
-        down,
-        grid=(d_model // 512,),
-        in_specs=[pl.BlockSpec((width, 512), lambda i: (0, i))],
-        out_specs=[pl.BlockSpec((tok_dev, 512), lambda i: (0, i))],
-        _explicit_indices=True,
-    )(w_down_hbm, base_hbm)
-
+    def hidden_of(rows, result, here):
+        def cols_of(cols):
+            gate_pre = jnp.dot(rows[here], w_gate[:, cols], preferred_element_type=jnp.float32)
+            up_pre = jnp.dot(rows[here], w_up[:, cols], preferred_element_type=jnp.float32)
+            result[here, cols] = (jax.nn.silu(gate_pre) * up_pre).astype(jnp.bfloat16)
+
+        whole = width // SPAN * SPAN
+
+        @pl.loop(0, width // SPAN)
+        def _(i):
+            cols_of(pl.ds(pl.multiple_of(i * SPAN, SPAN), SPAN))
+
+        if whole < width:
+            cols_of(pl.ds(whole, width - whole))
+
+    for load in loads[:3]:
+        load.wait()
+    hidden_of(own, own_hidden, pl.ds(0, tok_dev))
+
+    def store_peer(i):
+        return pltpu.make_async_copy(peer_hidden.at[parts[i]], peer_hbm.at[parts[i]], peer_sem.at[i])
+
+    to_tp[0].wait()
+    hidden_of(other, peer_hidden, parts[0])
+    store_peer(0).start()
+    loads[3].wait()
+
+    @pl.loop(0, d_model // SPAN)
+    def _(i):
+        cols = pl.ds(pl.multiple_of(i * SPAN, SPAN), SPAN)
+        down = jnp.dot(own_hidden[...], w_down[:, cols], preferred_element_type=jnp.float32)
+        base[:, cols] = own[:, cols].astype(jnp.float32) + down
+
+    store = pltpu.make_async_copy(base, base_hbm, store_sem)
+    store.start()
+    to_tp[1].wait()
+    hidden_of(other, peer_hidden, parts[1])
+    store_peer(1).start()
     to_chip.wait()
     onward.start()
-    to_tp.wait()
-    hidden_of(other, peer_hidden)
+    to_tp[2].wait()
+    hidden_of(other, peer_hidden, parts[2])
+    store_peer(2).start()
+    for i in range(3):
+        store_peer(i).wait()
+    store.wait()
     to_core.wait()
     onward.wait()
 
@@ -165,6 +189,7 @@
 def start(meta, owner, slot, tokens, w_gate, w_up, w_down, cap, local_exp):
     tok_dev, d_model = tokens.shape
     width = w_gate.shape[1]
+    n_groups = local_exp // GROUP
     vmem = pl.BlockSpec(memory_space=pltpu.VMEM)
     tok_shape = jax.ShapeDtypeStruct((tok_dev, d_model), jnp.bfloat16)
     return pl.pallas_call(
@@ -172,19 +197,26 @@
         out_shape=[
             jax.ShapeDtypeStruct((4,) + meta.shape, jnp.float32),
             tok_shape, tok_shape, tok_shape,
-            jax.ShapeDtypeStruct((4 * tok_dev, 3 * owner.shape[1]), jnp.bfloat16),
+            jax.ShapeDtypeStruct((n_groups, 4 * tok_dev, 3 * owner.shape[1] // n_groups), jnp.bfloat16),
             jax.ShapeDtypeStruct((tok_dev, d_model), jnp.float32),
             jax.ShapeDtypeStruct((tok_dev, width), jnp.bfloat16),
         ],
         in_specs=[vmem, vmem, vmem, ANY, ANY, ANY, ANY],
-        out_specs=[vmem, ANY, ANY, ANY, ANY, ANY, vmem],
+        out_specs=[vmem, ANY, ANY, ANY, ANY, ANY, ANY],
         scratch_shapes=[
             pltpu.VMEM((tok_dev, d_model), jnp.bfloat16),
             pltpu.VMEM((tok_dev, d_model), jnp.bfloat16),
             pltpu.VMEM((tok_dev, width), jnp.bfloat16),
+            pltpu.VMEM((tok_dev, width), jnp.bfloat16),
+            pltpu.VMEM((tok_dev, d_model), jnp.float32),
+            pltpu.VMEM((d_model, width), jnp.bfloat16),
+            pltpu.VMEM((d_model, width), jnp.bfloat16),
+            pltpu.VMEM((width, d_model), jnp.bfloat16),
+            pltpu.SemaphoreType.DMA((4,)),
             pltpu.SemaphoreType.DMA,
-            pltpu.SemaphoreType.DMA((7,)),
-            pltpu.SemaphoreType.DMA((7,)),
+            pltpu.SemaphoreType.DMA((3,)),
+            pltpu.SemaphoreType.DMA((9,)),
+            pltpu.SemaphoreType.DMA((9,)),
         ],
         compiler_params=pltpu.CompilerParams(collective_id=1, has_side_effects=True, vmem_limit_bytes=67043328),
         cost_estimate=cost(10 * tok_dev * d_model * width, 10 * d_model * width),
@@ -200,14 +232,15 @@
     d_model = tok.shape[2]
     top_k = meta_ref.shape[1] // 2
     spans = [slice(start, min(start + SPAN, width)) for start in range(0, width, SPAN)]
-    now = lax.rem(e, 2)
+    n_buf = gate_w.shape[0]
+    now = lax.rem(e, n_buf)
     first = (lax.axis_index("ep") * n_exp) * cap
 
     def load_tok(s):
         return pltpu.make_async_copy(tok_hbm[s], tok.at[s], tok_sem.at[s])
 
     def load(i):
-        slot = lax.rem(i, 2)
+        slot = lax.rem(i, n_buf)
         return (
             pltpu.make_async_copy(gate_hbm.at[i], gate_w.at[slot], gate_sem.at[slot]),
             pltpu.make_async_copy(up_hbm.at[i], up_w.at[slot], up_sem.at[slot]),
@@ -231,15 +264,16 @@
     def _():
         for s in range(4):
             load_tok(s).start()
-        for copy in load(0):
-            copy.start()
+        for i in range(n_buf - 1):
+            for copy in load(i):
+                copy.start()
         for s in range(4):
             load_tok(s).wait()
         pl.loop(0, 4)(lambda s: pick_rows(0, s))
 
-    @pl.when(e + 1 < n_exp)
-    def _():
-        for copy in load(e + 1):
+    @pl.when(e + n_buf - 1 < n_exp)
+    def _():
+        for copy in load(e + n_buf - 1):
             copy.start()
 
     @pl.when(e // BATCH < (n_exp - 1) // BATCH)
@@ -291,11 +325,11 @@
         scratch_shapes=[
             pltpu.VMEM((4, tok_dev, d_model), jnp.bfloat16),
             pltpu.VMEM((2, BATCH, 4 * pitch, d_model), jnp.bfloat16),
-            pltpu.VMEM((2, d_model, width), jnp.bfloat16),
-            pltpu.VMEM((2, d_model, width), jnp.bfloat16),
+            pltpu.VMEM((BUFFERS, d_model, width), jnp.bfloat16),
+            pltpu.VMEM((BUFFERS, d_model, width), jnp.bfloat16),
             pltpu.SemaphoreType.DMA((4,)),
-            pltpu.SemaphoreType.DMA((2,)),
-            pltpu.SemaphoreType.DMA((2,)),
+            pltpu.SemaphoreType.DMA((BUFFERS,)),
+            pltpu.SemaphoreType.DMA((BUFFERS,)),
         ],
         out_shape=jax.ShapeDtypeStruct((local_exp, rows, width), jnp.bfloat16),
         compiler_params=params(),
@@ -310,14 +344,23 @@
     peer_sem, combine_sem, hidden_sem, store_sem, core_send, core_recv, chip_send, chip_recv, tp_send, tp_recv,
 ):
     step, group = pl.program_id(0), pl.program_id(1)
+    n_groups = combine.shape[1]
     n_steps = 2 * n_blocks
     tok_dev, cols = base_ref.shape
     core_peer, chip_peer, _, tp_peer = peers()
     load_peer = pltpu.make_async_copy(peer_hbm, peer, peer_sem)
-
-    def load_combine(near, half):
-        source = half if near else 2 + half
-        return pltpu.make_async_copy(combine_hbm.at[pl.ds(source * tok_dev, tok_dev)], combine.at[half], combine_sem.at[half])
+    old_group = lax.rem(group + n_groups - 1, n_groups)
+    old_step = (step * n_groups + group - 1) // n_groups
+    slot = lax.rem(step * n_groups + group, 2)
+    done = step - 1
+
+    def load_combine(near, g):
+        return [
+            pltpu.make_async_copy(
+                combine_hbm.at[g, pl.ds((half if near else 2 + half) * tok_dev, tok_dev)], combine.at[half, g], combine_sem.at[half, g]
+            )
+            for half in range(2)
+        ]
 
     def load_hidden(near, g):
         experts = pl.ds(g * GROUP, GROUP)
@@ -326,7 +369,7 @@
 
     def core_copy(i):
         return pltpu.make_async_remote_copy(
-            src_ref=given, dst_ref=from_core.at[i],
+            src_ref=given.at[lax.rem(i, 2)], dst_ref=from_core.at[i],
             send_sem=core_send.at[i], recv_sem=core_recv.at[i], device_id=core_peer, device_id_type=MESH,
         )
 
@@ -352,87 +395,96 @@
         out[n] = (from_core[n_blocks + n] + from_chip[n] + from_tp[n]).astype(jnp.bfloat16)
         store(n).start()
 
-    def gated(half):
-        r = rows[lax.rem(step + 1, 2), half]
-        return jnp.dot(combine[half], jnp.concatenate([r, r, r], axis=0), preferred_element_type=jnp.float32)
-
-    @pl.when((step == 0) & (group == 0))
-    def _():
-        for g in range(hidden_sem.shape[0]):
-            load_hidden(False, g).start()
-        load_peer.start()
-        for half in (1, 0):
-            load_combine(False, half).start()
-        greet((core_peer, chip_peer, tp_peer))
-
-    @pl.when(step == 0)
-    def _():
-        load_hidden(False, group).wait()
-
-    @pl.when(step == n_blocks)
-    def _():
-        load_hidden(True, group).wait()
-
-    @pl.when(step < n_steps)
-    def _():
+    def expert_rows():
         results = []
         for k in range(GROUP):
             results.append(jnp.dot(hidden[group * GROUP + k], weight_ref[k], preferred_element_type=jnp.float32))
         gap = jnp.zeros((span - GROUP * cap, cols), jnp.float32)
-        place = pl.ds(pl.multiple_of(group * span, span), span)
         for half in range(2):
             part = jnp.concatenate([r[half * cap : (half + 1) * cap] for r in results] + [gap], axis=0)
-            rows[lax.rem(step, 2), half, place, :] = part.astype(jnp.bfloat16)
+            rows[slot, half] = part.astype(jnp.bfloat16)
+
+    def add_gated():
+        for half, sums in enumerate((kept, given)):
+            r = rows[1 - slot, half]
+            stacked = jnp.concatenate([r, r, r], axis=0)
+            more = jnp.dot(combine[half, old_group], stacked, preferred_element_type=jnp.float32)
+            place = lax.rem(old_step, 2)
+            sums[place] = jnp.where(old_group == 0, 0.0, sums[place]) + more
+
+    @pl.when((step == 0) & (group == 0))
+    def _():
+        for g in range(hidden_sem.shape[0]):
+            load_hidden(False, g).start()
+        load_peer.start()
+        for g in range(hidden_sem.shape[0]):
+            for copy in load_combine(False, g):
+                copy.start()
+        greet((core_peer, chip_peer, tp_peer))
+
+    for near in (False, True):
+        first = n_blocks if near else 0
+
+        @pl.when(step == first)
+        def _():
+            load_hidden(near, group).wait()
+
+        @pl.when((old_step == first) & (step + group >= 1))
+        def _():
+            for copy in load_combine(near, old_group):
+                copy.wait()
+
+    @pl.when((step == 0) & (group == 0))
+    def _():
+        expert_rows()
+
+    @pl.when((step + group >= 1) & (step < n_steps))
+    def _():
+        add_gated()
+        expert_rows()
+
+    @pl.when((step == n_steps) & (group == 0))
+    def _():
+        add_gated()
 
     @pl.when(step == n_blocks - 1)
     def _():
         load_hidden(True, group).start()
 
-    for near in (False, True):
-        start = n_blocks + 1 if near else 1
-
-        @pl.when((step == start) & (group < 2))
-        def _():
-            load_combine(near, 1 - group).wait()
+    @pl.when(old_step == n_blocks - 1)
+    def _():
+        for copy in load_combine(True, old_group):
+            copy.start()
 
     @pl.when((step >= 1) & (group == 0))
     def _():
-        given[...] = gated(1)
-        core_copy(step - 1).start()
-
-    @pl.when((step >= 1) & (group == 1))
-    def _():
-        kept[...] = gated(0)
-
-    @pl.when((step == n_blocks) & (group < 2))
-    def _():
-        load_combine(True, 1 - group).start()
+        core_copy(done).start()
 
     @pl.when((step >= 1) & (group == 2))
     def _():
-        core_copy(step - 1).wait()
-        from_core[step - 1] += kept[...]
+        core_copy(done).wait()
+        from_core[done] += kept[lax.rem(done, 2)]
 
     @pl.when((step >= 1) & (step <= n_blocks) & (group == 2))
     def _():
-        chip_copy(step - 1).start()
+        chip_copy(done).start()
 
     @pl.when((step > n_blocks) & (group == 2))
     def _():
-        from_core[step - 1] += base_ref[...]
-
-    @pl.when((step == 0) & (group == 2))
+        from_core[done] += base_ref[...]
+
+    @pl.when((step == 0) & (group == 1))
     def _():
         load_peer.wait()
 
-    @pl.when((step < n_blocks) & (group == 2))
+    @pl.when((step < n_blocks) & (group == 1))
     def _():
         for_tp[step] = jnp.dot(peer[...], shared_ref[...], preferred_element_type=jnp.float32)
         tp_copy(step).start()
 
     @pl.when((step > n_blocks) & (step <= n_blocks + 4) & (group == 2))
     def _():
-        finalize(step - 1 - n_blocks)
+        finalize(done - n_blocks)
 
     @pl.when((step == n_steps) & (group == 2))
     def _():
@@ -446,7 +498,7 @@
     local_exp, n_rows, width = hidden.shape
     n_groups = local_exp // GROUP
     cap = n_rows // 4
-    depth = combine.shape[1]
+    depth = combine.shape[2]
     tok_dev, d_model = base.shape
     shared_width = peer_hidden.shape[1]
     cols = d_model // COL_BLOCKS
@@ -459,7 +511,7 @@
         return jnp.where(running, g, n_groups - 1), 0, jnp.where(running, lax.rem(i, COL_BLOCKS), COL_BLOCKS - 1)
 
     return pl.pallas_call(
-        functools.partial(finish_kernel, cap, depth // 3 // n_groups, COL_BLOCKS),
+        functools.partial(finish_kernel, cap, depth // 3, COL_BLOCKS),
         grid=(2 * COL_BLOCKS + 1, n_groups),
         out_shape=jax.ShapeDtypeStruct((tok_dev, d_model), jnp.bfloat16),
         in_specs=[
@@ -472,19 +524,19 @@
         ],
         out_specs=ANY,
         scratch_shapes=[
-            pltpu.VMEM((2, tok_dev, depth), jnp.bfloat16),
+            pltpu.VMEM((2, n_groups, tok_dev, depth), jnp.bfloat16),
             pltpu.VMEM(peer_hidden.shape, jnp.bfloat16),
             pltpu.VMEM((local_exp, 2 * cap, width), jnp.bfloat16),
             pltpu.VMEM((2, 2, depth // 3, cols), jnp.bfloat16),
-            pltpu.VMEM((tok_dev, cols), jnp.float32),
-            pltpu.VMEM((tok_dev, cols), jnp.float32),
+            pltpu.VMEM((2, tok_dev, cols), jnp.float32),
+            pltpu.VMEM((2, tok_dev, cols), jnp.float32),
             pltpu.VMEM(blocks, jnp.float32),
             pltpu.VMEM((2 * COL_BLOCKS, tok_dev, cols), jnp.float32),
             pltpu.VMEM(blocks, jnp.float32),
             pltpu.VMEM(blocks, jnp.float32),
             pltpu.VMEM(blocks, jnp.bfloat16),
             pltpu.SemaphoreType.DMA,
-            pltpu.SemaphoreType.DMA((2,)),
+            pltpu.SemaphoreType.DMA((2, n_groups)),
             pltpu.SemaphoreType.DMA((n_groups,)),
             sems, two_sems, two_sems, sems, sems, sems, sems,
         ],

time: 257 us -> 243 us (0.946)
  Pallas kernels: 251 us -> 237 us
    pallas_call x1, Pallas kernels: 70.8 us -> 59.1 us  [start(): pl.pallas_call(functools.partial(start_kernel, cap, local_exp), out_shape...]
where the time goes in v5:
time: 243 us; the launch traced here: 242 us
  Pallas kernels  237 us (98%)
  local copies, waits for them, and re-layouts  3.16 us (1%)
    pallas_call x1, Pallas kernels, finish(): pl.pallas_call(functools.partial(finish_kernel, cap, depth // 3, COL_BLOC...  109 us
    pallas_call x1, Pallas kernels, expert_hidden(): pl.pallas_call(functools.partial(hidden_kernel, cap, pitch), grid=(local_...  68 us
    pallas_call x1, Pallas kernels, start(): pl.pallas_call(functools.partial(start_kernel, cap, local_exp), out_shape...  59.1 us

profile of v5, /device:TPU:0, one launch (start us, length us, event | category | flops | bytes accessed | tf_op | source)
XLA Modules:
  0.0 241.8 jit_solution(14410260079943163854)
XLA Ops:
  0.0 0.7 convert_bitcast_fusion
  0.7 1.3 pad_maximum_fusion.meta_ref
  2.0 59.1 %start.1 = (f32[4,8,512]{2,1,0:T(8,128)}, bf16[512,2048]{1,0:T(8,128)(2,1)}, bf16[512,2048]{1,0:T(8,128)(2,1)}, bf16[512,2048]{1,0:T(8,128)(2,1)}, bf16[3,2048,1...) custom-call(f32[8,512]{1,0:T(8,128)} %pad_maximum_fusion.meta_ref, ...), custom_call_target="tpu_custom_call" | custom-call | flops 29527900160 | bytes 57671680 | tf_op jit(solution)/shard_map/start/pallas_call | solution.py:195
  61.2 68.0 %expert_hidden.1.hidden_hbm = bf16[15,288,1408]{2,1,0:T(8,128)(2,1)} custom-call(f32[4,8,512]{2,1,0:T(8,128)} %get-tuple-element.14.meta_ref, bf16[512,2048]{1,0:T(8,128)(2,1)} %refs_0_.1, bf16[512,2048]{1,0:T(8,128)(2,1)} %get-tuple-element.15.refs_1_, bf16[512,2048]{1,0:T(8,128)(2,1)} %get-tuple-element.16.refs_2_, ...), custom_call_target="tpu_custom_call" | custom-call | flops 49828331520 | bytes 173015040 | tf_op jit(solution)/shard_map/expert_hidden/pallas_call | solution.py:320
  129.2 109.4 %finish.1 = bf16[512,2048]{1,0:T(8,128)(2,1)} custom-call(bf16[3,2048,1152]{2,1,0:T(8,128)(2,1)} %get-tuple-element.12.combine_hbm, bf16[512,2816]{1,0:T(8,128)(2,1)} %get-tuple-element.13.peer_hbm, bf16[15,288,1408]{2,1,0:T(8,128)(2,1)} %expert_hidden.1.hidden_hbm, f32[512,2048]{1,0:T(8,128)} %get-tuple-element.18.base_ref, ...), custom_call_target="tpu_custom_call" | custom-call | flops 57126420480 | bytes 86507520 | tf_op jit(solution)/shard_map/finish/pallas_call | solution.py:513
  238.7 3.2 %copy.14 = bf16[512,2048]{1,0:T(8,128)(2,1)} copy(bf16[512,2048]{1,0:T(8,128)(2,1)} %finish.1) | data formatting | bytes 4194304

commit v6 on v5

--- a/solution.py
+++ b/solution.py
@@ -104,14 +104,15 @@
     meta_copies = [remote(meta_ref, metas.at[i + 1], device, i) for i, device in enumerate((core, chip, both))]
     for copy in meta_copies:
         copy.start()
-    to_chip = remote(tok_hbm, tok_chip, chip, 3)
-    to_core = remote(tok_hbm, tok_core, core, 4)
-    onward = remote(tok_chip, tok_both, core, 5)
-    parts = [pl.ds(0, tok_dev // 2), pl.ds(tok_dev // 2, tok_dev // 4), pl.ds(tok_dev // 4 * 3, tok_dev // 4)]
-    to_tp = [remote(tok_hbm.at[part], other.at[part], tp, 6 + i) for i, part in enumerate(parts)]
-    to_chip.start()
-    for copy in to_tp:
-        copy.start()
+    to_core = remote(tok_hbm, tok_core, core, 3)
+    early = tok_dev // 4 * 3
+    parts = [pl.ds(0, early), pl.ds(early, tok_dev - early)]
+    to_tp = [remote(tok_hbm.at[part], other.at[part], tp, 4 + i) for i, part in enumerate(parts)]
+    to_chip = [remote(tok_hbm.at[part], tok_chip.at[part], chip, 6 + i) for i, part in enumerate(parts)]
+    onward = [remote(tok_chip.at[part], tok_both.at[part], core, 8 + i) for i, part in enumerate(parts)]
+    for i in range(2):
+        to_chip[i].start()
+        to_tp[i].start()
     to_core.start()
     pairs = ((tok_hbm, own), (w_gate_hbm, w_gate), (w_up_hbm, w_up), (w_down_hbm, w_down))
     loads = [pltpu.make_async_copy(src, dst, load_sem.at[i]) for i, (src, dst) in enumerate(pairs)]
@@ -158,9 +159,6 @@
     def store_peer(i):
         return pltpu.make_async_copy(peer_hidden.at[parts[i]], peer_hbm.at[parts[i]], peer_sem.at[i])
 
-    to_tp[0].wait()
-    hidden_of(other, peer_hidden, parts[0])
-    store_peer(0).start()
     loads[3].wait()
 
     @pl.loop(0, d_model // SPAN)
@@ -171,19 +169,18 @@
 
     store = pltpu.make_async_copy(base, base_hbm, store_sem)
     store.start()
-    to_tp[1].wait()
-    hidden_of(other, peer_hidden, parts[1])
-    store_peer(1).start()
-    to_chip.wait()
-    onward.start()
-    to_tp[2].wait()
-    hidden_of(other, peer_hidden, parts[2])
-    store_peer(2).start()
-    for i in range(3):
+    for i in range(2):
+        to_chip[i].wait()
+        onward[i].start()
+        to_tp[i].wait()
+        hidden_of(other, peer_hidden, parts[i])
+        store_peer(i).start()
+    for i in range(2):
         store_peer(i).wait()
     store.wait()
     to_core.wait()
-    onward.wait()
+    for copy in onward:
+        copy.wait()
 
 
 def start(meta, owner, slot, tokens, w_gate, w_up, w_down, cap, local_exp):
@@ -214,9 +211,9 @@
             pltpu.VMEM((width, d_model), jnp.bfloat16),
             pltpu.SemaphoreType.DMA((4,)),
             pltpu.SemaphoreType.DMA,
-            pltpu.SemaphoreType.DMA((3,)),
-            pltpu.SemaphoreType.DMA((9,)),
-            pltpu.SemaphoreType.DMA((9,)),
+            pltpu.SemaphoreType.DMA((2,)),
+            pltpu.SemaphoreType.DMA((10,)),
+            pltpu.SemaphoreType.DMA((10,)),
         ],
         compiler_params=pltpu.CompilerParams(collective_id=1, has_side_effects=True, vmem_limit_bytes=67043328),
         cost_estimate=cost(10 * tok_dev * d_model * width, 10 * d_model * width),
@@ -339,19 +336,16 @@
 
 
 def finish_kernel(
-    cap, span, n_blocks, combine_hbm, peer_hbm, hidden_hbm, base_ref, weight_ref, shared_ref, out_hbm,
-    combine, peer, hidden, rows, kept, given, for_tp, from_core, from_chip, from_tp, out,
-    peer_sem, combine_sem, hidden_sem, store_sem, core_send, core_recv, chip_send, chip_recv, tp_send, tp_recv,
+    cap, span, n_blocks, combine_hbm, peer_hbm, hidden_hbm, weight_hbm, base_hbm, shared_hbm, out_hbm,
+    base, shared, combine, peer, hidden, weight, rows, kept, given, for_tp, from_core, from_chip, from_tp, out,
+    base_sem, shared_sem, peer_sem, combine_sem, hidden_sem, weight_sem, store_sem, core_send, core_recv, chip_send, chip_recv, tp_send, tp_recv,
 ):
-    step, group = pl.program_id(0), pl.program_id(1)
+    step = pl.program_id(0)
     n_groups = combine.shape[1]
     n_steps = 2 * n_blocks
-    tok_dev, cols = base_ref.shape
+    tok_dev, cols = base.shape[1:]
     core_peer, chip_peer, _, tp_peer = peers()
     load_peer = pltpu.make_async_copy(peer_hbm, peer, peer_sem)
-    old_group = lax.rem(group + n_groups - 1, n_groups)
-    old_step = (step * n_groups + group - 1) // n_groups
-    slot = lax.rem(step * n_groups + group, 2)
     done = step - 1
 
     def load_combine(near, g):
@@ -367,6 +361,21 @@
         source = pl.ds(0 if near else 2 * cap, 2 * cap)
         return pltpu.make_async_copy(hidden_hbm.at[experts, source], hidden.at[experts], hidden_sem.at[g])
 
+    def load_weight(i, g):
+        here = pl.ds(pl.multiple_of(lax.rem(i, n_blocks) * cols, cols), cols)
+        return pltpu.make_async_copy(weight_hbm.at[pl.ds(g * GROUP, GROUP), :, here], weight.at[g], weight_sem.at[g])
+
+    def cols_of(n):
+        return pl.ds(pl.multiple_of(n * cols, cols), cols)
+
+    def load_base(n):
+        slot = lax.rem(n, 2)
+        return pltpu.make_async_copy(base_hbm.at[:, cols_of(n)], base.at[slot], base_sem.at[slot])
+
+    def load_shared(n):
+        slot = lax.rem(n, 2)
+        return pltpu.make_async_copy(shared_hbm.at[:, cols_of(n)], shared.at[slot], shared_sem.at[slot])
+
     def core_copy(i):
         return pltpu.make_async_remote_copy(
             src_ref=given.at[lax.rem(i, 2)], dst_ref=from_core.at[i],
@@ -395,98 +404,147 @@
         out[n] = (from_core[n_blocks + n] + from_chip[n] + from_tp[n]).astype(jnp.bfloat16)
         store(n).start()
 
-    def expert_rows():
+    def expert_rows(g):
         results = []
         for k in range(GROUP):
-            results.append(jnp.dot(hidden[group * GROUP + k], weight_ref[k], preferred_element_type=jnp.float32))
+            results.append(jnp.dot(hidden[g * GROUP + k], weight[g, k], preferred_element_type=jnp.float32))
         gap = jnp.zeros((span - GROUP * cap, cols), jnp.float32)
         for half in range(2):
             part = jnp.concatenate([r[half * cap : (half + 1) * cap] for r in results] + [gap], axis=0)
-            rows[slot, half] = part.astype(jnp.bfloat16)
-
-    def add_gated():
+            rows[g, half] = part.astype(jnp.bfloat16)
+
+    def add_gated(i, g):
+        place = lax.rem(i, 2)
         for half, sums in enumerate((kept, given)):
-            r = rows[1 - slot, half]
-            stacked = jnp.concatenate([r, r, r], axis=0)
-            more = jnp.dot(combine[half, old_group], stacked, preferred_element_type=jnp.float32)
-            place = lax.rem(old_step, 2)
-            sums[place] = jnp.where(old_group == 0, 0.0, sums[place]) + more
-
-    @pl.when((step == 0) & (group == 0))
-    def _():
-        for g in range(hidden_sem.shape[0]):
+            r = rows[g, half]
+            more = jnp.dot(combine[half, g], jnp.concatenate([r, r, r], axis=0), preferred_element_type=jnp.float32)
+            sums[place] = more if g == 0 else sums[place] + more
+
+    def share_peer():
+        load_shared(step).wait()
+        for_tp[step] = jnp.dot(peer[...], shared[lax.rem(step, 2)], preferred_element_type=jnp.float32)
+        tp_copy(step).start()
+
+    @pl.when(step == 0)
+    def _():
+        load_hidden(False, 0).start()
+        load_weight(step, 0).start()
+        load_hidden(False, 1).start()
+        load_weight(step, 1).start()
+        for copy in load_combine(False, 0):
+            copy.start()
+        greet((core_peer, chip_peer, tp_peer))
+
+    def ready(i, g):
+        for near in (False, True):
+
+            @pl.when(i == (n_blocks if near else 0))
+            def _():
+                for copy in load_combine(near, g):
+                    copy.wait()
+
+    def hidden_ready(g):
+        for near in (False, True):
+
+            @pl.when(step == (n_blocks if near else 0))
+            def _():
+                load_hidden(near, g).wait()
+
+    def refill(g):
+        @pl.when(step < n_steps - 1)
+        def _():
+            load_weight(step + 1, g).start()
+
+        @pl.when(step == n_blocks - 1)
+        def _():
+            load_hidden(True, g).start()
+
+    def refill_combine(i, g):
+        @pl.when(i == n_blocks - 1)
+        def _():
+            for copy in load_combine(True, g):
+                copy.start()
+
+    last = n_groups - 1
+    hidden_ready(0)
+    ready(done, last)
+
+    @pl.when(step == 0)
+    def _():
+        load_weight(step, 0).wait()
+        for g in range(2, n_groups):
             load_hidden(False, g).start()
-        load_peer.start()
-        for g in range(hidden_sem.shape[0]):
+            load_weight(step, g).start()
+        for g in range(1, n_groups):
             for copy in load_combine(False, g):
                 copy.start()
-        greet((core_peer, chip_peer, tp_peer))
-
-    for near in (False, True):
-        first = n_blocks if near else 0
-
-        @pl.when(step == first)
-        def _():
-            load_hidden(near, group).wait()
-
-        @pl.when((old_step == first) & (step + group >= 1))
-        def _():
-            for copy in load_combine(near, old_group):
-                copy.wait()
-
-    @pl.when((step == 0) & (group == 0))
-    def _():
-        expert_rows()
-
-    @pl.when((step + group >= 1) & (step < n_steps))
-    def _():
-        add_gated()
-        expert_rows()
-
-    @pl.when((step == n_steps) & (group == 0))
-    def _():
-        add_gated()
-
-    @pl.when(step == n_blocks - 1)
-    def _():
-        load_hidden(True, group).start()
-
-    @pl.when(old_step == n_blocks - 1)
-    def _():
-        for copy in load_combine(True, old_group):
-            copy.start()
-
-    @pl.when((step >= 1) & (group == 0))
-    def _():
+        load_peer.start()
+        load_shared(step).start()
+        expert_rows(0)
+
+    @pl.when((step > 0) & (step < n_steps))
+    def _():
+        add_gated(done, last)
         core_copy(done).start()
-
-    @pl.when((step >= 1) & (group == 2))
+        load_weight(step, 0).wait()
+        expert_rows(0)
+
+    @pl.when(step == n_steps)
+    def _():
+        add_gated(done, last)
+        core_copy(done).start()
+
+    refill(0)
+    refill_combine(done, last)
+
+    @pl.when((step >= 1) & (step <= n_blocks))
     def _():
         core_copy(done).wait()
         from_core[done] += kept[lax.rem(done, 2)]
-
-    @pl.when((step >= 1) & (step <= n_blocks) & (group == 2))
-    def _():
         chip_copy(done).start()
 
-    @pl.when((step > n_blocks) & (group == 2))
-    def _():
-        from_core[done] += base_ref[...]
-
-    @pl.when((step == 0) & (group == 1))
-    def _():
-        load_peer.wait()
-
-    @pl.when((step < n_blocks) & (group == 1))
-    def _():
-        for_tp[step] = jnp.dot(peer[...], shared_ref[...], preferred_element_type=jnp.float32)
-        tp_copy(step).start()
-
-    @pl.when((step > n_blocks) & (step <= n_blocks + 4) & (group == 2))
+    @pl.when(step > n_blocks)
+    def _():
+        core_copy(done).wait()
+        load_base(done - n_blocks).wait()
+        from_core[done] += kept[lax.rem(done, 2)] + base[lax.rem(done, 2)]
+
+    for g in range(1, n_groups):
+        hidden_ready(g)
+        ready(step, g - 1)
+
+        @pl.when(step < n_steps)
+        def _():
+            load_weight(step, g).wait()
+            add_gated(step, g - 1)
+            expert_rows(g)
+
+        refill(g)
+        refill_combine(step, g - 1)
+
+        if g == 1:
+
+            @pl.when(step == 0)
+            def _():
+                load_peer.wait()
+
+            @pl.when(step < n_blocks - 1)
+            def _():
+                load_shared(step + 1).start()
+
+            @pl.when(step < n_blocks)
+            def _():
+                share_peer()
+
+            @pl.when((step >= n_blocks) & (step < n_steps))
+            def _():
+                load_base(step - n_blocks).start()
+
+    @pl.when((step > n_blocks) & (step <= n_blocks + 4))
     def _():
         finalize(done - n_blocks)
 
-    @pl.when((step == n_steps) & (group == 2))
+    @pl.when(step == n_steps)
     def _():
         for n in range(4, n_blocks):
             finalize(n)
@@ -504,30 +562,25 @@
     cols = d_model // COL_BLOCKS
     sems = pltpu.SemaphoreType.DMA((COL_BLOCKS,))
     two_sems = pltpu.SemaphoreType.DMA((2 * COL_BLOCKS,))
+    group_sems = pltpu.SemaphoreType.DMA((n_groups,))
     blocks = (COL_BLOCKS, tok_dev, cols)
-
-    def weight_map(i, g):
-        running = i < 2 * COL_BLOCKS
-        return jnp.where(running, g, n_groups - 1), 0, jnp.where(running, lax.rem(i, COL_BLOCKS), COL_BLOCKS - 1)
-
     return pl.pallas_call(
         functools.partial(finish_kernel, cap, depth // 3, COL_BLOCKS),
-        grid=(2 * COL_BLOCKS + 1, n_groups),
+        grid=(2 * COL_BLOCKS + 1,),
         out_shape=jax.ShapeDtypeStruct((tok_dev, d_model), jnp.bfloat16),
         in_specs=[
-            ANY,
-            ANY,
-            ANY,
-            pl.BlockSpec((tok_dev, cols), lambda i, g: (0, jnp.maximum(i - COL_BLOCKS - 1, 0))),
-            pl.BlockSpec((GROUP, width, cols), weight_map),
-            pl.BlockSpec((shared_width, cols), lambda i, g: (0, jnp.minimum(i, COL_BLOCKS - 1))),
-        ],
+            ANY
+        ]
+        * 6,
         out_specs=ANY,
         scratch_shapes=[
+            pltpu.VMEM((2, tok_dev, cols), jnp.float32),
+            pltpu.VMEM((2, shared_width, cols), jnp.bfloat16),
             pltpu.VMEM((2, n_groups, tok_dev, depth), jnp.bfloat16),
             pltpu.VMEM(peer_hidden.shape, jnp.bfloat16),
             pltpu.VMEM((local_exp, 2 * cap, width), jnp.bfloat16),
-            pltpu.VMEM((2, 2, depth // 3, cols), jnp.bfloat16),
+            pltpu.VMEM((n_groups, GROUP, width, cols), jnp.bfloat16),
+            pltpu.VMEM((n_groups, 2, depth // 3, cols), jnp.bfloat16),
             pltpu.VMEM((2, tok_dev, cols), jnp.float32),
             pltpu.VMEM((2, tok_dev, cols), jnp.float32),
             pltpu.VMEM(blocks, jnp.float32),
@@ -535,17 +588,20 @@
             pltpu.VMEM(blocks, jnp.float32),
             pltpu.VMEM(blocks, jnp.float32),
             pltpu.VMEM(blocks, jnp.bfloat16),
+            pltpu.SemaphoreType.DMA((2,)),
+            pltpu.SemaphoreType.DMA((2,)),
             pltpu.SemaphoreType.DMA,
             pltpu.SemaphoreType.DMA((2, n_groups)),
-            pltpu.SemaphoreType.DMA((n_groups,)),
+            group_sems,
+            group_sems,
             sems, two_sems, two_sems, sems, sems, sems, sems,
         ],
         compiler_params=pltpu.CompilerParams(
-            collective_id=0, has_side_effects=True, vmem_limit_bytes=67043328, dimension_semantics=("arbitrary", "arbitrary")
+            collective_id=0, has_side_effects=True, vmem_limit_bytes=67043328, dimension_semantics=("arbitrary",)
         ),
         cost_estimate=cost(2 * d_model * local_exp * (n_rows * width + 4 * tok_dev * 256), 2 * local_exp * width * d_model),
         name="finish",
-    )(combine, peer_hidden, hidden, base, w_down, shared_down_w)
+    )(combine, peer_hidden, hidden, w_down, base, shared_down_w)
 
 
 def solution(mesh):

time: 243 us -> 239 us (0.984); the launches traced: 242 us -> 241 us
  no operation moved by 1% of the time
where the time goes in v6:
time: 239 us; the launch traced here: 241 us
  Pallas kernels  235 us (98%)
  local copies, waits for them, and re-layouts  3.16 us (1%)
    pallas_call x1, Pallas kernels, finish(): pl.pallas_call(functools.partial(finish_kernel, cap, depth // 3, COL_BLOC...  111 us
    pallas_call x1, Pallas kernels, expert_hidden(): pl.pallas_call(functools.partial(hidden_kernel, cap, pitch), grid=(local_...  66.5 us
    pallas_call x1, Pallas kernels, start(): pl.pallas_call(functools.partial(start_kernel, cap, local_exp), out_shape...  58 us

profile of v6, /device:TPU:0, one launch (start us, length us, event | category | flops | bytes accessed | tf_op | source)
XLA Modules:
  0.0 240.7 jit_solution(17342000743702146903)
XLA Ops:
  0.0 0.7 convert_bitcast_fusion
  0.7 1.3 pad_maximum_fusion.meta_ref
  2.0 58.0 %start.1 = (f32[4,8,512]{2,1,0:T(8,128)}, bf16[512,2048]{1,0:T(8,128)(2,1)}, bf16[512,2048]{1,0:T(8,128)(2,1)}, bf16[512,2048]{1,0:T(8,128)(2,1)}, bf16[3,2048,1...) custom-call(f32[8,512]{1,0:T(8,128)} %pad_maximum_fusion.meta_ref, ...), custom_call_target="tpu_custom_call" | custom-call | flops 29527900160 | bytes 57671680 | tf_op jit(solution)/shard_map/start/pallas_call | solution.py:192
  60.0 66.5 %expert_hidden.1.hidden_hbm = bf16[15,288,1408]{2,1,0:T(8,128)(2,1)} custom-call(f32[4,8,512]{2,1,0:T(8,128)} %get-tuple-element.14.meta_ref, bf16[512,2048]{1,0:T(8,128)(2,1)} %refs_0_.1, bf16[512,2048]{1,0:T(8,128)(2,1)} %get-tuple-element.15.refs_1_, bf16[512,2048]{1,0:T(8,128)(2,1)} %get-tuple-element.16.refs_2_, ...), custom_call_target="tpu_custom_call" | custom-call | flops 49828331520 | bytes 173015040 | tf_op jit(solution)/shard_map/expert_hidden/pallas_call | solution.py:317
  126.5 111.0 %finish.1 = bf16[512,2048]{1,0:T(8,128)(2,1)} custom-call(bf16[3,2048,1152]{2,1,0:T(8,128)(2,1)} %get-tuple-element.12.combine_hbm, bf16[512,2816]{1,0:T(8,128)(2,1)} %get-tuple-element.13.peer_hbm, bf16[15,288,1408]{2,1,0:T(8,128)(2,1)} %expert_hidden.1.hidden_hbm, bf16[15,1408,2048]{2,1,0:T(8,128)(2,1)} %weight_hbm.1, ...), custom_call_target="tpu_custom_call" | custom-call | flops 57126420480 | bytes 86507520 | tf_op jit(solution)/shard_map/finish/pallas_call | solution.py:567
  237.5 3.2 %copy.14 = bf16[512,2048]{1,0:T(8,128)(2,1)} copy(bf16[512,2048]{1,0:T(8,128)(2,1)} %finish.1) | data formatting | bytes 4194304

commit v7 on v6

--- a/solution.py
+++ b/solution.py
@@ -429,6 +429,8 @@
     def _():
         load_hidden(False, 0).start()
         load_weight(step, 0).start()
+        load_peer.start()
+        load_shared(step).start()
         load_hidden(False, 1).start()
         load_weight(step, 1).start()
         for copy in load_combine(False, 0):
@@ -478,9 +480,9 @@
         for g in range(1, n_groups):
             for copy in load_combine(False, g):
                 copy.start()
-        load_peer.start()
-        load_shared(step).start()
         expert_rows(0)
+        load_peer.wait()
+        share_peer()
 
     @pl.when((step > 0) & (step < n_steps))
     def _():
@@ -497,17 +499,17 @@
     refill(0)
     refill_combine(done, last)
 
-    @pl.when((step >= 1) & (step <= n_blocks))
-    def _():
+    def forward():
         core_copy(done).wait()
         from_core[done] += kept[lax.rem(done, 2)]
         chip_copy(done).start()
 
-    @pl.when(step > n_blocks)
-    def _():
+    def keep():
         core_copy(done).wait()
         load_base(done - n_blocks).wait()
         from_core[done] += kept[lax.rem(done, 2)] + base[lax.rem(done, 2)]
+
+    pl.when(step == 1)(forward)
 
     for g in range(1, n_groups):
         hidden_ready(g)
@@ -524,21 +526,20 @@
 
         if g == 1:
 
-            @pl.when(step == 0)
-            def _():
-                load_peer.wait()
-
             @pl.when(step < n_blocks - 1)
             def _():
                 load_shared(step + 1).start()
 
-            @pl.when(step < n_blocks)
+            @pl.when((step > 0) & (step < n_blocks))
             def _():
                 share_peer()
 
             @pl.when((step >= n_blocks) & (step < n_steps))
             def _():
                 load_base(step - n_blocks).start()
+
+    pl.when((step > 1) & (step <= n_blocks))(forward)
+    pl.when(step > n_blocks)(keep)
 
     @pl.when((step > n_blocks) & (step <= n_blocks + 4))
     def _():

time: 239 us -> 238 us (level)
    pallas_call x1, Pallas kernels: 111 us -> 108 us  [finish(): pl.pallas_call(functools.partial(finish_kernel, cap, depth // 3, COL_BLOC...]
where the time goes in v7:
time: 238 us
  Pallas kernels  233 us (98%)
  local copies, waits for them, and re-layouts  3.16 us (1%)
    pallas_call x1, Pallas kernels, finish(): pl.pallas_call(functools.partial(finish_kernel, cap, depth // 3, COL_BLOC...  108 us
    pallas_call x1, Pallas kernels, expert_hidden(): pl.pallas_call(functools.partial(hidden_kernel, cap, pitch), grid=(local_...  66.5 us
    pallas_call x1, Pallas kernels, start(): pl.pallas_call(functools.partial(start_kernel, cap, local_exp), out_shape...  58 us

profile of v7, /device:TPU:0, one launch (start us, length us, event | category | flops | bytes accessed | tf_op | source)
XLA Modules:
  0.0 238.1 jit_solution(11230488207021377085)
XLA Ops:
  0.0 0.7 convert_bitcast_fusion
  0.7 1.3 pad_maximum_fusion.meta_ref
  2.0 58.0 %start.1 = (f32[4,8,512]{2,1,0:T(8,128)}, bf16[512,2048]{1,0:T(8,128)(2,1)}, bf16[512,2048]{1,0:T(8,128)(2,1)}, bf16[512,2048]{1,0:T(8,128)(2,1)}, bf16[3,2048,1...) custom-call(f32[8,512]{1,0:T(8,128)} %pad_maximum_fusion.meta_ref, ...), custom_call_target="tpu_custom_call" | custom-call | flops 29527900160 | bytes 57671680 | tf_op jit(solution)/shard_map/start/pallas_call | solution.py:192
  60.0 66.5 %expert_hidden.1.hidden_hbm = bf16[15,288,1408]{2,1,0:T(8,128)(2,1)} custom-call(f32[4,8,512]{2,1,0:T(8,128)} %get-tuple-element.14.meta_ref, bf16[512,2048]{1,0:T(8,128)(2,1)} %refs_0_.1, bf16[512,2048]{1,0:T(8,128)(2,1)} %get-tuple-element.15.refs_1_, bf16[512,2048]{1,0:T(8,128)(2,1)} %get-tuple-element.16.refs_2_, ...), custom_call_target="tpu_custom_call" | custom-call | flops 49828331520 | bytes 173015040 | tf_op jit(solution)/shard_map/expert_hidden/pallas_call | solution.py:317
  126.5 108.5 %finish.1 = bf16[512,2048]{1,0:T(8,128)(2,1)} custom-call(bf16[3,2048,1152]{2,1,0:T(8,128)(2,1)} %get-tuple-element.12.combine_hbm, bf16[512,2816]{1,0:T(8,128)(2,1)} %get-tuple-element.13.peer_hbm, bf16[15,288,1408]{2,1,0:T(8,128)(2,1)} %expert_hidden.1.hidden_hbm, bf16[15,1408,2048]{2,1,0:T(8,128)(2,1)} %weight_hbm.1, ...), custom_call_target="tpu_custom_call" | custom-call | flops 57126420480 | bytes 86507520 | tf_op jit(solution)/shard_map/finish/pallas_call | solution.py:568
  235.0 3.2 %copy.14 = bf16[512,2048]{1,0:T(8,128)(2,1)} copy(bf16[512,2048]{1,0:T(8,128)(2,1)} %finish.1) | data formatting | bytes 4194304

commit v8 on v7

--- a/solution.py
+++ b/solution.py
@@ -86,7 +86,7 @@
 
 
 def start_kernel(
-    cap, local_exp, meta_ref, owner_ref, slot_ref, tok_hbm, w_gate_hbm, w_up_hbm, w_down_hbm,
+    cap, local_exp, id_ref, gate_ref, slots_ref, owner_ref, slot_ref, tok_hbm, w_gate_hbm, w_up_hbm, w_down_hbm,
     metas, tok_core, tok_chip, tok_both, combine_hbm, base_hbm, peer_hbm,
     own, other, own_hidden, peer_hidden, base, w_gate, w_up, w_down,
     load_sem, store_sem, peer_sem, send_sem, recv_sem,
@@ -100,8 +100,13 @@
             src_ref=src, dst_ref=dst, send_sem=send_sem.at[i], recv_sem=recv_sem.at[i], device_id=device, device_id_type=MESH
         )
 
+    ids, slots = id_ref[...], slots_ref[...]
+    code = jnp.where(slots >= 0, ids * cap + slots, -1).astype(jnp.float32)
+    top_k = code.shape[0]
+    metas[0, :top_k] = code
+    metas[0, top_k:] = gate_ref[...]
     greet((core, chip, both, tp))
-    meta_copies = [remote(meta_ref, metas.at[i + 1], device, i) for i, device in enumerate((core, chip, both))]
+    meta_copies = [remote(metas.at[0], metas.at[i + 1], device, i) for i, device in enumerate((core, chip, both))]
     for copy in meta_copies:
         copy.start()
     to_core = remote(tok_hbm, tok_core, core, 3)
@@ -118,7 +123,6 @@
     loads = [pltpu.make_async_copy(src, dst, load_sem.at[i]) for i, (src, dst) in enumerate(pairs)]
     for load in loads:
         load.start()
-    metas[0] = meta_ref[...]
     for copy in meta_copies:
         copy.wait()
 
@@ -183,7 +187,7 @@
         copy.wait()
 
 
-def start(meta, owner, slot, tokens, w_gate, w_up, w_down, cap, local_exp):
+def start(ids, gates, slots, owner, slot, tokens, w_gate, w_up, w_down, cap, local_exp):
     tok_dev, d_model = tokens.shape
     width = w_gate.shape[1]
     n_groups = local_exp // GROUP
@@ -192,13 +196,13 @@
     return pl.pallas_call(
         functools.partial(start_kernel, cap, local_exp),
         out_shape=[
-            jax.ShapeDtypeStruct((4,) + meta.shape, jnp.float32),
+            jax.ShapeDtypeStruct((4, 2 * ids.shape[0], tok_dev), jnp.float32),
             tok_shape, tok_shape, tok_shape,
             jax.ShapeDtypeStruct((n_groups, 4 * tok_dev, 3 * owner.shape[1] // n_groups), jnp.bfloat16),
             jax.ShapeDtypeStruct((tok_dev, d_model), jnp.float32),
             jax.ShapeDtypeStruct((tok_dev, width), jnp.bfloat16),
         ],
-        in_specs=[vmem, vmem, vmem, ANY, ANY, ANY, ANY],
+        in_specs=[vmem] * 5 + [ANY] * 4,
         out_specs=[vmem, ANY, ANY, ANY, ANY, ANY, ANY],
         scratch_shapes=[
             pltpu.VMEM((tok_dev, d_model), jnp.bfloat16),
@@ -218,7 +222,7 @@
         compiler_params=pltpu.CompilerParams(collective_id=1, has_side_effects=True, vmem_limit_bytes=67043328),
         cost_estimate=cost(10 * tok_dev * d_model * width, 10 * d_model * width),
         name="start",
-    )(meta, owner, slot, tokens, w_gate, w_up, w_down)
+    )(ids, gates, slots, owner, slot, tokens, w_gate, w_up, w_down)
 
 
 def hidden_kernel(cap, pitch, meta_ref, *refs):
@@ -615,10 +619,8 @@
         top_k = expert_ids.shape[1]
         local_exp = expert_w1.shape[0]
         cap = capacity_rows(tok_dev, top_k, local_exp * ep_size)
-        code = jnp.where(slots >= 0, expert_ids * cap + slots, -1)
-        meta = jnp.concatenate([code.astype(jnp.float32).T, gates.T], axis=0)
         _, owner, slot = lane_tables(cap, local_exp)
-        metas, tok_core, tok_chip, tok_both, combine, base, peer_hidden = start(meta, owner, slot, tokens, shared_w1, shared_w3, shared_w2, cap, local_exp)
+        metas, tok_core, tok_chip, tok_both, combine, base, peer_hidden = start(expert_ids.T, gates.T, slots.T, owner, slot, tokens, shared_w1, shared_w3, shared_w2, cap, local_exp)
         hidden = expert_hidden(metas, (tokens, tok_core, tok_chip, tok_both), expert_w1, expert_w3, cap)
         return finish(hidden, combine, base, peer_hidden, expert_w2, shared_w2)
 

time: 238 us -> 236 us (level)
  no operation moved by 1% of the time
where the time goes in v8:
time: 236 us
  Pallas kernels  233 us (99%)
  local copies, waits for them, and re-layouts  3.16 us (1%)
    pallas_call x1, Pallas kernels, finish(): pl.pallas_call(functools.partial(finish_kernel, cap, depth // 3, COL_BLOC...  106 us
    pallas_call x1, Pallas kernels, expert_hidden(): pl.pallas_call(functools.partial(hidden_kernel, cap, pitch), grid=(local_...  68.1 us
    pallas_call x1, Pallas kernels, start(): pl.pallas_call(functools.partial(start_kernel, cap, local_exp), out_shape...  58 us

profile of v8, /device:TPU:0, one launch (start us, length us, event | category | flops | bytes accessed | tf_op | source)
XLA Modules:
  0.0 235.8 jit_solution(12704046226364069928)
XLA Ops:
  0.0 58.0 %start.1 = (f32[4,8,512]{2,1,0:T(8,128)}, bf16[512,2048]{1,0:T(8,128)(2,1)}, bf16[512,2048]{1,0:T(8,128)(2,1)}, bf16[512,2048]{1,0:T(8,128)(2,1)}, bf16[3,2048,1...) custom-call(s32[4,512]{1,0:T(4,128)} %bitcast.3, f32[4,512]{1,0:T(4,128)} %bitcast.4, ...), custom_call_target="tpu_custom_call" | custom-call | flops 29527900160 | bytes 57671680 | tf_op jit(solution)/shard_map/start/pallas_call | solution.py:196
  58.0 68.1 %expert_hidden.1.hidden_hbm = bf16[15,288,1408]{2,1,0:T(8,128)(2,1)} custom-call(f32[4,8,512]{2,1,0:T(8,128)} %get-tuple-element.14.meta_ref, bf16[512,2048]{1,0:T(8,128)(2,1)} %refs_0_.1, bf16[512,2048]{1,0:T(8,128)(2,1)} %get-tuple-element.15.refs_1_, bf16[512,2048]{1,0:T(8,128)(2,1)} %get-tuple-element.16.refs_2_, ...), custom_call_target="tpu_custom_call" | custom-call | flops 49828331520 | bytes 173015040 | tf_op jit(solution)/shard_map/expert_hidden/pallas_call | solution.py:321
  126.1 106.5 %finish.1 = bf16[512,2048]{1,0:T(8,128)(2,1)} custom-call(bf16[3,2048,1152]{2,1,0:T(8,128)(2,1)} %get-tuple-element.12.combine_hbm, bf16[512,2816]{1,0:T(8,128)(2,1)} %get-tuple-element.13.peer_hbm, bf16[15,288,1408]{2,1,0:T(8,128)(2,1)} %expert_hidden.1.hidden_hbm, bf16[15,1408,2048]{2,1,0:T(8,128)(2,1)} %weight_hbm.1, ...), custom_call_target="tpu_custom_call" | custom-call | flops 57126420480 | bytes 86507520 | tf_op jit(solution)/shard_map/finish/pallas_call | solution.py:572
  232.6 3.2 %copy.14 = bf16[512,2048]{1,0:T(8,128)(2,1)} copy(bf16[512,2048]{1,0:T(8,128)(2,1)} %finish.1) | data formatting | bytes 4194304
